TPU v7x, 256 devices: a whole 4x4x8 slice. The times are simulated.
256 devices in a mesh: mem: 32 (over x_lo, z, core), space: 8 (over x_hi, y).
Axes of the slice: x: 4 (x_hi: 2, x_lo: 2; x = x_hi * 2 + x_lo), y: 4, z: 8, core: 2. Of those that a mesh axis runs over, the one named last changes fastest.
Arguments:
- prior_samples: bfloat16 [256, 128, 8192], P('mem', 'space'), may hold values from -6 to 6
- diffusivity_field: float32 [128, 8192], P('space'), may hold values from 0.05 to 0.24
- measured_site_position: int32 [8, 32, 512], P('space', 'mem'), may hold values from 0 to 4095
- measured_quantities: float32 [8, 32, 512], P('space', 'mem'), may hold values from -6 to 6
- measurement_weightings: float32 [8, 32, 512], P('space', 'mem'), may hold values from 0.5 to 8
Outputs:
- analysis: bfloat16 [256, 128, 8192], P('mem', 'space')
Inputs may be any that keep to these rules, and one draw needn't show every extreme that they name: measured_site_position[p, q, o] names cell a * 256 + b of patch (p, q) itself.
All inputs are finite; a program needn't handle non-finite values.
Results may differ from a plain program's by a relative error of at most 0.0077.
Values may be sent and summed in bfloat16 or wider, within the bound.
No kernel may reach another device: no remote copies, remote signals or barrier semaphores. Data moves between devices by JAX's collectives and lax.ppermute only.
A program may use at most 64 MiB of HBM per device.

v0:
```python
import jax
import jax.numpy as jnp
from jax import lax
from jax.sharding import Mesh
from jax.sharding import PartitionSpec as P

ITERS = 10
MEM = ("mem_0", "mem_1", "mem_2")


HIGHEST = lax.Precision.HIGHEST


def padded_2(block, sides, width):
    for axis, dim in sides:
        count = lax.axis_size(axis)
        forward = [(i, i + 1) for i in range(count - 1)]
        backward = [(target, source) for source, target in forward]
        low = lax.ppermute(
            lax.slice_in_dim(block, block.shape[dim] - width, None, axis=dim), axis, forward
        )
        high = lax.ppermute(lax.slice_in_dim(block, 0, width, axis=dim), axis, backward)
        block = jnp.concatenate([low, block, high], axis=dim)
    return block


def in_blocks(shard, dim, size):
    before, after = (shard.shape[:dim], shard.shape[dim + 1 :])
    return jnp.moveaxis(shard.reshape(*before, size, -1, *after), dim, 0)


def laid_out(tiles, dim):
    lengths = list(tiles.shape[1:])
    lengths[dim] *= tiles.shape[0]
    return jnp.moveaxis(tiles, 0, dim).reshape(lengths)


def turned_blocks(tiles, axes, sequence):
    lengths = [lax.axis_size(a) for a in axes]
    tiles = tiles.reshape(*lengths, *tiles.shape[1:])
    for k in sequence:
        tiles = lax.all_to_all(tiles, axes[k], split_axis=k, concat_axis=k, tiled=True)
    return tiles.reshape(-1, *tiles.shape[len(axes) :])


def core_and_chips(shard, groups, sequence, split_dim, concat_dim):
    size = lax.axis_size(groups[0]) * lax.axis_size(groups[1])
    tiles = in_blocks(shard, split_dim, size)
    return laid_out(turned_blocks(tiles, groups, sequence), concat_dim)


def interior(extended):
    middle = extended[:, 1:-1]
    padded = jnp.pad(middle, ((0, 0), (0, 0), (1, 1)))
    return extended[:, 2:] + extended[:, :-2] + padded[:, :, 2:] + padded[:, :, :-2] - 4.0 * middle


def body(
    prior_samples,
    diffusivity_field,
    measured_site_position,
    measured_quantities,
    measurement_weightings,
):
    extended = padded_2(prior_samples, (("space", 1),), 2).astype(jnp.float32)
    coef_wide = padded_2(diffusivity_field, (("space", 0),), 1)
    once_done = extended[:, 1:-1] + coef_wide[None] * interior(extended)
    present_sample = once_done[:, 1:-1] + diffusivity_field[None] * interior(once_done)
    advanced_sample = present_sample.astype(jnp.bfloat16)
    patch_cells = core_and_chips(advanced_sample, (("mem_0", "mem_1"), "mem_2"), (1, 0), 2, 0)
    members, rows_a, rows_b = patch_cells.shape
    patch_rows = patch_cells.reshape(members, rows_a * rows_b)
    observed = jnp.take(patch_rows, measured_site_position[0, 0], axis=1).astype(jnp.float32)
    obs_mean = jnp.mean(observed, axis=0)
    obs_root = jnp.sqrt(measurement_weightings[0, 0])
    spread = ((observed - obs_mean[None, :]) * obs_root[None, :]).astype(jnp.bfloat16)
    innovation = ((measured_quantities[0, 0] - obs_mean) * obs_root).astype(jnp.bfloat16)
    own_gram = lax.dot_general(
        spread, spread, (((1,), (1,)), ((), ())), preferred_element_type=jnp.float32
    )
    own_vector = jnp.dot(spread, innovation, preferred_element_type=jnp.float32)
    side_grams, side_vectors = (
        padded_2(own_gram[None], ((MEM, 0),), 1),
        padded_2(own_vector[None], ((MEM, 0),), 1),
    )
    band_gram = 0.5 * side_grams[0] + side_grams[1] + 0.5 * side_grams[2]
    band_vector = 0.5 * side_vectors[0] + side_vectors[1] + 0.5 * side_vectors[2]
    upper_grams, upper_vectors = (
        padded_2(band_gram[None], (("space", 0),), 1),
        padded_2(band_vector[None], (("space", 0),), 1),
    )
    gram = 0.5 * upper_grams[0] + upper_grams[1] + 0.5 * upper_grams[2]
    vector = 0.5 * upper_vectors[0] + upper_vectors[1] + 0.5 * upper_vectors[2]
    identity = jnp.eye(members, dtype=jnp.float32)
    system = gram + (members - 1.0) * identity
    frobenius = jnp.sqrt(jnp.sum(system * system))

    def newton(counter, pair):
        root_part, inverse_part = pair
        factor = 1.5 * identity - 0.5 * jnp.dot(inverse_part, root_part, precision=HIGHEST)
        return (
            jnp.dot(root_part, factor, precision=HIGHEST),
            jnp.dot(factor, inverse_part, precision=HIGHEST),
        )

    root_part, inverse_part = lax.fori_loop(0, ITERS, newton, (system / frobenius, identity))
    inverse_root = inverse_part / jnp.sqrt(frobenius)
    mean_weights = jnp.dot(
        inverse_root, jnp.dot(inverse_root, vector, precision=HIGHEST), precision=HIGHEST
    )
    transform = (jnp.sqrt(members - 1.0) * inverse_root + mean_weights[:, None]).astype(
        jnp.bfloat16
    )
    state_mean = jnp.mean(patch_rows, axis=0, dtype=jnp.float32)
    deviation = (patch_rows.astype(jnp.float32) - state_mean[None, :]).astype(jnp.bfloat16)
    moved = lax.dot_general(
        transform, deviation, (((0,), (0,)), ((), ())), preferred_element_type=jnp.float32
    )
    updated = (state_mean[None, :] + moved).astype(jnp.bfloat16).reshape(members, rows_a, rows_b)
    returned = lax.all_to_all(updated, MEM, split_axis=0, concat_axis=2, tiled=True)
    extended = padded_2(returned, (("space", 1),), 1).astype(jnp.float32)
    return (returned.astype(jnp.float32) + diffusivity_field[None] * interior(extended)).astype(
        jnp.bfloat16
    )


def solution(mesh):
    finer = Mesh(
        mesh.devices.reshape(2, 8, 2, mesh.shape["space"]), ("mem_0", "mem_1", "mem_2", "space")
    )
    in_specs = (
        P(MEM, "space", None),
        P("space", None),
        P("space", MEM, None),
        P("space", MEM, None),
        P("space", MEM, None),
    )
    out_specs = P(MEM, "space", None)
    return jax.shard_map(body, mesh=finer, in_specs=in_specs, out_specs=out_specs, check_vma=False)
```

profile of v0, /device:TPU:56, one launch (start us, length us, event | category | flops | bytes accessed | tf_op | source)
XLA Modules:
  0.0 245.3 jit_solution(6174302752995377443)
XLA Ops:
  1.1 4.6 %collective-permute-start.2 = (f32[1,8192]{1,0:T(1,128)S(1)}, f32[1,8192]{1,0:T(1,128)S(1)}, u32[]{:S(2)}, u32[]{:S(2)}) collective-permute-start(f32[1,8192]{1,0:T(1,128)S(1)} %get-tuple-element.66), channel_id=1, source_target_pairs={{0,1},{1,2},{2,3},{3,4},{4,5},{5,6},{6,7},{8,9},{9,10},{10,11},{11... | collective-permute-start | bytes 98312 | tf_op jit(solution)/shard_map/ppermute | solution.py:19
  7.7 2.8 %copy.42 = bf16[8,16,8192]{2,0,1:T(8,128)(2,1)S(1)} copy(bf16[8,16,8192]{2,1,0:T(8,128)(2,1)} %param.7) | data formatting | bytes 4194304 | tf_op args[0]
  10.5 7.5 %collective-permute-start = (bf16[8,2,8192]{2,0,1:T(8,128)(2,1)S(1)}, bf16[8,2,8192]{2,0,1:T(8,128)(2,1)S(1)}, u32[]{:S(2)}, u32[]{:S(2)}) collective-permute-start(bf16[8,2,8192]{2,0,1:T(8,128)(2,1)S(1)} %get-tuple-element.64), channel_id=1, source_target_pairs={{0,1},{1,2},{2,3},{3,4},{4,5},{5,6},{6,7},{8,9},{9,10},{10,11},{11... | collective-permute-start | bytes 786440 | tf_op jit(solution)/shard_map/ppermute | solution.py:19
  20.1 2.9 %collective-permute-done = bf16[8,2,8192]{2,0,1:T(8,128)(2,1)S(1)} collective-permute-done((bf16[8,2,8192]{2,0,1:T(8,128)(2,1)S(1)}, bf16[8,2,8192]{2,0,1:T(8,128)(2,1)S(1)}, u32[]{:S(2)}, u32[]{:S(2)}) %collective-permute-start) | collective-permute-done | bytes 262176 | tf_op jit(solution)/shard_map/ppermute | solution.py:19
  23.0 7.7 %collective-permute-done.1 = bf16[8,2,8192]{2,0,1:T(8,128)(2,1)S(1)} collective-permute-done((bf16[8,2,8192]{2,0,1:T(8,128)(2,1)S(1)}, bf16[8,2,8192]{2,0,1:T(8,128)(2,1)S(1)}, u32[]{:S(2)}, u32[]{:S(2)}) %collective-permute-start.1) | collective-permute-done | bytes 262176 | tf_op jit(solution)/shard_map/ppermute | solution.py:22
  31.5 3.1 %fusion.8 = f32[8,18,8192]{2,0,1:T(8,128)S(1)} fusion(f32[8,18,8192]{2,0,1:T(8,128)S(1)} %slice.90, f32[8,20,8192]{2,0,1:T(8,128)S(1)} %maximum_convert_fusion, f32[18,8192]{1,0:T(8,128)S(1)} %pad_maximum_fusion), kind=kLoop, calls=%fused_computation.13 | loop fusion | flops 8257536 | bytes 19464192 | tf_op jit(solution)/shard_map/add | solution.py:67
  34.9 2.6 %fusion.20 = bf16[8,16,8192]{2,0,1:T(8,128)(2,1)S(1)} fusion(f32[8,16,8192]{2,0,1:T(8,128)S(1)} %slice.93, f32[8,18,8192]{2,0,1:T(8,128)S(1)} %fusion.8, f32[16,8192]{1,0:T(8,128)S(1)} %copy-done), kind=kLoop, calls=%fused_computation.27 | loop fusion | flops 8388608 | bytes 15204352 | tf_op jit(solution)/shard_map/convert_element_type | solution.py:69
  40.2 5.4 %all_to_all.28 = bf16[16,2,8,16,256]{4,2,3,0,1:T(8,128)(2,1)S(1)} all-to-all(bf16[16,2,8,16,256]{4,2,3,0,1:T(8,128)(2,1)S(1)} %copy.47), channel_id=1, replica_groups=mesh['mem_0'=2,'mem_1'=8,'mem_2'=2,'space'=8] {'mem_2'}, dimensions={1} | all-to-all | bytes 4194304 | tf_op jit(solution)/shard_map/all_to_all | solution.py:42
  47.1 8.6 %all-to-all-start.1 = ((bf16[16,2,8,16,256]{4,2,3,1,0:T(8,128)(2,1)}), bf16[16,2,8,16,256]{4,2,3,1,0:T(8,128)(2,1)S(1)}, u32[]{:S(2)}, u32[]{:S(2)}) async-start(bf16[16,2,8,16,256]{4,2,3,1,0:T(8,128)(2,1)} %copy.48), calls=%async_computation.1 | async-start | bytes 4194304 | tf_op jit(solution)/shard_map/all_to_all | solution.py:42
  55.8 49.1 %all-to-all-done.1 = bf16[16,2,8,16,256]{4,2,3,1,0:T(8,128)(2,1)S(1)} async-done(((bf16[16,2,8,16,256]{4,2,3,1,0:T(8,128)(2,1)}), bf16[16,2,8,16,256]{4,2,3,1,0:T(8,128)(2,1)S(1)}, u32[]{:S(2)}, u32[]{:S(2)}) %all-to-all-start.1) | async-done | bytes 2097184 | tf_op jit(solution)/shard_map/all_to_all | solution.py:42
  104.9 2.4 copy.49
  107.4 3.4 %gather_fusion = bf16[512,256]{1,0:T(8,128)(2,1)S(1)} fusion(bf16[256,4096]{0,1:T(8,128)(2,1)} %copy.49, s32[1024]{0:T(1024)S(1)} %pad_clamp_fusion), kind=kCustom, calls=%fused_computation | custom fusion | bytes 526336 | tf_op jit(solution)/shard_map/jit(_take)/gather | solution.py:73
  113.5 3.6 %collective-permute-start.5 = (f32[1,256,256]{2,1,0:T(8,128)S(1)}, f32[1,256,256]{2,1,0:T(8,128)S(1)}, u32[]{:S(2)}, u32[]{:S(2)}) collective-permute-start(f32[1,256,256]{2,1,0:T(8,128)S(1)} %bitcast.110), channel_id=1, source_target_pairs={{8,0},{16,8},{24,16},{32,24},{40,32},{48,40},{56,48},{64,56},{72,6... | collective-permute-start | bytes 786440 | tf_op jit(solution)/shard_map/ppermute | solution.py:22
  119.3 3.6 %collective-permute-start.9 = (f32[1,256]{1,0:T(1,128)S(1)}, f32[1,256]{1,0:T(1,128)S(1)}, u32[]{:S(2)}, u32[]{:S(2)}) collective-permute-start(f32[1,256]{1,0:T(1,128)S(1)} %fusion.24), channel_id=1, source_target_pairs={{8,0},{16,8},{24,16},{32,24},{40,32},{48,40},{56,48},{64,56},{72,6... | collective-permute-start | bytes 3080 | tf_op jit(solution)/shard_map/ppermute | solution.py:22
  126.3 3.8 %collective-permute-start.11 = (f32[1,256]{1,0:T(1,128)S(1)}, f32[1,256]{1,0:T(1,128)S(1)}, u32[]{:S(2)}, u32[]{:S(2)}) collective-permute-start(f32[1,256]{1,0:T(1,128)S(1)} %bitcast.123), channel_id=1, source_target_pairs={{1,0},{2,1},{3,2},{4,3},{5,4},{6,5},{7,6},{9,8},{10,9},{11,10},{12... | collective-permute-start | bytes 3080 | tf_op jit(solution)/shard_map/ppermute | solution.py:22
  130.2 5.7 %collective-permute-start.6 = (f32[1,256,256]{2,1,0:T(8,128)S(1)}, f32[1,256,256]{2,1,0:T(8,128)S(1)}, u32[]{:S(2)}, u32[]{:S(2)}) collective-permute-start(f32[1,256,256]{2,1,0:T(8,128)S(1)} %fusion.32), channel_id=1, source_target_pairs={{0,1},{1,2},{2,3},{3,4},{4,5},{5,6},{6,7},{8,9},{9,10},{10,11},{11... | collective-permute-start | bytes 786440 | tf_op jit(solution)/shard_map/ppermute | solution.py:19
  138.0 2.7 %collective-permute-done.6 = f32[1,256,256]{2,1,0:T(8,128)S(1)} collective-permute-done((f32[1,256,256]{2,1,0:T(8,128)S(1)}, f32[1,256,256]{2,1,0:T(8,128)S(1)}, u32[]{:S(2)}, u32[]{:S(2)}) %collective-permute-start.6) | collective-permute-done | bytes 262176 | tf_op jit(solution)/shard_map/ppermute | solution.py:19
  140.7 7.7 %collective-permute-done.7 = f32[1,256,256]{2,1,0:T(8,128)S(1)} collective-permute-done((f32[1,256,256]{2,1,0:T(8,128)S(1)}, f32[1,256,256]{2,1,0:T(8,128)S(1)}, u32[]{:S(2)}, u32[]{:S(2)}) %collective-permute-start.7) | collective-permute-done | bytes 262176 | tf_op jit(solution)/shard_map/ppermute | solution.py:22
  150.1 14.8 %while.13 = (s32[]{:T(128)}, f32[256,256]{0,1:T(8,128)S(1)}, f32[256,256]{1,0:T(8,128)S(1)}, s32[]{:T(128)}) while((s32[]{:T(128)}, f32[256,256]{0,1:T(8,128)S(1)}, f32[256,256]{1,0:T(8,128)S(1)}, s32[]{:T(128)}) %tuple.32), condition=%wide.region_4.5_spmd.clone, body=%wide.region_3.4_spmd.clone.sunk | while | flops 604241920 | bytes 3407925 | solution.py:106
  167.1 58.9 %all_to_all.29 = bf16[256,16,256]{2,1,0:T(8,128)(2,1)S(1)} all-to-all(bf16[256,16,256]{2,1,0:T(8,128)(2,1)S(1)} %bitcast.106), channel_id=1, replica_groups=mesh['mem_0'=2,'mem_1'=8,'mem_2'=2,'space'=8] {'mem_0','mem_1','mem_2'}, dimensions={0} | all-to-all | bytes 4194304 | tf_op jit(solution)/shard_map/all_to_all | solution.py:120
  228.8 3.8 %collective-permute-start.13 = (bf16[8,1,8192]{2,0,1:T(8,128)(2,1)S(1)}, bf16[8,1,8192]{2,0,1:T(8,128)(2,1)S(1)}, u32[]{:S(2)}, u32[]{:S(2)}) collective-permute-start(bf16[8,1,8192]{2,0,1:T(8,128)(2,1)S(1)} %get-tuple-element.63), channel_id=1, source_target_pairs={{1,0},{2,1},{3,2},{4,3},{5,4},{6,5},{7,6},{9,8},{10,9},{11,10},{12... | collective-permute-start | bytes 393224 | tf_op jit(solution)/shard_map/ppermute | solution.py:22
  233.6 5.7 %collective-permute-done.13 = bf16[8,1,8192]{2,0,1:T(8,128)(2,1)S(1)} collective-permute-done((bf16[8,1,8192]{2,0,1:T(8,128)(2,1)S(1)}, bf16[8,1,8192]{2,0,1:T(8,128)(2,1)S(1)}, u32[]{:S(2)}, u32[]{:S(2)}) %collective-permute-start.13) | collective-permute-done | bytes 131104 | tf_op jit(solution)/shard_map/ppermute | solution.py:22
  240.0 2.7 %fusion.14 = bf16[8,16,8192]{2,0,1:T(8,128)(2,1)S(1)} fusion(f32[8,18,8192]{2,0,1:T(8,128)S(1)} %maximum_convert_fusion.1, f32[8,16,8192]{2,0,1:T(8,128)S(1)} %slice.100, bf16[8,16,8192]{2,0,1:T(8,128)(2,1)S(1)} %bitcast.101, f32[16,8192]{1,0:T(8,128)S(1)} %copy-done), kind=kLoop, calls=%fused_computation.20 | loop fusion | flops 9437184 | bytes 17301504 | tf_op jit(solution)/shard_map/convert_element_type | solution.py:122
  242.8 2.5 %copy.52 = bf16[8,16,8192]{2,1,0:T(8,128)(2,1)} copy(bf16[8,16,8192]{2,0,1:T(8,128)(2,1)S(1)} %fusion.14) | data formatting | bytes 4194304 | tf_op jit(solution)/shard_map/convert_element_type | solution.py:122
  (116 shorter events, 42.6 us)
Async XLA Ops:
  0.0 20.0 %copy-start = (f32[16,8192]{1,0:T(8,128)S(1)}, f32[16,8192]{1,0:T(8,128)}, u32[]{:S(2)}) copy-start(f32[16,8192]{1,0:T(8,128)} %param.8) | copy-start | bytes 1572868
  1.1 18.8 %collective-permute-start.2 = (f32[1,8192]{1,0:T(1,128)S(1)}, f32[1,8192]{1,0:T(1,128)S(1)}, u32[]{:S(2)}, u32[]{:S(2)}) collective-permute-start(f32[1,8192]{1,0:T(1,128)S(1)} %get-tuple-element.66), channel_id=1, source_target_pairs={{0,1},{1,2},{2,3},{3,4},{4,5},{5,6},{6,7},{8,9},{9,10},{10,11},{11... | collective-permute-start | bytes 98312 | tf_op jit(solution)/shard_map/ppermute | solution.py:19
  5.7 14.2 %collective-permute-start.3 = (f32[1,8192]{1,0:T(1,128)S(1)}, f32[1,8192]{1,0:T(1,128)S(1)}, u32[]{:S(2)}, u32[]{:S(2)}) collective-permute-start(f32[1,8192]{1,0:T(1,128)S(1)} %get-tuple-element.67), channel_id=1, source_target_pairs={{1,0},{2,1},{3,2},{4,3},{5,4},{6,5},{7,6},{9,8},{10,9},{11,10},{12... | collective-permute-start | bytes 98312 | tf_op jit(solution)/shard_map/ppermute | solution.py:22
  10.5 12.5 %collective-permute-start = (bf16[8,2,8192]{2,0,1:T(8,128)(2,1)S(1)}, bf16[8,2,8192]{2,0,1:T(8,128)(2,1)S(1)}, u32[]{:S(2)}, u32[]{:S(2)}) collective-permute-start(bf16[8,2,8192]{2,0,1:T(8,128)(2,1)S(1)} %get-tuple-element.64), channel_id=1, source_target_pairs={{0,1},{1,2},{2,3},{3,4},{4,5},{5,6},{6,7},{8,9},{9,10},{10,11},{11... | collective-permute-start | bytes 786440 | tf_op jit(solution)/shard_map/ppermute | solution.py:19
  18.0 12.7 %collective-permute-start.1 = (bf16[8,2,8192]{2,0,1:T(8,128)(2,1)S(1)}, bf16[8,2,8192]{2,0,1:T(8,128)(2,1)S(1)}, u32[]{:S(2)}, u32[]{:S(2)}) collective-permute-start(bf16[8,2,8192]{2,0,1:T(8,128)(2,1)S(1)} %get-tuple-element.65), channel_id=1, source_target_pairs={{1,0},{2,1},{3,2},{4,3},{5,4},{6,5},{7,6},{9,8},{10,9},{11,10},{12... | collective-permute-start | bytes 786440 | tf_op jit(solution)/shard_map/ppermute | solution.py:22
  45.7 10.1 %copy-start.2 = (f32[1,1,512]{2,1,0:T(1,128)S(1)}, f32[1,1,512]{2,1,0:T(1,128)}, u32[]{:S(2)}) copy-start(f32[1,1,512]{2,1,0:T(1,128)} %param.11) | copy-start | bytes 6148
  45.7 10.1 %copy-start.1 = (s32[1,1,512]{2,1,0:T(1,128)S(1)}, s32[1,1,512]{2,1,0:T(1,128)}, u32[]{:S(2)}) copy-start(s32[1,1,512]{2,1,0:T(1,128)} %param.9) | copy-start | bytes 6148
  47.1 57.8 %all-to-all-start.1 = ((bf16[16,2,8,16,256]{4,2,3,1,0:T(8,128)(2,1)}), bf16[16,2,8,16,256]{4,2,3,1,0:T(8,128)(2,1)S(1)}, u32[]{:S(2)}, u32[]{:S(2)}) async-start(bf16[16,2,8,16,256]{4,2,3,1,0:T(8,128)(2,1)} %copy.48), calls=%async_computation.1 | async-start | bytes 4194304 | tf_op jit(solution)/shard_map/all_to_all | solution.py:42
  55.7 55.3 %copy-start.3 = (f32[1,1,512]{2,1,0:T(1,128)S(1)}, f32[1,1,512]{2,1,0:T(1,128)}, u32[]{:S(2)}) copy-start(f32[1,1,512]{2,1,0:T(1,128)} %param.10) | copy-start | bytes 6148
  111.6 18.5 %collective-permute-start.4 = (f32[1,256,256]{2,1,0:T(8,128)S(1)}, f32[1,256,256]{2,1,0:T(8,128)S(1)}, u32[]{:S(2)}, u32[]{:S(2)}) collective-permute-start(f32[1,256,256]{2,1,0:T(8,128)S(1)} %bitcast.109), channel_id=1, source_target_pairs={{0,8},{8,16},{16,24},{24,32},{32,40},{40,48},{48,56},{56,64},{64,7... | collective-permute-start | bytes 786440 | tf_op jit(solution)/shard_map/ppermute | solution.py:19
  113.5 16.6 %collective-permute-start.5 = (f32[1,256,256]{2,1,0:T(8,128)S(1)}, f32[1,256,256]{2,1,0:T(8,128)S(1)}, u32[]{:S(2)}, u32[]{:S(2)}) collective-permute-start(f32[1,256,256]{2,1,0:T(8,128)S(1)} %bitcast.110), channel_id=1, source_target_pairs={{8,0},{16,8},{24,16},{32,24},{40,32},{48,40},{56,48},{64,56},{72,6... | collective-permute-start | bytes 786440 | tf_op jit(solution)/shard_map/ppermute | solution.py:22
  117.3 5.9 %collective-permute-start.8 = (f32[1,256]{1,0:T(1,128)S(1)}, f32[1,256]{1,0:T(1,128)S(1)}, u32[]{:S(2)}, u32[]{:S(2)}) collective-permute-start(f32[1,256]{1,0:T(1,128)S(1)} %fusion.24), channel_id=1, source_target_pairs={{0,8},{8,16},{16,24},{24,32},{32,40},{40,48},{48,56},{56,64},{64,7... | collective-permute-start | bytes 3080 | tf_op jit(solution)/shard_map/ppermute | solution.py:19
  119.3 4.9 %collective-permute-start.9 = (f32[1,256]{1,0:T(1,128)S(1)}, f32[1,256]{1,0:T(1,128)S(1)}, u32[]{:S(2)}, u32[]{:S(2)}) collective-permute-start(f32[1,256]{1,0:T(1,128)S(1)} %fusion.24), channel_id=1, source_target_pairs={{8,0},{16,8},{24,16},{32,24},{40,32},{48,40},{56,48},{64,56},{72,6... | collective-permute-start | bytes 3080 | tf_op jit(solution)/shard_map/ppermute | solution.py:22
  124.2 5.9 %collective-permute-start.10 = (f32[1,256]{1,0:T(1,128)S(1)}, f32[1,256]{1,0:T(1,128)S(1)}, u32[]{:S(2)}, u32[]{:S(2)}) collective-permute-start(f32[1,256]{1,0:T(1,128)S(1)} %bitcast.122), channel_id=1, source_target_pairs={{0,1},{1,2},{2,3},{3,4},{4,5},{5,6},{6,7},{8,9},{9,10},{10,11},{11... | collective-permute-start | bytes 3080 | tf_op jit(solution)/shard_map/ppermute | solution.py:19
  126.3 11.7 %collective-permute-start.11 = (f32[1,256]{1,0:T(1,128)S(1)}, f32[1,256]{1,0:T(1,128)S(1)}, u32[]{:S(2)}, u32[]{:S(2)}) collective-permute-start(f32[1,256]{1,0:T(1,128)S(1)} %bitcast.123), channel_id=1, source_target_pairs={{1,0},{2,1},{3,2},{4,3},{5,4},{6,5},{7,6},{9,8},{10,9},{11,10},{12... | collective-permute-start | bytes 3080 | tf_op jit(solution)/shard_map/ppermute | solution.py:22
  130.2 10.6 %collective-permute-start.6 = (f32[1,256,256]{2,1,0:T(8,128)S(1)}, f32[1,256,256]{2,1,0:T(8,128)S(1)}, u32[]{:S(2)}, u32[]{:S(2)}) collective-permute-start(f32[1,256,256]{2,1,0:T(8,128)S(1)} %fusion.32), channel_id=1, source_target_pairs={{0,1},{1,2},{2,3},{3,4},{4,5},{5,6},{6,7},{8,9},{9,10},{10,11},{11... | collective-permute-start | bytes 786440 | tf_op jit(solution)/shard_map/ppermute | solution.py:19
  135.9 12.6 %collective-permute-start.7 = (f32[1,256,256]{2,1,0:T(8,128)S(1)}, f32[1,256,256]{2,1,0:T(8,128)S(1)}, u32[]{:S(2)}, u32[]{:S(2)}) collective-permute-start(f32[1,256,256]{2,1,0:T(8,128)S(1)} %fusion.32), channel_id=1, source_target_pairs={{1,0},{2,1},{3,2},{4,3},{5,4},{6,5},{7,6},{9,8},{10,9},{11,10},{12... | collective-permute-start | bytes 786440 | tf_op jit(solution)/shard_map/ppermute | solution.py:22
  226.7 6.9 %collective-permute-start.12 = (bf16[8,1,8192]{2,0,1:T(8,128)(2,1)S(1)}, bf16[8,1,8192]{2,0,1:T(8,128)(2,1)S(1)}, u32[]{:S(2)}, u32[]{:S(2)}) collective-permute-start(bf16[8,1,8192]{2,0,1:T(8,128)(2,1)S(1)} %get-tuple-element.62), channel_id=1, source_target_pairs={{0,1},{1,2},{2,3},{3,4},{4,5},{5,6},{6,7},{8,9},{9,10},{10,11},{11... | collective-permute-start | bytes 393224 | tf_op jit(solution)/shard_map/ppermute | solution.py:19
  228.8 10.5 %collective-permute-start.13 = (bf16[8,1,8192]{2,0,1:T(8,128)(2,1)S(1)}, bf16[8,1,8192]{2,0,1:T(8,128)(2,1)S(1)}, u32[]{:S(2)}, u32[]{:S(2)}) collective-permute-start(bf16[8,1,8192]{2,0,1:T(8,128)(2,1)S(1)} %get-tuple-element.63), channel_id=1, source_target_pairs={{1,0},{2,1},{3,2},{4,3},{5,4},{6,5},{7,6},{9,8},{10,9},{11,10},{12... | collective-permute-start | bytes 393224 | tf_op jit(solution)/shard_map/ppermute | solution.py:22
where the time goes:
time: 246 us; the launch traced here: 245 us
  waiting for transfers between devices  77.8 us (32%)
  blocking collectives  64.3 us (26%)
  starting transfers between devices  55.1 us (22%)
  local copies, waits for them, and re-layouts  19.4 us (8%)
  matrix products  15.8 us (6%)
  other arithmetic  11 us (4%)
    all_to_all x1, blocking collectives, body(): lax.all_to_all(updated, MEM, split_axis=0, concat_axis=2, tiled=True)  58.9 us
    all_to_all x1, waiting for transfers between devices, turned_blocks(): lax.all_to_all(tiles, axes[k], split_axis=k, concat_axis=k, tiled=True)  49.1 us
    ppermute x7, starting transfers between devices, padded_2(): lax.ppermute(lax.slice_in_dim(block, block.shape[dim] - width, None, axis...  25.7 us
    ppermute x7, waiting for transfers between devices, padded_2(): lax.ppermute(lax.slice_in_dim(block, 0, width, axis=dim), axis, backward)  22.1 us
    ppermute x7, starting transfers between devices, padded_2(): lax.ppermute(lax.slice_in_dim(block, 0, width, axis=dim), axis, backward)  20.8 us
    all_to_all x1, starting transfers between devices, turned_blocks(): lax.all_to_all(tiles, axes[k], split_axis=k, concat_axis=k, tiled=True)  8.61 us
    ppermute x7, waiting for transfers between devices, padded_2(): lax.ppermute(lax.slice_in_dim(block, block.shape[dim] - width, None, axis...  6.65 us
    dot_general x10, matrix products, newton(): jnp.dot(root_part, factor, precision=HIGHEST)  5.96 us
  transfers between devices with their start and end apart: 15, of which 8 were waited for; matrix products, arithmetic and copies ran while one was open for 1% of the time, Pallas kernels for 0%

commit v1 on v0

v1 whole, which is shorter than its diff:
```python
import jax
import jax.numpy as jnp
from jax import lax
from jax.experimental import pallas as pl
from jax.experimental.pallas import tpu as pltpu
from jax.sharding import Mesh
from jax.sharding import PartitionSpec as P

ITERS = 10
MEM = ("mem_0", "mem_1", "mem_2")
F32 = jnp.float32
BF16 = jnp.bfloat16
VMEM_LIMIT = 48 << 20


def params():
    return pltpu.CompilerParams(vmem_limit_bytes=VMEM_LIMIT)


def vmem_specs(count):
    return [pl.BlockSpec(memory_space=pltpu.VMEM) for _ in range(count)]


def sides(window):
    width = window.shape[1]
    both = pltpu.roll(window, 1, axis=1) + pltpu.roll(window, width - 1, axis=1)
    return both[:, 128 : width - 128]


def forecast_kernel(x_ref, top_ref, bot_ref, coef_ref, out_ref, v1_ref):
    rows, _, width = x_ref.shape
    patches = out_ref.shape[0]
    cols = width // patches

    def source(r, off, size):
        if r < 0:
            piece = top_ref[r + 2, :, pl.ds(off, size)]
        elif r >= rows:
            piece = bot_ref[r - rows, :, pl.ds(off, size)]
        else:
            piece = x_ref[r, :, pl.ds(off, size)]
        return piece.astype(F32)

    def offsets(q):
        off = pl.multiple_of(q * cols, cols)
        before = pl.multiple_of(jnp.maximum(off - 128, 0), 128)
        after = pl.multiple_of(jnp.minimum(off + cols, width - 128), 128)
        return off, before, after

    def window(load, q):
        off, before, after = offsets(q)
        left = jnp.where(q > 0, load(before, 128), 0.0)
        right = jnp.where(q < patches - 1, load(after, 128), 0.0)
        return jnp.concatenate([left, load(off, cols), right], axis=1)

    def first(q, carry):
        off, _, _ = offsets(q)
        for e in range(rows + 2):
            r = e - 1
            wide = window(lambda o, s: source(r, o, s), q)
            mid = wide[:, 128 : 128 + cols]
            lap = source(r - 1, off, cols) + source(r + 1, off, cols) + sides(wide) - 4.0 * mid
            v1_ref[e, :, pl.ds(off, cols)] = mid + coef_ref[e : e + 1, pl.ds(off, cols)] * lap
        return carry

    def second(q, carry):
        off, _, _ = offsets(q)
        for a in range(rows):
            e = a + 1
            wide = window(lambda o, s: v1_ref[e, :, pl.ds(o, s)], q)
            mid = wide[:, 128 : 128 + cols]
            lap = (
                v1_ref[e - 1, :, pl.ds(off, cols)]
                + v1_ref[e + 1, :, pl.ds(off, cols)]
                + sides(wide)
                - 4.0 * mid
            )
            fresh = mid + coef_ref[e : e + 1, pl.ds(off, cols)] * lap
            out_ref[q, :, a * cols : (a + 1) * cols] = fresh.astype(BF16)
        return carry

    lax.fori_loop(0, patches, first, 0)
    lax.fori_loop(0, patches, second, 0)


def forecast(x, top, bot, coef, patches):
    rows, members, width = x.shape
    return pl.pallas_call(
        forecast_kernel,
        out_shape=jax.ShapeDtypeStruct((patches, members, rows * width // patches), BF16),
        in_specs=vmem_specs(4),
        out_specs=pl.BlockSpec(memory_space=pltpu.VMEM),
        scratch_shapes=[pltpu.VMEM((rows + 2, members, width), F32)],
        compiler_params=params(),
        name="forecast",
    )(x, top, bot, coef)


def observe_kernel(block_ref, site_ref, out_ref, *, cols):
    patches, members, cells = block_ref.shape
    count = site_ref.shape[1]
    rows = cells // cols

    def one(q, carry):
        site = site_ref[pl.ds(q, 1), :]
        row = lax.shift_right_logical(site, cols.bit_length() - 1)
        col = lax.bitwise_and(site, cols - 1)
        lanes = lax.broadcasted_iota(jnp.int32, (cols, count), 0)
        chosen = jnp.where(lanes == col, 1.0, 0.0).astype(BF16)
        stacked = jnp.concatenate(
            [block_ref[q, :, a * cols : (a + 1) * cols].astype(F32) for a in range(rows)], axis=0
        ).astype(BF16)
        picked = jnp.dot(stacked, chosen, preferred_element_type=F32)
        total = jnp.zeros((members, count), F32)
        for a in range(rows):
            total = jnp.where(row == a, picked[a * members : (a + 1) * members, :], total)
        out_ref[q, :, :] = total.astype(BF16)
        return carry

    lax.fori_loop(0, patches, one, 0)


def observe(blocks, sites, cols):
    patches, members, _ = blocks.shape
    return pl.pallas_call(
        lambda *refs: observe_kernel(*refs, cols=cols),
        out_shape=jax.ShapeDtypeStruct((patches, members, sites.shape[1]), BF16),
        in_specs=vmem_specs(2),
        out_specs=pl.BlockSpec(memory_space=pltpu.VMEM),
        compiler_params=params(),
        name="observe",
    )(blocks, sites)


def gram_kernel(obs_ref, value_ref, weight_ref, out_ref):
    groups, each, count = obs_ref.shape
    members = groups * each
    observed = obs_ref[...].astype(F32).reshape(members, count)
    mean = jnp.sum(observed, axis=0, keepdims=True) * (1.0 / members)
    root = jnp.sqrt(weight_ref[...])
    spread = ((observed - mean) * root).astype(BF16)
    innovation = ((value_ref[...] - mean) * root).astype(BF16)
    tail = jnp.broadcast_to(innovation.astype(F32), (16, count)).astype(BF16)
    left = jnp.concatenate([spread, tail], axis=0)
    both = lax.dot_general(left, spread, (((1,), (1,)), ((), ())), preferred_element_type=F32)
    out_ref[...] = both[: members + 8]


def gram_of(obs, values, weights):
    members = obs.shape[0] * obs.shape[1]
    return pl.pallas_call(
        gram_kernel,
        out_shape=jax.ShapeDtypeStruct((members + 8, members), F32),
        in_specs=vmem_specs(3),
        out_specs=pl.BlockSpec(memory_space=pltpu.VMEM),
        compiler_params=params(),
        name="gram",
    )(obs, values, weights)


def halves(value):
    high = value.astype(BF16)
    return high, (value - high.astype(F32)).astype(BF16)


def product(left, right):
    lh, ll = left
    rh, rl = right
    return (
        jnp.dot(lh, rh, preferred_element_type=F32)
        + jnp.dot(lh, rl, preferred_element_type=F32)
        + jnp.dot(ll, rh, preferred_element_type=F32)
    )


def root_kernel(low_ref, mid_ref, high_ref, out_ref):
    members = out_ref.shape[0]
    gram = 0.5 * low_ref[...] + mid_ref[...] + 0.5 * high_ref[...]
    vector = gram[members : members + 8]
    across = lax.broadcasted_iota(jnp.int32, (members, members), 0)
    along = lax.broadcasted_iota(jnp.int32, (members, members), 1)
    identity = jnp.where(across == along, 1.0, 0.0)
    system = gram[:members] + (members - 1.0) * identity
    squares = jnp.sum(jnp.sum(system * system, axis=0, keepdims=True), axis=1, keepdims=True)
    frob = jnp.sqrt(squares)
    root = system / frob
    factor = 1.5 * identity - 0.5 * root
    inverse = factor
    root = product(halves(root), halves(factor))
    for step in range(1, ITERS):
        root_h = halves(root)
        inverse_h = halves(inverse)
        factor_h = halves(1.5 * identity - 0.5 * product(inverse_h, root_h))
        if step < ITERS - 1:
            root = product(root_h, factor_h)
        inverse = product(factor_h, inverse_h)
    inverse_h = halves(inverse)
    weights = product(halves(product(halves(vector), inverse_h)), inverse_h) / frob
    scale = jnp.sqrt(members - 1.0) * lax.rsqrt(frob)
    out_ref[...] = (scale * inverse + weights[0:1]).astype(BF16)


def root_of(low, mid, high):
    members = mid.shape[1]
    return pl.pallas_call(
        root_kernel,
        out_shape=jax.ShapeDtypeStruct((members, members), BF16),
        in_specs=vmem_specs(3),
        out_specs=pl.BlockSpec(memory_space=pltpu.VMEM),
        compiler_params=params(),
        name="root",
    )(low, mid, high)


def update_kernel(turned_ref, block_ref, out_ref):
    groups, each, cells = block_ref.shape
    members = groups * each
    step = 512

    def one(c, carry):
        where = pl.ds(pl.multiple_of(c * step, step), step)
        cellwise = block_ref[:, :, where].astype(F32).reshape(members, step)
        mean = jnp.sum(cellwise, axis=0, keepdims=True) * (1.0 / members)
        deviation = (cellwise - mean).astype(BF16)
        moved = jnp.dot(turned_ref[...], deviation, preferred_element_type=F32)
        out_ref[:, :, where] = (mean + moved).reshape(groups, each, step).astype(BF16)
        return carry

    lax.fori_loop(0, cells // step, one, 0)


def update(turned, blocks):
    return pl.pallas_call(
        update_kernel,
        out_shape=jax.ShapeDtypeStruct(blocks.shape, BF16),
        in_specs=vmem_specs(2),
        out_specs=pl.BlockSpec(memory_space=pltpu.VMEM),
        compiler_params=params(),
        name="update",
    )(turned, blocks)


def finish_kernel(block_ref, top_ref, bot_ref, coef_ref, out_ref):
    patches, _, _ = block_ref.shape
    rows, _, width = out_ref.shape
    cols = width // patches

    def one(q, carry):
        off = pl.multiple_of(q * cols, cols)
        before = jnp.maximum(q - 1, 0)
        after = jnp.minimum(q + 1, patches - 1)
        mids = [top_ref[q].astype(F32)]
        for a in range(rows):
            mids.append(block_ref[q, :, a * cols : (a + 1) * cols].astype(F32))
        mids.append(bot_ref[q].astype(F32))
        for a in range(rows):
            left = block_ref[before, :, (a + 1) * cols - 128 : (a + 1) * cols].astype(F32)
            right = block_ref[after, :, a * cols : a * cols + 128].astype(F32)
            left = jnp.where(q > 0, left, 0.0)
            right = jnp.where(q < patches - 1, right, 0.0)
            mid = mids[a + 1]
            wide = jnp.concatenate([left, mid, right], axis=1)
            lap = mids[a] + mids[a + 2] + sides(wide) - 4.0 * mid
            done = mid + coef_ref[a : a + 1, pl.ds(off, cols)] * lap
            out_ref[a, :, pl.ds(off, cols)] = done.astype(BF16)
        return carry

    lax.fori_loop(0, patches, one, 0)


def finish(blocks, top, bot, coef):
    _, members, _ = blocks.shape
    rows, width = coef.shape
    return pl.pallas_call(
        finish_kernel,
        out_shape=jax.ShapeDtypeStruct((rows, members, width), BF16),
        in_specs=vmem_specs(4),
        out_specs=pl.BlockSpec(memory_space=pltpu.VMEM),
        compiler_params=params(),
        name="finish",
    )(blocks, top, bot, coef)


def from_both(axis, low_part, high_part):
    count = lax.axis_size(axis)
    forward = [(i, i + 1) for i in range(count - 1)]
    backward = [(i + 1, i) for i in range(count - 1)]
    return lax.ppermute(low_part, axis, forward), lax.ppermute(high_part, axis, backward)


def body(
    prior_samples,
    diffusivity_field,
    measured_site_position,
    measured_quantities,
    measurement_weightings,
):
    _, _, width = prior_samples.shape
    patches = lax.axis_size(MEM)
    cols = width // patches
    coef_low, coef_high = from_both("space", diffusivity_field[-1:], diffusivity_field[:1])
    top, bot = from_both(
        "space", jnp.swapaxes(prior_samples[:, -2:], 0, 1), jnp.swapaxes(prior_samples[:, :2], 0, 1)
    )
    sites = lax.all_to_all(
        jnp.broadcast_to(measured_site_position[0], (patches, measured_site_position.shape[2])),
        MEM, 0, 0, tiled=True,
    )
    coef = jnp.concatenate([coef_low, diffusivity_field, coef_high], axis=0)
    blocks = forecast(jnp.swapaxes(prior_samples, 0, 1), top, bot, coef, patches)
    obs = lax.all_to_all(observe(blocks, sites, cols), MEM, 0, 0, tiled=True)
    gathered = lax.all_to_all(blocks, MEM, 0, 0, tiled=True)
    own = gram_of(obs, measured_quantities[0], measurement_weightings[0])
    low, high = from_both(MEM, own, own)
    band = 0.5 * low + own + 0.5 * high
    low, high = from_both("space", band, band)
    turned = root_of(low, band, high)
    updated = update(turned, gathered)
    returned = lax.all_to_all(updated, MEM, 0, 0, tiled=True)
    top, bot = from_both("space", returned[:, :, -cols:], returned[:, :, :cols])
    done = finish(returned, top, bot, diffusivity_field)
    return jnp.swapaxes(done, 0, 1)


def solution(mesh):
    finer = Mesh(
        mesh.devices.reshape(2, 8, 2, mesh.shape["space"]), ("mem_0", "mem_1", "mem_2", "space")
    )
    in_specs = (
        P(MEM, "space", None),
        P("space", None),
        P("space", MEM, None),
        P("space", MEM, None),
        P("space", MEM, None),
    )
    out_specs = P(MEM, "space", None)
    return jax.shard_map(body, mesh=finer, in_specs=in_specs, out_specs=out_specs, check_vma=False)
```

time: 246 us -> 240 us (0.976)
  Pallas kernels: 0 us -> 34.2 us
  matrix products: 15.8 us -> 0 us
  local copies, waits for them, and re-layouts: 19.4 us -> 7.83 us
  blocking collectives: 64.3 us -> 75.2 us
  other arithmetic: 11 us -> 0.17 us
  waiting for transfers between devices: 77.8 us -> 69.8 us
  starting transfers between devices: 55.1 us -> 51.4 us
    all_to_all x1 -> x2, waiting for transfers between devices: 49.1 us -> 7.76 us  [the longest x1 7.75 us: body(): lax.all_to_all(jnp.broadcast_to(measured_site_position[0], (patches, meas...]
    pallas_call x0 -> x6, Pallas kernels: none -> 34.2 us  [the longest x1 12.4 us: forecast(): pl.pallas_call(forecast_kernel, out_shape=jax.ShapeDtypeStruct((patches,...]
    ppermute x14 -> x10, waiting for transfers between devices: 28.7 us -> 62 us  [the longest x5 48.6 us: from_both(): lax.ppermute(low_part, axis, forward)]
    dot_general x35 -> x0, matrix products: 15.8 us -> none  [the longest x10 5.96 us: newton(): jnp.dot(root_part, factor, precision=HIGHEST)]
    all_to_all x2, blocking collectives: 64.3 us -> 75.2 us  [the longest x1 59 us: body(): returned = lax.all_to_all(updated, MEM, 0, 0, tiled=True)]
    ppermute x14 -> x10, starting transfers between devices: 46.5 us -> 37.6 us  [the longest x5 24.3 us: from_both(): lax.ppermute(low_part, axis, forward)]
    convert_element_type x6 -> x0, other arithmetic: 6.41 us -> none  [the longest x1 2.75 us: body(): (returned.astype(jnp.float32) + diffusivity_field[None] * interior(extend...]
    all_to_all x1 -> x2, starting transfers between devices: 8.61 us -> 13.8 us  [the longest x1 8.75 us: body(): lax.all_to_all(jnp.broadcast_to(measured_site_position[0], (patches, meas...]
  transfers between devices with their start and end apart: 15 -> 12, of which waited for: 8 -> 6; matrix products, arithmetic and copies ran while one was open for 1% -> 2% of each run, Pallas kernels for 0% -> 3%
where the time goes in v1:
time: 240 us; the launch traced here: 239 us
  blocking collectives  75.2 us (31%)
  waiting for transfers between devices  69.8 us (29%)
  starting transfers between devices  51.4 us (21%)
  Pallas kernels  34.2 us (14%)
  local copies, waits for them, and re-layouts  7.83 us (3%)
    all_to_all x1, blocking collectives, body(): returned = lax.all_to_all(updated, MEM, 0, 0, tiled=True)  59 us
    ppermute x5, waiting for transfers between devices, from_both(): lax.ppermute(low_part, axis, forward)  48.6 us
    ppermute x5, starting transfers between devices, from_both(): lax.ppermute(low_part, axis, forward)  24.3 us
    all_to_all x1, blocking collectives, body(): obs = lax.all_to_all(observe(blocks, sites, cols), MEM, 0, 0, tiled=True)  16.2 us
    ppermute x5, waiting for transfers between devices, from_both(): lax.ppermute(high_part, axis, backward)  13.4 us
    ppermute x5, starting transfers between devices, from_both(): lax.ppermute(high_part, axis, backward)  13.2 us
    pallas_call x1, Pallas kernels, forecast(): pl.pallas_call(forecast_kernel, out_shape=jax.ShapeDtypeStruct((patches,...  12.4 us
    all_to_all x1, starting transfers between devices, body(): lax.all_to_all(jnp.broadcast_to(measured_site_position[0], (patches, meas...  8.75 us
  transfers between devices with their start and end apart: 12, of which 6 were waited for; matrix products, arithmetic and copies ran while one was open for 2% of the time, Pallas kernels for 3%

profile of v1, /device:TPU:56, one launch (start us, length us, event | category | flops | bytes accessed | tf_op | source)
XLA Modules:
  0.0 238.8 jit_solution(8347624423044341290)
XLA Ops:
  1.1 4.6 %collective-permute-start.2 = (f32[1,8192]{1,0:T(1,128)S(1)}, f32[1,8192]{1,0:T(1,128)S(1)}, u32[]{:S(2)}, u32[]{:S(2)}) collective-permute-start(f32[1,8192]{1,0:T(1,128)S(1)} %get-tuple-element.11), channel_id=1, source_target_pairs={{0,1},{1,2},{2,3},{3,4},{4,5},{5,6},{6,7},{8,9},{9,10},{10,11},{11... | collective-permute-start | bytes 98312 | tf_op jit(solution)/shard_map/ppermute | solution.py:288
  5.7 2.1 collective-permute-start.3
  7.8 2.8 %copy.19 = bf16[8,16,8192]{2,0,1:T(8,128)(2,1)S(1)} copy(bf16[8,16,8192]{2,1,0:T(8,128)(2,1)} %param.5) | data formatting | bytes 4194304 | tf_op args[0]
  11.3 7.5 %collective-permute-start = (bf16[2,8,8192]{2,1,0:T(8,128)(2,1)}, bf16[2,8,8192]{2,1,0:T(8,128)(2,1)}, u32[]{:S(2)}, u32[]{:S(2)}) collective-permute-start(bf16[2,8,8192]{2,1,0:T(8,128)(2,1)} %get-tuple-element.8), channel_id=1, source_target_pairs={{0,1},{1,2},{2,3},{3,4},{4,5},{5,6},{6,7},{8,9},{9,10},{10,11},{11... | collective-permute-start | bytes 786440 | tf_op jit(solution)/shard_map/ppermute | solution.py:288
  21.5 8.8 %all-to-all-start = ((s32[32,1,512]{2,1,0:T(1,128)}), s32[32,1,512]{2,1,0:T(1,128)S(1)}, u32[]{:S(2)}, u32[]{:S(2)}) async-start(s32[32,1,512]{2,1,0:T(1,128)} %broadcast_in_dim.2), calls=%async_computation | async-start | bytes 131072 | tf_op jit(solution)/shard_map/all_to_all | solution.py:305
  30.4 7.8 %all-to-all-done = s32[32,1,512]{2,1,0:T(1,128)S(1)} async-done(((s32[32,1,512]{2,1,0:T(1,128)}), s32[32,1,512]{2,1,0:T(1,128)S(1)}, u32[]{:S(2)}, u32[]{:S(2)}) %all-to-all-start) | async-done | bytes 65568 | tf_op jit(solution)/shard_map/all_to_all | solution.py:305
  38.2 12.4 %forecast.1.refs_0_ = bf16[32,8,4096]{2,1,0:T(8,128)(2,1)} custom-call(bf16[16,8,8192]{2,1,0:T(8,128)(2,1)S(1)} %bitcast.13, bf16[2,8,8192]{2,1,0:T(8,128)(2,1)} %collective-permute-done.top_ref, bf16[2,8,8192]{2,1,0:T(8,128)(2,1)} %collective-permute-done.1.bot_ref, f32[18,8192]{1,0:T(8,128)S(1)} %pad_maximum_fusion.coef_ref), custom_call_target="tpu_custom_call" | custom-call | tf_op jit(solution)/shard_map/forecast/pallas_call | solution.py:88
  50.5 7.9 %observe.1 = bf16[32,8,512]{2,1,0:T(8,128)(2,1)S(1)} custom-call(bf16[32,8,4096]{2,1,0:T(8,128)(2,1)} %forecast.1.refs_0_, s32[32,512]{1,0:T(8,128)S(1)} %bitcast.15), custom_call_target="tpu_custom_call" | custom-call | tf_op jit(solution)/shard_map/observe/pallas_call | solution.py:125
  58.5 16.2 %all_to_all.23.obs_ref = bf16[32,8,512]{2,1,0:T(8,128)(2,1)S(1)} all-to-all(bf16[32,8,512]{2,1,0:T(8,128)(2,1)S(1)} %observe.1), channel_id=1, replica_groups=mesh['mem_0'=2,'mem_1'=8,'mem_2'=2,'space'=8] {'mem_0','mem_1','mem_2'}, dimensions={0} | all-to-all | bytes 524288 | tf_op jit(solution)/shard_map/all_to_all | solution.py:311
  74.7 5.1 %all-to-all-start.2 = ((bf16[32,8,4096]{2,1,0:T(8,128)(2,1)}), bf16[32,8,4096]{2,1,0:T(8,128)(2,1)S(1)}, u32[]{:S(2)}, u32[]{:S(2)}) async-start(bf16[32,8,4096]{2,1,0:T(8,128)(2,1)} %forecast.1.refs_0_), calls=%async_computation.2 | async-start | bytes 4194304 | tf_op jit(solution)/shard_map/all_to_all | solution.py:312
  80.2 2.0 collective-permute-start.4
  82.2 3.5 %collective-permute-start.5 = (f32[264,256]{1,0:T(8,128)S(1)}, f32[264,256]{1,0:T(8,128)S(1)}, u32[]{:S(2)}, u32[]{:S(2)}) collective-permute-start(f32[264,256]{1,0:T(8,128)S(1)} %gram.1), channel_id=1, source_target_pairs={{8,0},{16,8},{24,16},{32,24},{40,32},{48,40},{56,48},{64,56},{72,6... | collective-permute-start | bytes 811016 | tf_op jit(solution)/shard_map/ppermute | solution.py:288
  85.7 43.5 %collective-permute-done.4 = f32[264,256]{1,0:T(8,128)S(1)} collective-permute-done((f32[264,256]{1,0:T(8,128)S(1)}, f32[264,256]{1,0:T(8,128)S(1)}, u32[]{:S(2)}, u32[]{:S(2)}) %collective-permute-start.4) | collective-permute-done | bytes 270368 | tf_op jit(solution)/shard_map/ppermute | solution.py:288
  129.3 8.1 %collective-permute-start.6 = (f32[264,256]{1,0:T(8,128)S(1)}, f32[264,256]{1,0:T(8,128)S(1)}, u32[]{:S(2)}, u32[]{:S(2)}) collective-permute-start(f32[264,256]{1,0:T(8,128)S(1)} %multiply_add_fusion.mid_ref), channel_id=1, source_target_pairs={{0,1},{1,2},{2,3},{3,4},{4,5},{5,6},{6,7},{8,9},{9,10},{10,11},{11... | collective-permute-start | bytes 811016 | tf_op jit(solution)/shard_map/ppermute | solution.py:288
  139.4 4.1 %collective-permute-done.6.low_ref = f32[264,256]{1,0:T(8,128)S(1)} collective-permute-done((f32[264,256]{1,0:T(8,128)S(1)}, f32[264,256]{1,0:T(8,128)S(1)}, u32[]{:S(2)}, u32[]{:S(2)}) %collective-permute-start.6) | collective-permute-done | bytes 270368 | tf_op jit(solution)/shard_map/ppermute | solution.py:288
  143.5 7.7 %collective-permute-done.7.high_ref = f32[264,256]{1,0:T(8,128)S(1)} collective-permute-done((f32[264,256]{1,0:T(8,128)S(1)}, f32[264,256]{1,0:T(8,128)S(1)}, u32[]{:S(2)}, u32[]{:S(2)}) %collective-permute-start.7) | collective-permute-done | bytes 270368 | tf_op jit(solution)/shard_map/ppermute | solution.py:288
  151.2 6.8 %root.1.turned_ref = bf16[256,256]{1,0:T(8,128)(2,1)S(1)} custom-call(f32[264,256]{1,0:T(8,128)S(1)} %collective-permute-done.6.low_ref, f32[264,256]{1,0:T(8,128)S(1)} %multiply_add_fusion.mid_ref, f32[264,256]{1,0:T(8,128)S(1)} %collective-permute-done.7.high_ref), custom_call_target="tpu_custom_call" | custom-call | tf_op jit(solution)/shard_map/root/pallas_call | solution.py:205
  158.0 2.6 %update.1 = bf16[32,8,4096]{2,1,0:T(8,128)(2,1)S(1)} custom-call(bf16[256,256]{1,0:T(8,128)(2,1)S(1)} %root.1.turned_ref, bf16[32,8,4096]{2,1,0:T(8,128)(2,1)S(1)} %all-to-all-done.2.block_ref), custom_call_target="tpu_custom_call" | custom-call | tf_op jit(solution)/shard_map/update/pallas_call | solution.py:233
  160.6 59.0 %all_to_all.24.block_ref = bf16[32,8,4096]{2,1,0:T(8,128)(2,1)S(1)} all-to-all(bf16[32,8,4096]{2,1,0:T(8,128)(2,1)S(1)} %update.1), channel_id=1, replica_groups=mesh['mem_0'=2,'mem_1'=8,'mem_2'=2,'space'=8] {'mem_0','mem_1','mem_2'}, dimensions={0} | all-to-all | bytes 4194304 | tf_op jit(solution)/shard_map/all_to_all | solution.py:319
  219.6 2.1 collective-permute-start.8
  221.6 3.8 %collective-permute-start.9 = (bf16[32,8,256]{2,1,0:T(8,128)(2,1)S(1)}, bf16[32,8,256]{2,1,0:T(8,128)(2,1)S(1)}, u32[]{:S(2)}, u32[]{:S(2)}) collective-permute-start(bf16[32,8,256]{2,1,0:T(8,128)(2,1)S(1)} %get-tuple-element.5), channel_id=1, source_target_pairs={{1,0},{2,1},{3,2},{4,3},{5,4},{6,5},{7,6},{9,8},{10,9},{11,10},{12... | collective-permute-start | bytes 393224 | tf_op jit(solution)/shard_map/ppermute | solution.py:288
  226.4 5.7 %collective-permute-done.9.bot_ref = bf16[32,8,256]{2,1,0:T(8,128)(2,1)S(1)} collective-permute-done((bf16[32,8,256]{2,1,0:T(8,128)(2,1)S(1)}, bf16[32,8,256]{2,1,0:T(8,128)(2,1)S(1)}, u32[]{:S(2)}, u32[]{:S(2)}) %collective-permute-start.9) | collective-permute-done | bytes 131104 | tf_op jit(solution)/shard_map/ppermute | solution.py:288
  232.1 4.2 %finish.1 = bf16[16,8,8192]{2,1,0:T(8,128)(2,1)S(1)} custom-call(bf16[32,8,4096]{2,1,0:T(8,128)(2,1)S(1)} %all_to_all.24.block_ref, bf16[32,8,256]{2,1,0:T(8,128)(2,1)S(1)} %collective-permute-done.8.top_ref, bf16[32,8,256]{2,1,0:T(8,128)(2,1)S(1)} %collective-permute-done.9.bot_ref, f32[16,8192]{1,0:T(8,128)S(1)} %copy-done), custom_call_target="tpu_custom_call" | custom-call | tf_op jit(solution)/shard_map/finish/pallas_call | solution.py:274
  236.3 2.5 %copy.13 = bf16[8,16,8192]{2,1,0:T(8,128)(2,1)} copy(bf16[8,16,8192]{2,0,1:T(8,128)(2,1)S(1)} %bitcast.14) | data formatting | bytes 4194304 | tf_op jit(solution)/shard_map/transpose | solution.py:322
  (25 shorter events, 8.0 us)
Async XLA Ops:
  1.1 29.2 %collective-permute-start.2 = (f32[1,8192]{1,0:T(1,128)S(1)}, f32[1,8192]{1,0:T(1,128)S(1)}, u32[]{:S(2)}, u32[]{:S(2)}) collective-permute-start(f32[1,8192]{1,0:T(1,128)S(1)} %get-tuple-element.11), channel_id=1, source_target_pairs={{0,1},{1,2},{2,3},{3,4},{4,5},{5,6},{6,7},{8,9},{9,10},{10,11},{11... | collective-permute-start | bytes 98312 | tf_op jit(solution)/shard_map/ppermute | solution.py:288
  5.7 15.1 %copy-start.3 = (s32[1,1,512]{2,1,0:T(1,128)S(1)}, s32[1,1,512]{2,1,0:T(1,128)}, u32[]{:S(2)}) copy-start(s32[1,1,512]{2,1,0:T(1,128)} %param.7) | copy-start | bytes 6148
  5.7 24.6 %copy-start = (f32[16,8192]{1,0:T(8,128)S(1)}, f32[16,8192]{1,0:T(8,128)}, u32[]{:S(2)}) copy-start(f32[16,8192]{1,0:T(8,128)} %coef_ref.1) | copy-start | bytes 1572868
  5.7 24.5 %collective-permute-start.3 = (f32[1,8192]{1,0:T(1,128)S(1)}, f32[1,8192]{1,0:T(1,128)S(1)}, u32[]{:S(2)}, u32[]{:S(2)}) collective-permute-start(f32[1,8192]{1,0:T(1,128)S(1)} %get-tuple-element.12), channel_id=1, source_target_pairs={{1,0},{2,1},{3,2},{4,3},{5,4},{6,5},{7,6},{9,8},{10,9},{11,10},{12... | collective-permute-start | bytes 98312 | tf_op jit(solution)/shard_map/ppermute | solution.py:288
  11.3 26.8 %collective-permute-start = (bf16[2,8,8192]{2,1,0:T(8,128)(2,1)}, bf16[2,8,8192]{2,1,0:T(8,128)(2,1)}, u32[]{:S(2)}, u32[]{:S(2)}) collective-permute-start(bf16[2,8,8192]{2,1,0:T(8,128)(2,1)} %get-tuple-element.8), channel_id=1, source_target_pairs={{0,1},{1,2},{2,3},{3,4},{4,5},{5,6},{6,7},{8,9},{9,10},{10,11},{11... | collective-permute-start | bytes 786440 | tf_op jit(solution)/shard_map/ppermute | solution.py:288
  18.9 19.3 %collective-permute-start.1 = (bf16[2,8,8192]{2,1,0:T(8,128)(2,1)}, bf16[2,8,8192]{2,1,0:T(8,128)(2,1)}, u32[]{:S(2)}, u32[]{:S(2)}) collective-permute-start(bf16[2,8,8192]{2,1,0:T(8,128)(2,1)} %get-tuple-element.7), channel_id=1, source_target_pairs={{1,0},{2,1},{3,2},{4,3},{5,4},{6,5},{7,6},{9,8},{10,9},{11,10},{12... | collective-permute-start | bytes 786440 | tf_op jit(solution)/shard_map/ppermute | solution.py:288
  21.5 16.7 %all-to-all-start = ((s32[32,1,512]{2,1,0:T(1,128)}), s32[32,1,512]{2,1,0:T(1,128)S(1)}, u32[]{:S(2)}, u32[]{:S(2)}) async-start(s32[32,1,512]{2,1,0:T(1,128)} %broadcast_in_dim.2), calls=%async_computation | async-start | bytes 131072 | tf_op jit(solution)/shard_map/all_to_all | solution.py:305
  74.7 5.1 %copy-start.1 = (f32[1,1,512]{2,1,0:T(1,128)S(1)}, f32[1,1,512]{2,1,0:T(1,128)}, u32[]{:S(2)}) copy-start(f32[1,1,512]{2,1,0:T(1,128)} %param.8) | copy-start | bytes 6148
  74.7 5.1 %copy-start.2 = (f32[1,1,512]{2,1,0:T(1,128)S(1)}, f32[1,1,512]{2,1,0:T(1,128)}, u32[]{:S(2)}) copy-start(f32[1,1,512]{2,1,0:T(1,128)} %param.9) | copy-start | bytes 6148
  74.7 83.3 %all-to-all-start.2 = ((bf16[32,8,4096]{2,1,0:T(8,128)(2,1)}), bf16[32,8,4096]{2,1,0:T(8,128)(2,1)S(1)}, u32[]{:S(2)}, u32[]{:S(2)}) async-start(bf16[32,8,4096]{2,1,0:T(8,128)(2,1)} %forecast.1.refs_0_), calls=%async_computation.2 | async-start | bytes 4194304 | tf_op jit(solution)/shard_map/all_to_all | solution.py:312
  80.2 49.1 %collective-permute-start.4 = (f32[264,256]{1,0:T(8,128)S(1)}, f32[264,256]{1,0:T(8,128)S(1)}, u32[]{:S(2)}, u32[]{:S(2)}) collective-permute-start(f32[264,256]{1,0:T(8,128)S(1)} %gram.1), channel_id=1, source_target_pairs={{0,8},{8,16},{16,24},{24,32},{32,40},{40,48},{48,56},{56,64},{64,7... | collective-permute-start | bytes 811016 | tf_op jit(solution)/shard_map/ppermute | solution.py:288
  82.2 47.0 %collective-permute-start.5 = (f32[264,256]{1,0:T(8,128)S(1)}, f32[264,256]{1,0:T(8,128)S(1)}, u32[]{:S(2)}, u32[]{:S(2)}) collective-permute-start(f32[264,256]{1,0:T(8,128)S(1)} %gram.1), channel_id=1, source_target_pairs={{8,0},{16,8},{24,16},{32,24},{40,32},{48,40},{56,48},{64,56},{72,6... | collective-permute-start | bytes 811016 | tf_op jit(solution)/shard_map/ppermute | solution.py:288
  129.3 14.2 %collective-permute-start.6 = (f32[264,256]{1,0:T(8,128)S(1)}, f32[264,256]{1,0:T(8,128)S(1)}, u32[]{:S(2)}, u32[]{:S(2)}) collective-permute-start(f32[264,256]{1,0:T(8,128)S(1)} %multiply_add_fusion.mid_ref), channel_id=1, source_target_pairs={{0,1},{1,2},{2,3},{3,4},{4,5},{5,6},{6,7},{8,9},{9,10},{10,11},{11... | collective-permute-start | bytes 811016 | tf_op jit(solution)/shard_map/ppermute | solution.py:288
  137.4 13.8 %collective-permute-start.7 = (f32[264,256]{1,0:T(8,128)S(1)}, f32[264,256]{1,0:T(8,128)S(1)}, u32[]{:S(2)}, u32[]{:S(2)}) collective-permute-start(f32[264,256]{1,0:T(8,128)S(1)} %multiply_add_fusion.mid_ref), channel_id=1, source_target_pairs={{1,0},{2,1},{3,2},{4,3},{5,4},{6,5},{7,6},{9,8},{10,9},{11,10},{12... | collective-permute-start | bytes 811016 | tf_op jit(solution)/shard_map/ppermute | solution.py:288
  219.6 6.9 %collective-permute-start.8 = (bf16[32,8,256]{2,1,0:T(8,128)(2,1)S(1)}, bf16[32,8,256]{2,1,0:T(8,128)(2,1)S(1)}, u32[]{:S(2)}, u32[]{:S(2)}) collective-permute-start(bf16[32,8,256]{2,1,0:T(8,128)(2,1)S(1)} %get-tuple-element.6), channel_id=1, source_target_pairs={{0,1},{1,2},{2,3},{3,4},{4,5},{5,6},{6,7},{8,9},{9,10},{10,11},{11... | collective-permute-start | bytes 393224 | tf_op jit(solution)/shard_map/ppermute | solution.py:288
  221.6 10.5 %collective-permute-start.9 = (bf16[32,8,256]{2,1,0:T(8,128)(2,1)S(1)}, bf16[32,8,256]{2,1,0:T(8,128)(2,1)S(1)}, u32[]{:S(2)}, u32[]{:S(2)}) collective-permute-start(bf16[32,8,256]{2,1,0:T(8,128)(2,1)S(1)} %get-tuple-element.5), channel_id=1, source_target_pairs={{1,0},{2,1},{3,2},{4,3},{5,4},{6,5},{7,6},{9,8},{10,9},{11,10},{12... | collective-permute-start | bytes 393224 | tf_op jit(solution)/shard_map/ppermute | solution.py:288

commit v2 on v1

v2 whole, which is shorter than its diff:
```python
import jax
import jax.numpy as jnp
from jax import lax
from jax.experimental import pallas as pl
from jax.experimental.pallas import tpu as pltpu
from jax.sharding import Mesh
from jax.sharding import PartitionSpec as P

ITERS = 10
MEM = ("mem_0", "mem_1", "mem_2")
F32 = jnp.float32
BF16 = jnp.bfloat16
VMEM_LIMIT = 48 << 20


def params():
    return pltpu.CompilerParams(vmem_limit_bytes=VMEM_LIMIT)


def vmem_specs(count):
    return [pl.BlockSpec(memory_space=pltpu.VMEM) for _ in range(count)]


def sides(window):
    width = window.shape[1]
    both = pltpu.roll(window, 1, axis=1) + pltpu.roll(window, width - 1, axis=1)
    return both[:, 128 : width - 128]


def sweep(load, coef_ref, put, first, count, shift, off, width):
    above = load(first - 1)[:, 128 : 128 + width]
    here = load(first)
    for r in range(first, first + count):
        below = load(r + 1)
        mid = here[:, 128 : 128 + width]
        lap = (above + below[:, 128 : 128 + width]) + sides(here) - 4.0 * mid
        put(r, mid + coef_ref[r + shift : r + shift + 1, pl.ds(off, width)] * lap)
        above, here = mid, below


def edges_of(index, width, total):
    off = pl.multiple_of(index * width, width)
    before = pl.multiple_of(jnp.maximum(off - 128, 0), 128)
    after = pl.multiple_of(jnp.minimum(off + width, total - 128), 128)
    return off, before, after


def framed(left, mid, right, index, count):
    left = jnp.where(index > 0, left, 0.0)
    right = jnp.where(index < count - 1, right, 0.0)
    return jnp.concatenate([left, mid, right], axis=1)


CHUNK = 512


def forecast_kernel(x_ref, low_ref, high_ref, field_ref, out_ref, v1_ref, coef_ref):
    rows, _, width = x_ref.shape
    patches = out_ref.shape[0]
    cols = width // patches
    chunks = width // CHUNK
    coef_ref[pl.ds(8, rows), :] = field_ref[...]
    for ref, at in ((low_ref, 7), (high_ref, 8 + rows)):
        parts = ref[2].astype(F32)
        coef_ref[at : at + 1, :] = parts[0:1] + parts[1:2] + parts[2:3]

    def first(c, carry):
        off, before, after = edges_of(c, CHUNK, width)

        def load(r):
            ref, at = x_ref, r
            if r < 0:
                ref, at = low_ref, r + 2
            elif r >= rows:
                ref, at = high_ref, r - rows
            pieces = [ref[at, :, pl.ds(o, s)].astype(F32) for o, s in ((before, 128), (off, CHUNK), (after, 128))]
            return framed(*pieces, c, chunks)

        def put(r, value):
            v1_ref[r + 1, :, pl.ds(off, CHUNK)] = value

        sweep(load, coef_ref, put, -1, rows + 2, 8, off, CHUNK)
        return carry

    def second(c, carry):
        off, before, after = edges_of(c, CHUNK, width)

        def load(r):
            pieces = [v1_ref[r + 1, :, pl.ds(o, s)] for o, s in ((before, 128), (off, CHUNK), (after, 128))]
            return framed(*pieces, c, chunks)

        def put(r, value):
            for k in range(CHUNK // cols):
                out_ref[c * (CHUNK // cols) + k, :, r * cols : (r + 1) * cols] = value[
                    :, k * cols : (k + 1) * cols
                ].astype(BF16)

        sweep(load, coef_ref, put, 0, rows, 8, off, CHUNK)
        return carry

    lax.fori_loop(0, chunks, first, 0)
    lax.fori_loop(0, chunks, second, 0)


def forecast(x, low, high, field, patches):
    rows, members, width = x.shape
    return pl.pallas_call(
        forecast_kernel,
        out_shape=jax.ShapeDtypeStruct((patches, members, rows * width // patches), BF16),
        in_specs=vmem_specs(4),
        out_specs=pl.BlockSpec(memory_space=pltpu.VMEM),
        scratch_shapes=[pltpu.VMEM((rows + 2, members, width), F32), pltpu.VMEM((rows + 16, width), F32)],
        compiler_params=params(),
        name="forecast",
    )(x, low, high, field)


def gram_kernel(block_ref, site_ref, value_ref, weight_ref, out_ref):
    groups, each, cells = block_ref.shape
    members = groups * each
    count = site_ref.shape[1]
    half = members // 2
    step = 512
    site = site_ref[...]
    observed = jnp.zeros((members, count), F32)
    for c in range(cells // step):
        cell = lax.broadcasted_iota(jnp.int32, (step, count), 0) + c * step
        chosen = jnp.where(cell == site, 1.0, 0.0).astype(BF16)
        piece = block_ref[:, :, c * step : (c + 1) * step].reshape(members, step)
        observed += jnp.dot(piece, chosen, preferred_element_type=F32)
    mean = jnp.sum(observed, axis=0, keepdims=True) * (1.0 / members)
    root = jnp.sqrt(weight_ref[...])
    spread = ((observed - mean) * root).astype(BF16)
    innovation = ((value_ref[...] - mean) * root).astype(BF16)
    tail = jnp.broadcast_to(innovation.astype(F32), (16, count)).astype(BF16)
    left = jnp.concatenate([spread, tail], axis=0)
    both = lax.dot_general(left, spread, (((1,), (1,)), ((), ())), preferred_element_type=F32)
    low = both[half:members, half:]
    across = lax.broadcasted_iota(jnp.int32, (half, half), 0)
    along = lax.broadcasted_iota(jnp.int32, (half, half), 1)
    corner = jnp.sum(jnp.where(across == along, low, 0.0), axis=0, keepdims=True)
    out_ref[:half, :half] = jnp.where(across <= along, both[:half, :half], low)
    out_ref[:half, half:] = both[:half, half:]
    out_ref[half:, :] = both[members : members + 8]
    out_ref[half + 1 : half + 2, :half] = corner


def gram_of(blocks, sites, values, weights):
    members = blocks.shape[0] * blocks.shape[1]
    return pl.pallas_call(
        gram_kernel,
        out_shape=jax.ShapeDtypeStruct((members // 2 + 8, members), F32),
        in_specs=vmem_specs(4),
        out_specs=pl.BlockSpec(memory_space=pltpu.VMEM),
        compiler_params=params(),
        name="gram",
    )(blocks, sites, values, weights)


def unpacked(packed, half):
    across = lax.broadcasted_iota(jnp.int32, (half, half), 0)
    along = lax.broadcasted_iota(jnp.int32, (half, half), 1)
    block = packed[:half, :half]
    turned = block.T
    upper = jnp.where(across <= along, block, turned)
    lower = jnp.where(across > along, block, turned)
    lower = jnp.where(across == along, packed[half + 1 : half + 2, :half], lower)
    side = packed[:half, half:]
    return jnp.concatenate(
        [jnp.concatenate([upper, side], axis=1), jnp.concatenate([side.T, lower], axis=1)], axis=0
    )


def halves(value):
    high = value.astype(BF16)
    return high, (value - high.astype(F32)).astype(BF16)


def product(left, right):
    lh, ll = left
    rh, rl = right
    return (
        jnp.dot(lh, rh, preferred_element_type=F32)
        + jnp.dot(lh, rl, preferred_element_type=F32)
        + jnp.dot(ll, rh, preferred_element_type=F32)
    )


def root_kernel(low_ref, mid_ref, high_ref, out_ref):
    members = out_ref.shape[0]
    half = members // 2
    packed = 0.5 * low_ref[...] + mid_ref[...] + 0.5 * high_ref[...]
    vector = packed[half : half + 8]
    gram = unpacked(packed, half)
    across = lax.broadcasted_iota(jnp.int32, (members, members), 0)
    along = lax.broadcasted_iota(jnp.int32, (members, members), 1)
    identity = jnp.where(across == along, 1.0, 0.0)
    system = gram + (members - 1.0) * identity
    squares = jnp.sum(jnp.sum(system * system, axis=0, keepdims=True), axis=1, keepdims=True)
    frob = jnp.sqrt(squares)
    root = system / frob
    factor = 1.5 * identity - 0.5 * root
    inverse = factor
    root = product(halves(root), halves(factor))
    for step in range(1, ITERS):
        root_h = halves(root)
        inverse_h = halves(inverse)
        factor_h = halves(1.5 * identity - 0.5 * product(inverse_h, root_h))
        if step < ITERS - 1:
            root = product(root_h, factor_h)
        inverse = product(factor_h, inverse_h)
    inverse_h = halves(inverse)
    weights = product(halves(product(halves(vector), inverse_h)), inverse_h) / frob
    scale = jnp.sqrt(members - 1.0) * lax.rsqrt(frob)
    out_ref[...] = (scale * inverse + weights[0:1]).astype(BF16)


def root_of(low, mid, high):
    members = mid.shape[1]
    return pl.pallas_call(
        root_kernel,
        out_shape=jax.ShapeDtypeStruct((members, members), BF16),
        in_specs=vmem_specs(3),
        out_specs=pl.BlockSpec(memory_space=pltpu.VMEM),
        compiler_params=params(),
        name="root",
    )(low, mid, high)


def center_kernel(block_ref, mean_ref, out_ref):
    groups, each, cells = block_ref.shape
    members = groups * each
    step = 256

    def one(c, carry):
        where = pl.ds(pl.multiple_of(c * step, step), step)
        cellwise = block_ref[:, :, where].astype(F32)
        mean = jnp.sum(jnp.sum(cellwise, axis=0), axis=0, keepdims=True) * (1.0 / members)
        mean_ref[:, where] = mean
        out_ref[:, where] = (cellwise.reshape(members, step) - mean).astype(BF16)
        return carry

    lax.fori_loop(0, cells // step, one, 0)


def centered(blocks):
    groups, each, cells = blocks.shape
    return pl.pallas_call(
        center_kernel,
        out_shape=(
            jax.ShapeDtypeStruct((1, cells), F32),
            jax.ShapeDtypeStruct((groups * each, cells), BF16),
        ),
        in_specs=vmem_specs(1),
        out_specs=tuple(vmem_specs(2)),
        compiler_params=params(),
        name="center",
    )(blocks)


def update_kernel(turned_ref, mean_ref, deviation_ref, out_ref):
    groups, each, cells = out_ref.shape
    step = 512

    def one(c, carry):
        where = pl.ds(pl.multiple_of(c * step, step), step)
        moved = jnp.dot(turned_ref[...], deviation_ref[:, where], preferred_element_type=F32)
        out_ref[:, :, where] = (mean_ref[:, where] + moved).reshape(groups, each, step).astype(BF16)
        return carry

    lax.fori_loop(0, cells // step, one, 0)


def update(turned, mean, deviation, shape):
    return pl.pallas_call(
        update_kernel,
        out_shape=jax.ShapeDtypeStruct(shape, BF16),
        in_specs=vmem_specs(3),
        out_specs=pl.BlockSpec(memory_space=pltpu.VMEM),
        compiler_params=params(),
        name="update",
    )(turned, mean, deviation)


def finish_kernel(block_ref, low_ref, high_ref, coef_ref, out_ref):
    patches, _, _ = block_ref.shape
    rows, _, width = out_ref.shape
    cols = width // patches
    chunks = width // CHUNK
    each = CHUNK // cols

    def one(c, carry):
        off = pl.multiple_of(c * CHUNK, CHUNK)
        base = c * each
        before = jnp.maximum(base - 1, 0)
        after = jnp.minimum(base + each, patches - 1)

        def load(r):
            ref, at = block_ref, r * cols
            if r < 0:
                ref, at = low_ref, 0
            elif r >= rows:
                ref, at = high_ref, 0
            pieces = [ref[before, :, at + cols - 128 : at + cols]]
            pieces += [ref[base + k, :, at : at + cols] for k in range(each)]
            pieces += [ref[after, :, at : at + 128]]
            pieces = [p.astype(F32) for p in pieces]
            return framed(pieces[0], jnp.concatenate(pieces[1:-1], axis=1), pieces[-1], c, chunks)

        def put(r, value):
            out_ref[r, :, pl.ds(off, CHUNK)] = value.astype(BF16)

        sweep(load, coef_ref, put, 0, rows, 0, off, CHUNK)
        return carry

    lax.fori_loop(0, chunks, one, 0)


def finish(blocks, top, bot, coef):
    _, members, _ = blocks.shape
    rows, width = coef.shape
    return pl.pallas_call(
        finish_kernel,
        out_shape=jax.ShapeDtypeStruct((rows, members, width), BF16),
        in_specs=vmem_specs(4),
        out_specs=pl.BlockSpec(memory_space=pltpu.VMEM),
        compiler_params=params(),
        name="finish",
    )(blocks, top, bot, coef)


def from_both(axis, to_next, to_previous):
    count = lax.axis_size(axis)
    forward = [(i, i + 1) for i in range(count - 1)]
    backward = [(i + 1, i) for i in range(count - 1)]
    return lax.ppermute(to_next, axis, forward), lax.ppermute(to_previous, axis, backward)


def in_three(row):
    high = lax.reduce_precision(row, 8, 7)
    middle = lax.reduce_precision(row - high, 8, 7)
    parts = jnp.concatenate([high, middle, row - high - middle], axis=0).astype(BF16)
    return jnp.pad(parts, ((0, 5), (0, 0)))[None]


def body(
    prior_samples,
    diffusivity_field,
    measured_site_position,
    measured_quantities,
    measurement_weightings,
):
    patches = lax.axis_size(MEM)
    cols = prior_samples.shape[2] // patches
    low, high = from_both(
        "space",
        jnp.concatenate(
            [jnp.swapaxes(prior_samples[:, -2:], 0, 1), in_three(diffusivity_field[-1:])], axis=0
        ),
        jnp.concatenate(
            [jnp.swapaxes(prior_samples[:, :2], 0, 1), in_three(diffusivity_field[:1])], axis=0
        ),
    )
    turned_prior = jnp.swapaxes(prior_samples, 0, 1)
    blocks = forecast(turned_prior, low, high, diffusivity_field, patches)
    gathered = lax.all_to_all(blocks, MEM, 0, 0, tiled=True)
    own = gram_of(
        gathered, measured_site_position[0], measured_quantities[0], measurement_weightings[0]
    )
    low, high = from_both(MEM, own, own)
    mean, deviation = centered(gathered)
    band = 0.5 * low + own + 0.5 * high
    low, high = from_both("space", band, band)
    updated = update(root_of(low, band, high), mean, deviation, gathered.shape)
    returned = lax.all_to_all(updated, MEM, 0, 0, tiled=True)
    low, high = from_both("space", returned[:, :, -cols:], returned[:, :, :cols])
    done = finish(returned, low, high, diffusivity_field)
    return jnp.swapaxes(done, 0, 1)


def solution(mesh):
    finer = Mesh(
        mesh.devices.reshape(2, 8, 2, mesh.shape["space"]), ("mem_0", "mem_1", "mem_2", "space")
    )
    in_specs = (
        P(MEM, "space", None),
        P("space", None),
        P("space", MEM, None),
        P("space", MEM, None),
        P("space", MEM, None),
    )
    out_specs = P(MEM, "space", None)
    return jax.shard_map(body, mesh=finer, in_specs=in_specs, out_specs=out_specs, check_vma=False)
```

time: 240 us -> 202 us (0.84); the launches traced: 239 us -> 198 us
  waiting for transfers between devices: 69.8 us -> 22.2 us
  blocking collectives: 75.2 us -> 117 us
  starting transfers between devices: 51.4 us -> 30.8 us
  Pallas kernels: 34.2 us -> 21.1 us
  local copies, waits for them, and re-layouts: 7.83 us -> 5.31 us
    all_to_all x1, blocking collectives: 16.2 us -> 60.1 us  [body(): gathered = lax.all_to_all(blocks, MEM, 0, 0, tiled=True)]
    ppermute x10 -> x8, waiting for transfers between devices: 62 us -> 22.2 us  [the longest x4 13 us: from_both(): lax.ppermute(to_next, axis, forward)]
    all_to_all x2 -> x0, starting transfers between devices: 13.8 us -> none  [the longest x1 8.75 us: body(): lax.all_to_all(jnp.broadcast_to(measured_site_position[0], (patches, meas...]
    all_to_all x2 -> x0, waiting for transfers between devices: 7.76 us -> none  [the longest x1 7.75 us: body(): lax.all_to_all(jnp.broadcast_to(measured_site_position[0], (patches, meas...]
    ppermute x10 -> x8, starting transfers between devices: 37.6 us -> 30.8 us  [the longest x4 23.1 us: from_both(): lax.ppermute(to_next, axis, forward)]
    pallas_call x3, Pallas kernels: 10.8 us -> 4.49 us  [the longest x1 1.87 us: update(): pl.pallas_call(update_kernel, out_shape=jax.ShapeDtypeStruct(shape, BF16)...]
    pallas_call x1, Pallas kernels: 12.4 us -> 6.97 us  [forecast(): pl.pallas_call(forecast_kernel, out_shape=jax.ShapeDtypeStruct((patches,...]
  transfers between devices with their start and end apart: 12 -> 8, of which waited for: 6 -> 8; matrix products, arithmetic and copies ran while one was open for 2% -> 0% of each run, Pallas kernels for 3% -> 1%
where the time goes in v2:
time: 202 us; the launch traced here: 198 us
  blocking collectives  117 us (58%)
  starting transfers between devices  30.8 us (15%)
  waiting for transfers between devices  22.2 us (11%)
  Pallas kernels  21.1 us (10%)
  local copies, waits for them, and re-layouts  5.31 us (3%)
    all_to_all x1, blocking collectives, body(): gathered = lax.all_to_all(blocks, MEM, 0, 0, tiled=True)  60.1 us
    all_to_all x1, blocking collectives, body(): returned = lax.all_to_all(updated, MEM, 0, 0, tiled=True)  57.2 us
    ppermute x4, starting transfers between devices, from_both(): lax.ppermute(to_next, axis, forward)  23.1 us
    ppermute x4, waiting for transfers between devices, from_both(): lax.ppermute(to_next, axis, forward)  13 us
    ppermute x4, waiting for transfers between devices, from_both(): lax.ppermute(to_previous, axis, backward)  9.15 us
    ppermute x4, starting transfers between devices, from_both(): lax.ppermute(to_previous, axis, backward)  7.68 us
    pallas_call x1, Pallas kernels, forecast(): pl.pallas_call(forecast_kernel, out_shape=jax.ShapeDtypeStruct((patches,...  6.97 us
    pallas_call x1, Pallas kernels, root_of(): pl.pallas_call(root_kernel, out_shape=jax.ShapeDtypeStruct((members, memb...  6.81 us
  transfers between devices with their start and end apart: 8, of which 8 were waited for; matrix products, arithmetic and copies ran while one was open for 0% of the time, Pallas kernels for 1%

profile of v2, /device:TPU:56, one launch (start us, length us, event | category | flops | bytes accessed | tf_op | source)
XLA Modules:
  0.0 198.4 jit_solution(5655115719097529942)
XLA Ops:
  0.0 1.2 reduce-precision_convert_fusion.1
  1.2 2.8 %copy.12 = bf16[8,16,8192]{2,0,1:T(8,128)(2,1)S(1)} copy(bf16[8,16,8192]{2,1,0:T(8,128)(2,1)} %param.5) | data formatting | bytes 4194304 | tf_op args[0]
  4.2 4.6 %collective-permute-start = (bf16[3,8,8192]{2,1,0:T(8,128)(2,1)S(1)}, bf16[3,8,8192]{2,1,0:T(8,128)(2,1)S(1)}, u32[]{:S(2)}, u32[]{:S(2)}) collective-permute-start(bf16[3,8,8192]{2,1,0:T(8,128)(2,1)S(1)} %pad_maximum_fusion), channel_id=1, source_target_pairs={{0,1},{1,2},{2,3},{3,4},{4,5},{5,6},{6,7},{8,9},{9,10},{10,11},{11... | collective-permute-start | bytes 1179656 | tf_op jit(solution)/shard_map/ppermute | solution.py:336
  9.0 1.9 collective-permute-start.1
  10.9 6.2 %collective-permute-done.low_ref = bf16[3,8,8192]{2,1,0:T(8,128)(2,1)S(1)} collective-permute-done((bf16[3,8,8192]{2,1,0:T(8,128)(2,1)S(1)}, bf16[3,8,8192]{2,1,0:T(8,128)(2,1)S(1)}, u32[]{:S(2)}, u32[]{:S(2)}) %collective-permute-start) | collective-permute-done | bytes 393248 | tf_op jit(solution)/shard_map/ppermute | solution.py:336
  17.1 7.9 %collective-permute-done.1.high_ref = bf16[3,8,8192]{2,1,0:T(8,128)(2,1)S(1)} collective-permute-done((bf16[3,8,8192]{2,1,0:T(8,128)(2,1)S(1)}, bf16[3,8,8192]{2,1,0:T(8,128)(2,1)S(1)}, u32[]{:S(2)}, u32[]{:S(2)}) %collective-permute-start.1) | collective-permute-done | bytes 393248 | tf_op jit(solution)/shard_map/ppermute | solution.py:336
  25.0 7.0 %forecast.1 = bf16[32,8,4096]{2,1,0:T(8,128)(2,1)S(1)} custom-call(bf16[16,8,8192]{2,1,0:T(8,128)(2,1)S(1)} %bitcast.14, bf16[3,8,8192]{2,1,0:T(8,128)(2,1)S(1)} %collective-permute-done.low_ref, bf16[3,8,8192]{2,1,0:T(8,128)(2,1)S(1)} %collective-permute-done.1.high_ref, f32[16,8192]{1,0:T(8,128)S(1)} %copy-done), custom_call_target="tpu_custom_call" | custom-call | tf_op jit(solution)/shard_map/forecast/pallas_call | solution.py:107
  32.1 60.1 %all_to_all.10.block_ref = bf16[32,8,4096]{2,1,0:T(8,128)(2,1)S(1)} all-to-all(bf16[32,8,4096]{2,1,0:T(8,128)(2,1)S(1)} %forecast.1), channel_id=1, replica_groups=mesh['mem_0'=2,'mem_1'=8,'mem_2'=2,'space'=8] {'mem_0','mem_1','mem_2'}, dimensions={0} | all-to-all | bytes 4194304 | tf_op jit(solution)/shard_map/all_to_all | solution.py:366
  92.2 1.6 gram.1
  93.8 1.9 collective-permute-start.3
  95.7 2.4 %collective-permute-start.2 = (f32[136,256]{1,0:T(8,128)S(1)}, f32[136,256]{1,0:T(8,128)S(1)}, u32[]{:S(2)}, u32[]{:S(2)}) collective-permute-start(f32[136,256]{1,0:T(8,128)S(1)} %gram.1), channel_id=1, source_target_pairs={{0,8},{8,16},{16,24},{24,32},{32,40},{40,48},{48,56},{56,64},{64,7... | collective-permute-start | bytes 417800 | tf_op jit(solution)/shard_map/ppermute | solution.py:336
  98.3 3.8 %collective-permute-done.2 = f32[136,256]{1,0:T(8,128)S(1)} collective-permute-done((f32[136,256]{1,0:T(8,128)S(1)}, f32[136,256]{1,0:T(8,128)S(1)}, u32[]{:S(2)}, u32[]{:S(2)}) %collective-permute-start.2) | collective-permute-done | bytes 139296 | tf_op jit(solution)/shard_map/ppermute | solution.py:336
  102.1 1.9 collective-permute-start.5
  104.1 7.5 %collective-permute-start.4 = (f32[136,256]{1,0:T(8,128)S(1)}, f32[136,256]{1,0:T(8,128)S(1)}, u32[]{:S(2)}, u32[]{:S(2)}) collective-permute-start(f32[136,256]{1,0:T(8,128)S(1)} %multiply_add_fusion.mid_ref), channel_id=1, source_target_pairs={{0,1},{1,2},{2,3},{3,4},{4,5},{5,6},{6,7},{8,9},{9,10},{10,11},{11... | collective-permute-start | bytes 417800 | tf_op jit(solution)/shard_map/ppermute | solution.py:336
  111.6 1.0 center.1
  112.7 1.5 collective-permute-done.4.low_ref
  114.2 6.8 %root.1.turned_ref = bf16[256,256]{1,0:T(8,128)(2,1)S(1)} custom-call(f32[136,256]{1,0:T(8,128)S(1)} %collective-permute-done.4.low_ref, f32[136,256]{1,0:T(8,128)S(1)} %multiply_add_fusion.mid_ref, f32[136,256]{1,0:T(8,128)S(1)} %collective-permute-done.5.high_ref), custom_call_target="tpu_custom_call" | custom-call | tf_op jit(solution)/shard_map/root/pallas_call | solution.py:220
  121.0 1.9 update.1
  122.9 57.2 %all_to_all.11.block_ref = bf16[32,8,4096]{2,1,0:T(8,128)(2,1)S(1)} all-to-all(bf16[32,8,4096]{2,1,0:T(8,128)(2,1)S(1)} %update.1), channel_id=1, replica_groups=mesh['mem_0'=2,'mem_1'=8,'mem_2'=2,'space'=8] {'mem_0','mem_1','mem_2'}, dimensions={0} | all-to-all | bytes 4194304 | tf_op jit(solution)/shard_map/all_to_all | solution.py:375
  180.1 1.9 collective-permute-start.7
  182.0 8.6 %collective-permute-start.6 = (bf16[32,8,256]{2,1,0:T(8,128)(2,1)S(1)}, bf16[32,8,256]{2,1,0:T(8,128)(2,1)S(1)}, u32[]{:S(2)}, u32[]{:S(2)}) collective-permute-start(bf16[32,8,256]{2,1,0:T(8,128)(2,1)S(1)} %get-tuple-element.10), channel_id=1, source_target_pairs={{0,1},{1,2},{2,3},{3,4},{4,5},{5,6},{6,7},{8,9},{9,10},{10,11},{11... | collective-permute-start | bytes 393224 | tf_op jit(solution)/shard_map/ppermute | solution.py:336
  191.6 1.5 collective-permute-done.6.low_ref
  193.1 2.8 %finish.1 = bf16[16,8,8192]{2,1,0:T(8,128)(2,1)S(1)} custom-call(bf16[32,8,4096]{2,1,0:T(8,128)(2,1)S(1)} %all_to_all.11.block_ref, bf16[32,8,256]{2,1,0:T(8,128)(2,1)S(1)} %collective-permute-done.6.low_ref, bf16[32,8,256]{2,1,0:T(8,128)(2,1)S(1)} %collective-permute-done.7.high_ref, f32[16,8192]{1,0:T(8,128)S(1)} %copy-done), custom_call_target="tpu_custom_call" | custom-call | tf_op jit(solution)/shard_map/finish/pallas_call | solution.py:322
  195.9 2.5 %copy.9 = bf16[8,16,8192]{2,1,0:T(8,128)(2,1)} copy(bf16[8,16,8192]{2,0,1:T(8,128)(2,1)S(1)} %bitcast.15) | data formatting | bytes 4194304 | tf_op jit(solution)/shard_map/transpose | solution.py:378
  (18 shorter events, 1.7 us)
Async XLA Ops:
  3.9 21.1 %copy-start = (f32[16,8192]{1,0:T(8,128)S(1)}, f32[16,8192]{1,0:T(8,128)}, u32[]{:S(2)}) copy-start(f32[16,8192]{1,0:T(8,128)} %coef_ref.1) | copy-start | bytes 1572868
  4.2 12.9 %collective-permute-start = (bf16[3,8,8192]{2,1,0:T(8,128)(2,1)S(1)}, bf16[3,8,8192]{2,1,0:T(8,128)(2,1)S(1)}, u32[]{:S(2)}, u32[]{:S(2)}) collective-permute-start(bf16[3,8,8192]{2,1,0:T(8,128)(2,1)S(1)} %pad_maximum_fusion), channel_id=1, source_target_pairs={{0,1},{1,2},{2,3},{3,4},{4,5},{5,6},{6,7},{8,9},{9,10},{10,11},{11... | collective-permute-start | bytes 1179656 | tf_op jit(solution)/shard_map/ppermute | solution.py:336
  9.0 16.1 %collective-permute-start.1 = (bf16[3,8,8192]{2,1,0:T(8,128)(2,1)S(1)}, bf16[3,8,8192]{2,1,0:T(8,128)(2,1)S(1)}, u32[]{:S(2)}, u32[]{:S(2)}) collective-permute-start(bf16[3,8,8192]{2,1,0:T(8,128)(2,1)S(1)} %pad_maximum_fusion.1), channel_id=1, source_target_pairs={{1,0},{2,1},{3,2},{4,3},{5,4},{6,5},{7,6},{9,8},{10,9},{11,10},{12... | collective-permute-start | bytes 1179656 | tf_op jit(solution)/shard_map/ppermute | solution.py:336
  32.0 60.2 %copy-start.1 = (s32[1,1,512]{2,1,0:T(1,128)S(1)}, s32[1,1,512]{2,1,0:T(1,128)}, u32[]{:S(2)}) copy-start(s32[1,1,512]{2,1,0:T(1,128)} %param.7) | copy-start | bytes 6148
  32.0 60.2 %copy-start.2 = (f32[1,1,512]{2,1,0:T(1,128)S(1)}, f32[1,1,512]{2,1,0:T(1,128)}, u32[]{:S(2)}) copy-start(f32[1,1,512]{2,1,0:T(1,128)} %param.8) | copy-start | bytes 6148
  32.1 60.1 %copy-start.3 = (f32[1,1,512]{2,1,0:T(1,128)S(1)}, f32[1,1,512]{2,1,0:T(1,128)}, u32[]{:S(2)}) copy-start(f32[1,1,512]{2,1,0:T(1,128)} %param.9) | copy-start | bytes 6148
  93.8 4.5 %collective-permute-start.3 = (f32[136,256]{1,0:T(8,128)S(1)}, f32[136,256]{1,0:T(8,128)S(1)}, u32[]{:S(2)}, u32[]{:S(2)}) collective-permute-start(f32[136,256]{1,0:T(8,128)S(1)} %gram.1), channel_id=1, source_target_pairs={{8,0},{16,8},{24,16},{32,24},{40,32},{48,40},{56,48},{64,56},{72,6... | collective-permute-start | bytes 417800 | tf_op jit(solution)/shard_map/ppermute | solution.py:336
  95.7 6.4 %collective-permute-start.2 = (f32[136,256]{1,0:T(8,128)S(1)}, f32[136,256]{1,0:T(8,128)S(1)}, u32[]{:S(2)}, u32[]{:S(2)}) collective-permute-start(f32[136,256]{1,0:T(8,128)S(1)} %gram.1), channel_id=1, source_target_pairs={{0,8},{8,16},{16,24},{24,32},{32,40},{40,48},{48,56},{56,64},{64,7... | collective-permute-start | bytes 417800 | tf_op jit(solution)/shard_map/ppermute | solution.py:336
  102.1 10.6 %collective-permute-start.5 = (f32[136,256]{1,0:T(8,128)S(1)}, f32[136,256]{1,0:T(8,128)S(1)}, u32[]{:S(2)}, u32[]{:S(2)}) collective-permute-start(f32[136,256]{1,0:T(8,128)S(1)} %multiply_add_fusion.mid_ref), channel_id=1, source_target_pairs={{1,0},{2,1},{3,2},{4,3},{5,4},{6,5},{7,6},{9,8},{10,9},{11,10},{12... | collective-permute-start | bytes 417800 | tf_op jit(solution)/shard_map/ppermute | solution.py:336
  104.1 10.1 %collective-permute-start.4 = (f32[136,256]{1,0:T(8,128)S(1)}, f32[136,256]{1,0:T(8,128)S(1)}, u32[]{:S(2)}, u32[]{:S(2)}) collective-permute-start(f32[136,256]{1,0:T(8,128)S(1)} %multiply_add_fusion.mid_ref), channel_id=1, source_target_pairs={{0,1},{1,2},{2,3},{3,4},{4,5},{5,6},{6,7},{8,9},{9,10},{10,11},{11... | collective-permute-start | bytes 417800 | tf_op jit(solution)/shard_map/ppermute | solution.py:336
  180.1 11.5 %collective-permute-start.7 = (bf16[32,8,256]{2,1,0:T(8,128)(2,1)S(1)}, bf16[32,8,256]{2,1,0:T(8,128)(2,1)S(1)}, u32[]{:S(2)}, u32[]{:S(2)}) collective-permute-start(bf16[32,8,256]{2,1,0:T(8,128)(2,1)S(1)} %get-tuple-element.9), channel_id=1, source_target_pairs={{1,0},{2,1},{3,2},{4,3},{5,4},{6,5},{7,6},{9,8},{10,9},{11,10},{12... | collective-permute-start | bytes 393224 | tf_op jit(solution)/shard_map/ppermute | solution.py:336
  182.0 11.1 %collective-permute-start.6 = (bf16[32,8,256]{2,1,0:T(8,128)(2,1)S(1)}, bf16[32,8,256]{2,1,0:T(8,128)(2,1)S(1)}, u32[]{:S(2)}, u32[]{:S(2)}) collective-permute-start(bf16[32,8,256]{2,1,0:T(8,128)(2,1)S(1)} %get-tuple-element.10), channel_id=1, source_target_pairs={{0,1},{1,2},{2,3},{3,4},{4,5},{5,6},{6,7},{8,9},{9,10},{10,11},{11... | collective-permute-start | bytes 393224 | tf_op jit(solution)/shard_map/ppermute | solution.py:336

commit v3 on v2

--- a/solution.py
+++ b/solution.py
@@ -54,65 +54,164 @@
 CHUNK = 512
 
 
-def forecast_kernel(x_ref, low_ref, high_ref, field_ref, out_ref, v1_ref, coef_ref):
-    rows, _, width = x_ref.shape
-    patches = out_ref.shape[0]
-    cols = width // patches
-    chunks = width // CHUNK
-    coef_ref[pl.ds(8, rows), :] = field_ref[...]
-    for ref, at in ((low_ref, 7), (high_ref, 8 + rows)):
-        parts = ref[2].astype(F32)
-        coef_ref[at : at + 1, :] = parts[0:1] + parts[1:2] + parts[2:3]
-
-    def first(c, carry):
-        off, before, after = edges_of(c, CHUNK, width)
-
-        def load(r):
-            ref, at = x_ref, r
-            if r < 0:
-                ref, at = low_ref, r + 2
-            elif r >= rows:
-                ref, at = high_ref, r - rows
-            pieces = [ref[at, :, pl.ds(o, s)].astype(F32) for o, s in ((before, 128), (off, CHUNK), (after, 128))]
-            return framed(*pieces, c, chunks)
+def ends_kernel(odd_ref, x_ref, field_ref, one_ref, two_ref):
+    members, rows, width = x_ref.shape
+    odd = odd_ref[0] > 0
+
+    def put(where, low, high):
+        one_ref[:, where] = jnp.where(odd, low, high).astype(BF16)
+        two_ref[:, where] = jnp.where(odd, high, low).astype(BF16)
+
+    def some(c, carry):
+        off = pl.multiple_of(c * CHUNK, CHUNK)
+        tall = [x_ref[m, :, pl.ds(off, CHUNK)].astype(F32) for m in range(members)]
+        for k in range(2):
+            low = jnp.concatenate([t[k : k + 1] for t in tall], axis=0)
+            high = jnp.concatenate([t[rows - 2 + k : rows - 1 + k] for t in tall], axis=0)
+            put(pl.ds(pl.multiple_of(k * width + off, CHUNK), CHUNK), low, high)
+        return carry
+
+    lax.fori_loop(0, width // CHUNK, some, 0)
+    piece = width // members
+
+    def folded(row):
+        lines = [field_ref[row : row + 1, s * piece : (s + 1) * piece] for s in range(members)]
+        whole = jnp.concatenate(lines, axis=0)
+        high, rest = halves(whole)
+        low = whole - high.astype(F32) - rest.astype(F32)
+        return [high.astype(F32), rest.astype(F32), low]
+
+    for k, (low, high) in enumerate(zip(folded(0), folded(rows - 1))):
+        begin = 2 * width + k * piece
+        put(slice(begin, begin + piece), low, high)
+
+
+def ends(odd, x, field):
+    members, _, width = x.shape
+    shape = jax.ShapeDtypeStruct((members, 2 * width + 3 * width // members), BF16)
+    return pl.pallas_call(
+        ends_kernel,
+        out_shape=(shape, shape),
+        in_specs=[pl.BlockSpec(memory_space=pltpu.SMEM)] + vmem_specs(2),
+        out_specs=tuple(vmem_specs(2)),
+        compiler_params=params(),
+        name="ends",
+    )(odd, x, field)
+
+
+def first_pass(source, coef_ref, v1_ref, index, width, spans, shift):
+    off, before, after = edges_of(index, CHUNK, width)
+
+    def load(r):
+        pieces = [source(r, o, s) for o, s in ((before, 128), (off, CHUNK), (after, 128))]
+        return framed(*pieces, index, width // CHUNK)
+
+    for begin, count in spans:
 
         def put(r, value):
             v1_ref[r + 1, :, pl.ds(off, CHUNK)] = value
 
-        sweep(load, coef_ref, put, -1, rows + 2, 8, off, CHUNK)
+        sweep(load, coef_ref, put, begin, count, shift, off, CHUNK)
+
+
+def second_pass(coef_ref, v1_ref, out_ref, index, width, spans, shift):
+    cols = width // out_ref.shape[0]
+    each = CHUNK // cols
+    off, before, after = edges_of(index, CHUNK, width)
+
+    def load(r):
+        pieces = [v1_ref[r + 1, :, pl.ds(o, s)] for o, s in ((before, 128), (off, CHUNK), (after, 128))]
+        return framed(*pieces, index, width // CHUNK)
+
+    def put(r, value):
+        for k in range(each):
+            out_ref[index * each + k, :, r * cols : (r + 1) * cols] = value[
+                :, k * cols : (k + 1) * cols
+            ].astype(BF16)
+
+    for begin, count in spans:
+        sweep(load, coef_ref, put, begin, count, shift, off, CHUNK)
+
+
+def inner_kernel(x_ref, field_ref, out_ref, v1_ref):
+    rows, _, width = x_ref.shape
+
+    def first(c, carry):
+        def source(r, off, size):
+            return x_ref[r, :, pl.ds(off, size)].astype(F32)
+
+        first_pass(source, field_ref, v1_ref, c, width, ((1, rows - 2),), 0)
         return carry
 
     def second(c, carry):
-        off, before, after = edges_of(c, CHUNK, width)
-
-        def load(r):
-            pieces = [v1_ref[r + 1, :, pl.ds(o, s)] for o, s in ((before, 128), (off, CHUNK), (after, 128))]
-            return framed(*pieces, c, chunks)
-
-        def put(r, value):
-            for k in range(CHUNK // cols):
-                out_ref[c * (CHUNK // cols) + k, :, r * cols : (r + 1) * cols] = value[
-                    :, k * cols : (k + 1) * cols
-                ].astype(BF16)
-
-        sweep(load, coef_ref, put, 0, rows, 8, off, CHUNK)
-        return carry
-
-    lax.fori_loop(0, chunks, first, 0)
-    lax.fori_loop(0, chunks, second, 0)
-
-
-def forecast(x, low, high, field, patches):
+        second_pass(field_ref, v1_ref, out_ref, c, width, ((2, rows - 4),), 0)
+        return carry
+
+    lax.fori_loop(0, width // CHUNK, first, 0)
+    lax.fori_loop(0, width // CHUNK, second, 0)
+
+
+def inner_forecast(x, field, patches):
     rows, members, width = x.shape
     return pl.pallas_call(
-        forecast_kernel,
+        inner_kernel,
         out_shape=jax.ShapeDtypeStruct((patches, members, rows * width // patches), BF16),
-        in_specs=vmem_specs(4),
+        in_specs=vmem_specs(2),
+        out_specs=pl.BlockSpec(memory_space=pltpu.VMEM),
+        scratch_shapes=[pltpu.VMEM((rows + 2, members, width), F32)],
+        compiler_params=params(),
+        name="inner",
+    )(x, field)
+
+
+def outer_kernel(odd_ref, x_ref, one_ref, two_ref, field_ref, part_ref, out_ref, v1_ref, coef_ref):
+    rows, members, width = x_ref.shape
+    del part_ref
+    odd = odd_ref[0] > 0
+    piece = width // members
+    coef_ref[pl.ds(8, rows), :] = field_ref[...]
+    one = one_ref[:, 2 * width :].astype(F32)
+    two = two_ref[:, 2 * width :].astype(F32)
+    one = one[:, :piece] + one[:, piece : 2 * piece] + one[:, 2 * piece :]
+    two = two[:, :piece] + two[:, piece : 2 * piece] + two[:, 2 * piece :]
+    low = jnp.where(odd, one, two)
+    high = jnp.where(odd, two, one)
+    for s in range(members):
+        coef_ref[7:8, s * piece : (s + 1) * piece] = low[s : s + 1]
+        coef_ref[8 + rows : 9 + rows, s * piece : (s + 1) * piece] = high[s : s + 1]
+
+    def first(c, carry):
+        def source(r, off, size):
+            if 0 <= r < rows:
+                return x_ref[r, :, pl.ds(off, size)].astype(F32)
+            at = (r + 2 if r < 0 else r - rows) * width
+            a = one_ref[:, pl.ds(at + off, size)].astype(F32)
+            b = two_ref[:, pl.ds(at + off, size)].astype(F32)
+            return jnp.where(odd, a, b) if r < 0 else jnp.where(odd, b, a)
+
+        first_pass(source, coef_ref, v1_ref, c, width, ((-1, 4), (rows - 3, 4)), 8)
+        return carry
+
+    def second(c, carry):
+        second_pass(coef_ref, v1_ref, out_ref, c, width, ((0, 2), (rows - 2, 2)), 8)
+        return carry
+
+    lax.fori_loop(0, width // CHUNK, first, 0)
+    lax.fori_loop(0, width // CHUNK, second, 0)
+
+
+def outer_forecast(odd, x, one, two, field, part):
+    rows, members, width = x.shape
+    return pl.pallas_call(
+        outer_kernel,
+        out_shape=jax.ShapeDtypeStruct(part.shape, BF16),
+        in_specs=[pl.BlockSpec(memory_space=pltpu.SMEM)] + vmem_specs(5),
         out_specs=pl.BlockSpec(memory_space=pltpu.VMEM),
         scratch_shapes=[pltpu.VMEM((rows + 2, members, width), F32), pltpu.VMEM((rows + 16, width), F32)],
-        compiler_params=params(),
-        name="forecast",
-    )(x, low, high, field)
+        input_output_aliases={5: 0},
+        compiler_params=params(),
+        name="outer",
+    )(odd, x, one, two, field, part)
 
 
 def gram_kernel(block_ref, site_ref, value_ref, weight_ref, out_ref):
@@ -186,10 +285,10 @@
     )
 
 
-def root_kernel(low_ref, mid_ref, high_ref, out_ref):
+def root_kernel(one_ref, mid_ref, two_ref, out_ref):
     members = out_ref.shape[0]
     half = members // 2
-    packed = 0.5 * low_ref[...] + mid_ref[...] + 0.5 * high_ref[...]
+    packed = mid_ref[...] + 0.5 * (one_ref[...] + two_ref[...])
     vector = packed[half : half + 8]
     gram = unpacked(packed, half)
     across = lax.broadcasted_iota(jnp.int32, (members, members), 0)
@@ -215,7 +314,7 @@
     out_ref[...] = (scale * inverse + weights[0:1]).astype(BF16)
 
 
-def root_of(low, mid, high):
+def root_of(one, mid, two):
     members = mid.shape[1]
     return pl.pallas_call(
         root_kernel,
@@ -224,7 +323,7 @@
         out_specs=pl.BlockSpec(memory_space=pltpu.VMEM),
         compiler_params=params(),
         name="root",
-    )(low, mid, high)
+    )(one, mid, two)
 
 
 def center_kernel(block_ref, mean_ref, out_ref):
@@ -282,65 +381,96 @@
     )(turned, mean, deviation)
 
 
-def finish_kernel(block_ref, low_ref, high_ref, coef_ref, out_ref):
-    patches, _, _ = block_ref.shape
-    rows, _, width = out_ref.shape
-    cols = width // patches
-    chunks = width // CHUNK
+def final_rows(source, coef_ref, out_ref, index, cols, patches, spans):
     each = CHUNK // cols
+    base = index * each
+    off = pl.multiple_of(index * CHUNK, CHUNK)
+    before = jnp.maximum(base - 1, 0)
+    after = jnp.minimum(base + each, patches - 1)
+
+    def load(r):
+        left = source(r, before, cols - 128, cols)
+        mid = jnp.concatenate([source(r, base + k, 0, cols) for k in range(each)], axis=1)
+        return framed(left, mid, source(r, after, 0, 128), index, patches // each)
+
+    def put(r, value):
+        out_ref[r, :, pl.ds(off, CHUNK)] = value.astype(BF16)
+
+    for begin, count in spans:
+        sweep(load, coef_ref, put, begin, count, 0, off, CHUNK)
+
+
+def middle_kernel(block_ref, coef_ref, out_ref):
+    patches, _, cells = block_ref.shape
+    rows = coef_ref.shape[0]
+    cols = cells // rows
 
     def one(c, carry):
-        off = pl.multiple_of(c * CHUNK, CHUNK)
-        base = c * each
-        before = jnp.maximum(base - 1, 0)
-        after = jnp.minimum(base + each, patches - 1)
-
-        def load(r):
-            ref, at = block_ref, r * cols
-            if r < 0:
-                ref, at = low_ref, 0
-            elif r >= rows:
-                ref, at = high_ref, 0
-            pieces = [ref[before, :, at + cols - 128 : at + cols]]
-            pieces += [ref[base + k, :, at : at + cols] for k in range(each)]
-            pieces += [ref[after, :, at : at + 128]]
-            pieces = [p.astype(F32) for p in pieces]
-            return framed(pieces[0], jnp.concatenate(pieces[1:-1], axis=1), pieces[-1], c, chunks)
-
-        def put(r, value):
-            out_ref[r, :, pl.ds(off, CHUNK)] = value.astype(BF16)
-
-        sweep(load, coef_ref, put, 0, rows, 0, off, CHUNK)
-        return carry
-
-    lax.fori_loop(0, chunks, one, 0)
-
-
-def finish(blocks, top, bot, coef):
+        def source(r, q, begin, end):
+            return block_ref[q, :, r * cols + begin : r * cols + end].astype(F32)
+
+        final_rows(source, coef_ref, out_ref, c, cols, patches, ((1, rows - 2),))
+        return carry
+
+    lax.fori_loop(0, patches * cols // CHUNK, one, 0)
+
+
+def middle_rows(blocks, coef):
     _, members, _ = blocks.shape
     rows, width = coef.shape
     return pl.pallas_call(
-        finish_kernel,
+        middle_kernel,
         out_shape=jax.ShapeDtypeStruct((rows, members, width), BF16),
-        in_specs=vmem_specs(4),
-        out_specs=pl.BlockSpec(memory_space=pltpu.VMEM),
-        compiler_params=params(),
-        name="finish",
-    )(blocks, top, bot, coef)
-
-
-def from_both(axis, to_next, to_previous):
+        in_specs=vmem_specs(2),
+        out_specs=pl.BlockSpec(memory_space=pltpu.VMEM),
+        compiler_params=params(),
+        name="middle",
+    )(blocks, coef)
+
+
+def rim_kernel(odd_ref, block_ref, one_ref, two_ref, coef_ref, part_ref, out_ref):
+    patches, _, cells = block_ref.shape
+    rows = coef_ref.shape[0]
+    cols = cells // rows
+    odd = odd_ref[0] > 0
+    del part_ref
+
+    def one(c, carry):
+        def source(r, q, begin, end):
+            if 0 <= r < rows:
+                return block_ref[q, :, r * cols + begin : r * cols + end].astype(F32)
+            a = one_ref[q, :, begin:end].astype(F32)
+            b = two_ref[q, :, begin:end].astype(F32)
+            return jnp.where(odd, a, b) if r < 0 else jnp.where(odd, b, a)
+
+        final_rows(source, coef_ref, out_ref, c, cols, patches, ((0, 1), (rows - 1, 1)))
+        return carry
+
+    lax.fori_loop(0, patches * cols // CHUNK, one, 0)
+
+
+def rim_rows(odd, blocks, one, two, coef, part):
+    return pl.pallas_call(
+        rim_kernel,
+        out_shape=jax.ShapeDtypeStruct(part.shape, BF16),
+        in_specs=[pl.BlockSpec(memory_space=pltpu.SMEM)] + vmem_specs(5),
+        out_specs=pl.BlockSpec(memory_space=pltpu.VMEM),
+        input_output_aliases={5: 0},
+        compiler_params=params(),
+        name="rim",
+    )(odd, blocks, one, two, coef, part)
+
+
+def swaps(axis, in_one, in_two):
     count = lax.axis_size(axis)
-    forward = [(i, i + 1) for i in range(count - 1)]
-    backward = [(i + 1, i) for i in range(count - 1)]
-    return lax.ppermute(to_next, axis, forward), lax.ppermute(to_previous, axis, backward)
-
-
-def in_three(row):
-    high = lax.reduce_precision(row, 8, 7)
-    middle = lax.reduce_precision(row - high, 8, 7)
-    parts = jnp.concatenate([high, middle, row - high - middle], axis=0).astype(BF16)
-    return jnp.pad(parts, ((0, 5), (0, 0)))[None]
+
+    def pairs(first):
+        both = [(i, i + 1) for i in range(first, count - 1, 2)]
+        return both + [(j, i) for i, j in both]
+
+    two = lax.ppermute(in_two, axis, pairs(1))
+    one = lax.ppermute(in_one, axis, pairs(0))
+    return one, two
 
 
 def body(
@@ -351,30 +481,28 @@
     measurement_weightings,
 ):
     patches = lax.axis_size(MEM)
-    cols = prior_samples.shape[2] // patches
-    low, high = from_both(
-        "space",
-        jnp.concatenate(
-            [jnp.swapaxes(prior_samples[:, -2:], 0, 1), in_three(diffusivity_field[-1:])], axis=0
-        ),
-        jnp.concatenate(
-            [jnp.swapaxes(prior_samples[:, :2], 0, 1), in_three(diffusivity_field[:1])], axis=0
-        ),
-    )
+    _, _, width = prior_samples.shape
+    cols = width // patches
+    odd = lax.bitwise_and(lax.axis_index("space"), 1)
+    flag = odd.reshape(1)
+    one, two = swaps("space", *ends(flag, prior_samples, diffusivity_field))
     turned_prior = jnp.swapaxes(prior_samples, 0, 1)
-    blocks = forecast(turned_prior, low, high, diffusivity_field, patches)
+    part = inner_forecast(turned_prior, diffusivity_field, patches)
+    blocks = outer_forecast(flag, turned_prior, one, two, diffusivity_field, part)
     gathered = lax.all_to_all(blocks, MEM, 0, 0, tiled=True)
     own = gram_of(
         gathered, measured_site_position[0], measured_quantities[0], measurement_weightings[0]
     )
-    low, high = from_both(MEM, own, own)
+    one, two = swaps(MEM, own, own)
     mean, deviation = centered(gathered)
-    band = 0.5 * low + own + 0.5 * high
-    low, high = from_both("space", band, band)
-    updated = update(root_of(low, band, high), mean, deviation, gathered.shape)
+    band = own + 0.5 * (one + two)
+    one, two = swaps("space", band, band)
+    updated = update(root_of(one, band, two), mean, deviation, gathered.shape)
     returned = lax.all_to_all(updated, MEM, 0, 0, tiled=True)
-    low, high = from_both("space", returned[:, :, -cols:], returned[:, :, :cols])
-    done = finish(returned, low, high, diffusivity_field)
+    last, start = returned[:, :, -cols:], returned[:, :, :cols]
+    one, two = swaps("space", jnp.where(odd > 0, start, last), jnp.where(odd > 0, last, start))
+    part = middle_rows(returned, diffusivity_field)
+    done = rim_rows(flag, returned, one, two, diffusivity_field, part)
     return jnp.swapaxes(done, 0, 1)
 
 

time: 202 us -> 184 us (0.911); the launches traced: 198 us -> 183 us
  blocking collectives: 117 us -> 61 us
  waiting for transfers between devices: 22.2 us -> 65.8 us
  starting transfers between devices: 30.8 us -> 22.6 us
  Pallas kernels: 21.1 us -> 25.8 us
  local copies, waits for them, and re-layouts: 5.31 us -> 7.61 us
    all_to_all x1 -> x0, blocking collectives: 57.2 us -> none  [body(): returned = lax.all_to_all(updated, MEM, 0, 0, tiled=True)]
    all_to_all x0 -> x1, waiting for transfers between devices: none -> 51.3 us  [body(): returned = lax.all_to_all(updated, MEM, 0, 0, tiled=True)]
    ppermute x8, starting transfers between devices: 30.8 us -> 18.8 us  [the longest x4 17.7 us: swaps(): two = lax.ppermute(in_two, axis, pairs(1))]
    ppermute x8, waiting for transfers between devices: 22.2 us -> 14.6 us  [the longest x4 14.6 us: swaps(): two = lax.ppermute(in_two, axis, pairs(1))]
    pallas_call x2 -> x5, Pallas kernels: 9.77 us -> 14.5 us  [the longest x1 5.72 us: inner_forecast(): pl.pallas_call(inner_kernel, out_shape=jax.ShapeDtypeStruct((patches, mem...]
    all_to_all x0 -> x1, starting transfers between devices: none -> 3.8 us  [body(): returned = lax.all_to_all(updated, MEM, 0, 0, tiled=True)]
    unnamed x9 -> x15, local copies, waits for them, and re-layouts: 2.78 us -> 5.13 us
  transfers between devices with their start and end apart: 8 -> 9, of which waited for: 8 -> 5; matrix products, arithmetic and copies ran while one was open for 0% -> 1% of each run, Pallas kernels for 1% -> 5%
where the time goes in v3:
time: 184 us; the launch traced here: 183 us
  waiting for transfers between devices  65.8 us (36%)
  blocking collectives  61 us (33%)
  Pallas kernels  25.8 us (14%)
  starting transfers between devices  22.6 us (12%)
  local copies, waits for them, and re-layouts  7.61 us (4%)
    all_to_all x1, blocking collectives, body(): gathered = lax.all_to_all(blocks, MEM, 0, 0, tiled=True)  61 us
    all_to_all x1, waiting for transfers between devices, body(): returned = lax.all_to_all(updated, MEM, 0, 0, tiled=True)  51.3 us
    ppermute x4, starting transfers between devices, swaps(): two = lax.ppermute(in_two, axis, pairs(1))  17.7 us
    ppermute x4, waiting for transfers between devices, swaps(): two = lax.ppermute(in_two, axis, pairs(1))  14.6 us
    pallas_call x1, Pallas kernels, root_of(): pl.pallas_call(root_kernel, out_shape=jax.ShapeDtypeStruct((members, memb...  6.81 us
    pallas_call x1, Pallas kernels, inner_forecast(): pl.pallas_call(inner_kernel, out_shape=jax.ShapeDtypeStruct((patches, mem...  5.72 us
    unnamed x15, local copies, waits for them, and re-layouts  5.13 us
    pallas_call x1, Pallas kernels, outer_forecast(): pl.pallas_call(outer_kernel, out_shape=jax.ShapeDtypeStruct(part.shape, B...  3.93 us
  transfers between devices with their start and end apart: 9, of which 5 were waited for; matrix products, arithmetic and copies ran while one was open for 1% of the time, Pallas kernels for 5%

profile of v3, /device:TPU:56, one launch (start us, length us, event | category | flops | bytes accessed | tf_op | source)
XLA Modules:
  0.0 183.2 jit_solution(8159208237414492929)
XLA Ops:
  0.0 1.0 copy-done
  1.0 1.6 copy-done.2
  4.4 5.5 %collective-permute-start.1 = (bf16[8,19456]{1,0:T(8,128)(2,1)S(1)}, bf16[8,19456]{1,0:T(8,128)(2,1)S(1)}, u32[]{:S(2)}, u32[]{:S(2)}) collective-permute-start(bf16[8,19456]{1,0:T(8,128)(2,1)S(1)} %get-tuple-element.10), channel_id=1, source_target_pairs={{1,2},{3,4},{5,6},{2,1},{4,3},{6,5},{9,10},{11,12},{13,14},{10,9},... | collective-permute-start | bytes 933896 | tf_op jit(solution)/shard_map/ppermute | solution.py:471
  9.9 1.2 copy.11
  11.1 5.7 %inner.1.part_ref = bf16[32,8,4096]{2,1,0:T(8,128)(2,1)S(1)} custom-call(bf16[16,8,8192]{2,1,0:T(8,128)(2,1)S(1)} %bitcast.9, f32[16,8192]{1,0:T(8,128)S(1)} %copy-done.1), custom_call_target="tpu_custom_call" | custom-call | tf_op jit(solution)/shard_map/inner/pallas_call | solution.py:156
  16.8 2.0 %collective-permute-done.1.two_ref = bf16[8,19456]{1,0:T(8,128)(2,1)S(1)} collective-permute-done((bf16[8,19456]{1,0:T(8,128)(2,1)S(1)}, bf16[8,19456]{1,0:T(8,128)(2,1)S(1)}, u32[]{:S(2)}, u32[]{:S(2)}) %collective-permute-start.1) | collective-permute-done | bytes 311328 | tf_op jit(solution)/shard_map/ppermute | solution.py:471
  18.8 3.9 %outer.1 = bf16[32,8,4096]{2,1,0:T(8,128)(2,1)S(1)} custom-call(s32[1]{0:T(128)} %bitcast.odd_ref, bf16[16,8,8192]{2,1,0:T(8,128)(2,1)S(1)} %bitcast.10, bf16[8,19456]{1,0:T(8,128)(2,1)S(1)} %collective-permute-done.one_ref, bf16[8,19456]{1,0:T(8,128)(2,1)S(1)} %collective-permute-done.1.two_ref, ...), custom_call_target="tpu_custom_call", output_to_operand_aliasing={{}: (5, {})} | custom-call | tf_op jit(solution)/shard_map/outer/pallas_call | solution.py:205
  22.8 61.0 %all_to_all.10.block_ref = bf16[32,8,4096]{2,1,0:T(8,128)(2,1)S(1)} all-to-all(bf16[32,8,4096]{2,1,0:T(8,128)(2,1)S(1)} %outer.1), channel_id=1, replica_groups=mesh['mem_0'=2,'mem_1'=8,'mem_2'=2,'space'=8] {'mem_0','mem_1','mem_2'}, dimensions={0} | all-to-all | bytes 4194304 | tf_op jit(solution)/shard_map/all_to_all | solution.py:492
  83.8 1.6 gram.1
  85.5 1.9 %collective-permute-start.3 = (f32[136,256]{1,0:T(8,128)S(1)}, f32[136,256]{1,0:T(8,128)S(1)}, u32[]{:S(2)}, u32[]{:S(2)}) collective-permute-start(f32[136,256]{1,0:T(8,128)S(1)} %gram.1), channel_id=1, source_target_pairs={{8,16},{24,32},{40,48},{56,64},{72,80},{88,96},{104,112},{120,128}... | collective-permute-start | bytes 417800 | tf_op jit(solution)/shard_map/ppermute | solution.py:471
  87.5 4.4 %collective-permute-done.3 = f32[136,256]{1,0:T(8,128)S(1)} collective-permute-done((f32[136,256]{1,0:T(8,128)S(1)}, f32[136,256]{1,0:T(8,128)S(1)}, u32[]{:S(2)}, u32[]{:S(2)}) %collective-permute-start.3) | collective-permute-done | bytes 139296 | tf_op jit(solution)/shard_map/ppermute | solution.py:471
  92.0 5.1 %collective-permute-start.5 = (f32[136,256]{1,0:T(8,128)S(1)}, f32[136,256]{1,0:T(8,128)S(1)}, u32[]{:S(2)}, u32[]{:S(2)}) collective-permute-start(f32[136,256]{1,0:T(8,128)S(1)} %multiply_add_fusion.mid_ref), channel_id=1, source_target_pairs={{1,2},{3,4},{5,6},{2,1},{4,3},{6,5},{9,10},{11,12},{13,14},{10,9},... | collective-permute-start | bytes 417800 | tf_op jit(solution)/shard_map/ppermute | solution.py:471
  97.2 1.0 center.1
  98.2 5.4 %collective-permute-done.5.two_ref = f32[136,256]{1,0:T(8,128)S(1)} collective-permute-done((f32[136,256]{1,0:T(8,128)S(1)}, f32[136,256]{1,0:T(8,128)S(1)}, u32[]{:S(2)}, u32[]{:S(2)}) %collective-permute-start.5) | collective-permute-done | bytes 139296 | tf_op jit(solution)/shard_map/ppermute | solution.py:471
  103.6 6.8 %root.1.turned_ref = bf16[256,256]{1,0:T(8,128)(2,1)S(1)} custom-call(f32[136,256]{1,0:T(8,128)S(1)} %collective-permute-done.4.one_ref, f32[136,256]{1,0:T(8,128)S(1)} %multiply_add_fusion.mid_ref, f32[136,256]{1,0:T(8,128)S(1)} %collective-permute-done.5.two_ref), custom_call_target="tpu_custom_call" | custom-call | tf_op jit(solution)/shard_map/root/pallas_call | solution.py:319
  110.4 1.9 %update.1 = bf16[32,8,4096]{2,1,0:T(8,128)(2,1)S(1)} custom-call(bf16[256,256]{1,0:T(8,128)(2,1)S(1)} %root.1.turned_ref, f32[1,4096]{1,0:T(1,128)S(1)} %get-tuple-element.11.mean_ref, bf16[256,4096]{1,0:T(8,128)(2,1)S(1)} %get-tuple-element.12.deviation_ref), custom_call_target="tpu_custom_call" | custom-call | tf_op jit(solution)/shard_map/update/pallas_call | solution.py:374
  112.3 1.3 copy-done.3
  113.6 3.8 %all-to-all-start.1 = ((bf16[32,8,4096]{2,1,0:T(8,128)(2,1)}), bf16[32,8,4096]{2,1,0:T(8,128)(2,1)S(1)}, u32[]{:S(2)}, u32[]{:S(2)}) async-start(bf16[32,8,4096]{2,1,0:T(8,128)(2,1)} %copy-done.3), calls=%async_computation.1 | async-start | bytes 4194304 | tf_op jit(solution)/shard_map/all_to_all | solution.py:501
  117.4 51.3 %all-to-all-done.1.block_ref = bf16[32,8,4096]{2,1,0:T(8,128)(2,1)S(1)} async-done(((bf16[32,8,4096]{2,1,0:T(8,128)(2,1)}), bf16[32,8,4096]{2,1,0:T(8,128)(2,1)S(1)}, u32[]{:S(2)}, u32[]{:S(2)}) %all-to-all-start.1) | async-done | bytes 2097184 | tf_op jit(solution)/shard_map/all_to_all | solution.py:501
  168.8 5.1 %collective-permute-start.7 = (bf16[32,8,256]{2,1,0:T(8,128)(2,1)S(1)}, bf16[32,8,256]{2,1,0:T(8,128)(2,1)S(1)}, u32[]{:S(2)}, u32[]{:S(2)}) collective-permute-start(bf16[32,8,256]{2,1,0:T(8,128)(2,1)S(1)} %get-tuple-element.13), channel_id=1, source_target_pairs={{1,2},{3,4},{5,6},{2,1},{4,3},{6,5},{9,10},{11,12},{13,14},{10,9},... | collective-permute-start | bytes 393224 | tf_op jit(solution)/shard_map/ppermute | solution.py:471
  174.0 2.6 %middle.1.part_ref = bf16[16,8,8192]{2,1,0:T(8,128)(2,1)S(1)} custom-call(bf16[32,8,4096]{2,1,0:T(8,128)(2,1)S(1)} %all-to-all-done.1.block_ref, f32[16,8192]{1,0:T(8,128)S(1)} %copy-done.1), custom_call_target="tpu_custom_call" | custom-call | tf_op jit(solution)/shard_map/middle/pallas_call | solution.py:421
  176.6 2.7 %collective-permute-done.7.two_ref = bf16[32,8,256]{2,1,0:T(8,128)(2,1)S(1)} collective-permute-done((bf16[32,8,256]{2,1,0:T(8,128)(2,1)S(1)}, bf16[32,8,256]{2,1,0:T(8,128)(2,1)S(1)}, u32[]{:S(2)}, u32[]{:S(2)}) %collective-permute-start.7) | collective-permute-done | bytes 131104 | tf_op jit(solution)/shard_map/ppermute | solution.py:471
  179.3 1.4 rim.1
  180.7 2.5 %copy.9 = bf16[8,16,8192]{2,1,0:T(8,128)(2,1)} copy(bf16[8,16,8192]{2,0,1:T(8,128)(2,1)S(1)} %bitcast.8) | data formatting | bytes 4194304 | tf_op jit(solution)/shard_map/transpose | solution.py:506
  (22 shorter events, 2.1 us)
Async XLA Ops:
  0.0 1.0 copy-start
  1.0 1.6 copy-start.2
  3.6 13.3 %collective-permute-start = (bf16[8,19456]{1,0:T(8,128)(2,1)S(1)}, bf16[8,19456]{1,0:T(8,128)(2,1)S(1)}, u32[]{:S(2)}, u32[]{:S(2)}) collective-permute-start(bf16[8,19456]{1,0:T(8,128)(2,1)S(1)} %get-tuple-element.9), channel_id=1, source_target_pairs={{0,1},{2,3},{4,5},{6,7},{1,0},{3,2},{5,4},{7,6},{8,9},{10,11},{12,... | collective-permute-start | bytes 933896 | tf_op jit(solution)/shard_map/ppermute | solution.py:472
  4.4 6.7 %copy-start.1 = (f32[16,8192]{1,0:T(8,128)S(1)}, f32[16,8192]{1,0:T(8,128)}, u32[]{:S(2)}) copy-start(f32[16,8192]{1,0:T(8,128)} %coef_ref.3) | copy-start | bytes 1572868
  4.4 14.4 %collective-permute-start.1 = (bf16[8,19456]{1,0:T(8,128)(2,1)S(1)}, bf16[8,19456]{1,0:T(8,128)(2,1)S(1)}, u32[]{:S(2)}, u32[]{:S(2)}) collective-permute-start(bf16[8,19456]{1,0:T(8,128)(2,1)S(1)} %get-tuple-element.10), channel_id=1, source_target_pairs={{1,2},{3,4},{5,6},{2,1},{4,3},{6,5},{9,10},{11,12},{13,14},{10,9},... | collective-permute-start | bytes 933896 | tf_op jit(solution)/shard_map/ppermute | solution.py:471
  22.8 61.1 %copy-start.4 = (s32[1,1,512]{2,1,0:T(1,128)S(1)}, s32[1,1,512]{2,1,0:T(1,128)}, u32[]{:S(2)}) copy-start(s32[1,1,512]{2,1,0:T(1,128)} %param.7) | copy-start | bytes 6148
  22.8 61.1 %copy-start.5 = (f32[1,1,512]{2,1,0:T(1,128)S(1)}, f32[1,1,512]{2,1,0:T(1,128)}, u32[]{:S(2)}) copy-start(f32[1,1,512]{2,1,0:T(1,128)} %param.8) | copy-start | bytes 6148
  22.8 61.0 %copy-start.6 = (f32[1,1,512]{2,1,0:T(1,128)S(1)}, f32[1,1,512]{2,1,0:T(1,128)}, u32[]{:S(2)}) copy-start(f32[1,1,512]{2,1,0:T(1,128)} %param.9) | copy-start | bytes 6148
  85.4 2.0 %collective-permute-start.2 = (f32[136,256]{1,0:T(8,128)S(1)}, f32[136,256]{1,0:T(8,128)S(1)}, u32[]{:S(2)}, u32[]{:S(2)}) collective-permute-start(f32[136,256]{1,0:T(8,128)S(1)} %gram.1), channel_id=1, source_target_pairs={{0,8},{16,24},{32,40},{48,56},{64,72},{80,88},{96,104},{112,120},{... | collective-permute-start | bytes 417800 | tf_op jit(solution)/shard_map/ppermute | solution.py:472
  85.5 6.4 %collective-permute-start.3 = (f32[136,256]{1,0:T(8,128)S(1)}, f32[136,256]{1,0:T(8,128)S(1)}, u32[]{:S(2)}, u32[]{:S(2)}) collective-permute-start(f32[136,256]{1,0:T(8,128)S(1)} %gram.1), channel_id=1, source_target_pairs={{8,16},{24,32},{40,48},{56,64},{72,80},{88,96},{104,112},{120,128}... | collective-permute-start | bytes 417800 | tf_op jit(solution)/shard_map/ppermute | solution.py:471
  91.9 6.3 %collective-permute-start.4 = (f32[136,256]{1,0:T(8,128)S(1)}, f32[136,256]{1,0:T(8,128)S(1)}, u32[]{:S(2)}, u32[]{:S(2)}) collective-permute-start(f32[136,256]{1,0:T(8,128)S(1)} %multiply_add_fusion.mid_ref), channel_id=1, source_target_pairs={{0,1},{2,3},{4,5},{6,7},{1,0},{3,2},{5,4},{7,6},{8,9},{10,11},{12,... | collective-permute-start | bytes 417800 | tf_op jit(solution)/shard_map/ppermute | solution.py:472
  92.0 11.6 %collective-permute-start.5 = (f32[136,256]{1,0:T(8,128)S(1)}, f32[136,256]{1,0:T(8,128)S(1)}, u32[]{:S(2)}, u32[]{:S(2)}) collective-permute-start(f32[136,256]{1,0:T(8,128)S(1)} %multiply_add_fusion.mid_ref), channel_id=1, source_target_pairs={{1,2},{3,4},{5,6},{2,1},{4,3},{6,5},{9,10},{11,12},{13,14},{10,9},... | collective-permute-start | bytes 417800 | tf_op jit(solution)/shard_map/ppermute | solution.py:471
  112.3 1.3 copy-start.3
  113.6 55.1 %all-to-all-start.1 = ((bf16[32,8,4096]{2,1,0:T(8,128)(2,1)}), bf16[32,8,4096]{2,1,0:T(8,128)(2,1)S(1)}, u32[]{:S(2)}, u32[]{:S(2)}) async-start(bf16[32,8,4096]{2,1,0:T(8,128)(2,1)} %copy-done.3), calls=%async_computation.1 | async-start | bytes 4194304 | tf_op jit(solution)/shard_map/all_to_all | solution.py:501
  168.7 7.8 %collective-permute-start.6 = (bf16[32,8,256]{2,1,0:T(8,128)(2,1)S(1)}, bf16[32,8,256]{2,1,0:T(8,128)(2,1)S(1)}, u32[]{:S(2)}, u32[]{:S(2)}) collective-permute-start(bf16[32,8,256]{2,1,0:T(8,128)(2,1)S(1)} %get-tuple-element.14), channel_id=1, source_target_pairs={{0,1},{2,3},{4,5},{6,7},{1,0},{3,2},{5,4},{7,6},{8,9},{10,11},{12,... | collective-permute-start | bytes 393224 | tf_op jit(solution)/shard_map/ppermute | solution.py:472
  168.8 10.5 %collective-permute-start.7 = (bf16[32,8,256]{2,1,0:T(8,128)(2,1)S(1)}, bf16[32,8,256]{2,1,0:T(8,128)(2,1)S(1)}, u32[]{:S(2)}, u32[]{:S(2)}) collective-permute-start(bf16[32,8,256]{2,1,0:T(8,128)(2,1)S(1)} %get-tuple-element.13), channel_id=1, source_target_pairs={{1,2},{3,4},{5,6},{2,1},{4,3},{6,5},{9,10},{11,12},{13,14},{10,9},... | collective-permute-start | bytes 393224 | tf_op jit(solution)/shard_map/ppermute | solution.py:471

commit v4 on v3

--- a/solution.py
+++ b/solution.py
@@ -15,6 +15,10 @@
 
 def params():
     return pltpu.CompilerParams(vmem_limit_bytes=VMEM_LIMIT)
+
+
+def is_odd():
+    return lax.bitwise_and(lax.axis_index("space"), 1) > 0
 
 
 def vmem_specs(count):
@@ -54,9 +58,9 @@
 CHUNK = 512
 
 
-def ends_kernel(odd_ref, x_ref, field_ref, one_ref, two_ref):
+def ends_kernel(x_ref, field_ref, one_ref, two_ref):
     members, rows, width = x_ref.shape
-    odd = odd_ref[0] > 0
+    odd = is_odd()
 
     def put(where, low, high):
         one_ref[:, where] = jnp.where(odd, low, high).astype(BF16)
@@ -81,22 +85,22 @@
         low = whole - high.astype(F32) - rest.astype(F32)
         return [high.astype(F32), rest.astype(F32), low]
 
-    for k, (low, high) in enumerate(zip(folded(0), folded(rows - 1))):
+    for k, (low, high) in enumerate(zip(folded(0), folded(1))):
         begin = 2 * width + k * piece
         put(slice(begin, begin + piece), low, high)
 
 
-def ends(odd, x, field):
+def ends(x, field):
     members, _, width = x.shape
     shape = jax.ShapeDtypeStruct((members, 2 * width + 3 * width // members), BF16)
     return pl.pallas_call(
         ends_kernel,
         out_shape=(shape, shape),
-        in_specs=[pl.BlockSpec(memory_space=pltpu.SMEM)] + vmem_specs(2),
+        in_specs=vmem_specs(2),
         out_specs=tuple(vmem_specs(2)),
         compiler_params=params(),
         name="ends",
-    )(odd, x, field)
+    )(x, field)
 
 
 def first_pass(source, coef_ref, v1_ref, index, width, spans, shift):
@@ -164,10 +168,10 @@
     )(x, field)
 
 
-def outer_kernel(odd_ref, x_ref, one_ref, two_ref, field_ref, part_ref, out_ref, v1_ref, coef_ref):
+def outer_kernel(x_ref, one_ref, two_ref, field_ref, part_ref, out_ref, v1_ref, coef_ref):
     rows, members, width = x_ref.shape
     del part_ref
-    odd = odd_ref[0] > 0
+    odd = is_odd()
     piece = width // members
     coef_ref[pl.ds(8, rows), :] = field_ref[...]
     one = one_ref[:, 2 * width :].astype(F32)
@@ -196,22 +200,22 @@
         second_pass(coef_ref, v1_ref, out_ref, c, width, ((0, 2), (rows - 2, 2)), 8)
         return carry
 
-    lax.fori_loop(0, width // CHUNK, first, 0)
-    lax.fori_loop(0, width // CHUNK, second, 0)
-
-
-def outer_forecast(odd, x, one, two, field, part):
+    lax.fori_loop(0, width // CHUNK, first, 0, unroll=2)
+    lax.fori_loop(0, width // CHUNK, second, 0, unroll=4)
+
+
+def outer_forecast(x, one, two, field, part):
     rows, members, width = x.shape
     return pl.pallas_call(
         outer_kernel,
         out_shape=jax.ShapeDtypeStruct(part.shape, BF16),
-        in_specs=[pl.BlockSpec(memory_space=pltpu.SMEM)] + vmem_specs(5),
+        in_specs=vmem_specs(5),
         out_specs=pl.BlockSpec(memory_space=pltpu.VMEM),
         scratch_shapes=[pltpu.VMEM((rows + 2, members, width), F32), pltpu.VMEM((rows + 16, width), F32)],
-        input_output_aliases={5: 0},
+        input_output_aliases={4: 0},
         compiler_params=params(),
         name="outer",
-    )(odd, x, one, two, field, part)
+    )(x, one, two, field, part)
 
 
 def gram_kernel(block_ref, site_ref, value_ref, weight_ref, out_ref):
@@ -285,7 +289,7 @@
     )
 
 
-def root_kernel(one_ref, mid_ref, two_ref, out_ref):
+def root_kernel(one_ref, mid_ref, two_ref, out_ref, root_ref, inverse_ref):
     members = out_ref.shape[0]
     half = members // 2
     packed = mid_ref[...] + 0.5 * (one_ref[...] + two_ref[...])
@@ -293,21 +297,36 @@
     gram = unpacked(packed, half)
     across = lax.broadcasted_iota(jnp.int32, (members, members), 0)
     along = lax.broadcasted_iota(jnp.int32, (members, members), 1)
-    identity = jnp.where(across == along, 1.0, 0.0)
-    system = gram + (members - 1.0) * identity
+    on_diagonal = across == along
+    system = jnp.where(on_diagonal, gram + (members - 1.0), gram)
     squares = jnp.sum(jnp.sum(system * system, axis=0, keepdims=True), axis=1, keepdims=True)
     frob = jnp.sqrt(squares)
     root = system / frob
-    factor = 1.5 * identity - 0.5 * root
-    inverse = factor
-    root = product(halves(root), halves(factor))
-    for step in range(1, ITERS):
-        root_h = halves(root)
-        inverse_h = halves(inverse)
-        factor_h = halves(1.5 * identity - 0.5 * product(inverse_h, root_h))
-        if step < ITERS - 1:
-            root = product(root_h, factor_h)
-        inverse = product(factor_h, inverse_h)
+
+    def factor_of(value):
+        return jnp.where(on_diagonal, 1.5 - 0.5 * value, -0.5 * value)
+
+    def keep(ref, pair):
+        ref[0], ref[1] = pair
+
+    def kept(ref):
+        return ref[0], ref[1]
+
+    factor_h = halves(factor_of(root))
+    keep(inverse_ref, factor_h)
+    keep(root_ref, halves(product(halves(root), factor_h)))
+
+    def newton(step, carry):
+        factor_h = halves(factor_of(product(kept(inverse_ref), kept(root_ref))))
+        new_root = product(kept(root_ref), factor_h)
+        new_inverse = product(factor_h, kept(inverse_ref))
+        keep(root_ref, halves(new_root))
+        keep(inverse_ref, halves(new_inverse))
+        return carry
+
+    lax.fori_loop(1, ITERS - 1, newton, 0)
+    factor_h = halves(factor_of(product(kept(inverse_ref), kept(root_ref))))
+    inverse = product(factor_h, kept(inverse_ref))
     inverse_h = halves(inverse)
     weights = product(halves(product(halves(vector), inverse_h)), inverse_h) / frob
     scale = jnp.sqrt(members - 1.0) * lax.rsqrt(frob)
@@ -321,6 +340,7 @@
         out_shape=jax.ShapeDtypeStruct((members, members), BF16),
         in_specs=vmem_specs(3),
         out_specs=pl.BlockSpec(memory_space=pltpu.VMEM),
+        scratch_shapes=[pltpu.VMEM((2, members, members), BF16)] * 2,
         compiler_params=params(),
         name="root",
     )(one, mid, two)
@@ -339,7 +359,7 @@
         out_ref[:, where] = (cellwise.reshape(members, step) - mean).astype(BF16)
         return carry
 
-    lax.fori_loop(0, cells // step, one, 0)
+    lax.fori_loop(0, cells // step, one, 0, unroll=2)
 
 
 def centered(blocks):
@@ -367,7 +387,7 @@
         out_ref[:, :, where] = (mean_ref[:, where] + moved).reshape(groups, each, step).astype(BF16)
         return carry
 
-    lax.fori_loop(0, cells // step, one, 0)
+    lax.fori_loop(0, cells // step, one, 0, unroll=2)
 
 
 def update(turned, mean, deviation, shape):
@@ -381,7 +401,29 @@
     )(turned, mean, deviation)
 
 
-def final_rows(source, coef_ref, out_ref, index, cols, patches, spans):
+def edges_kernel(block_ref, one_ref, two_ref):
+    cols = one_ref.shape[2]
+    odd = is_odd()
+    for q in range(block_ref.shape[0]):
+        first = block_ref[q, :, :cols].astype(F32)
+        last = block_ref[q, :, -cols:].astype(F32)
+        one_ref[q] = jnp.where(odd, first, last).astype(BF16)
+        two_ref[q] = jnp.where(odd, last, first).astype(BF16)
+
+
+def edges(blocks, cols):
+    shape = jax.ShapeDtypeStruct((*blocks.shape[:2], cols), BF16)
+    return pl.pallas_call(
+        edges_kernel,
+        out_shape=(shape, shape),
+        in_specs=vmem_specs(1),
+        out_specs=tuple(vmem_specs(2)),
+        compiler_params=params(),
+        name="edges",
+    )(blocks)
+
+
+def final_rows(source, coef_ref, put, index, cols, patches, spans):
     each = CHUNK // cols
     base = index * each
     off = pl.multiple_of(index * CHUNK, CHUNK)
@@ -393,23 +435,31 @@
         mid = jnp.concatenate([source(r, base + k, 0, cols) for k in range(each)], axis=1)
         return framed(left, mid, source(r, after, 0, 128), index, patches // each)
 
-    def put(r, value):
-        out_ref[r, :, pl.ds(off, CHUNK)] = value.astype(BF16)
-
     for begin, count in spans:
         sweep(load, coef_ref, put, begin, count, 0, off, CHUNK)
 
 
-def middle_kernel(block_ref, coef_ref, out_ref):
-    patches, _, cells = block_ref.shape
+def middle_kernel(block_ref, coef_ref, out_ref, lines_ref):
+    patches, members, cells = block_ref.shape
     rows = coef_ref.shape[0]
     cols = cells // rows
+    pitch = rows + 8
+    lines_ref[...] = jnp.zeros_like(lines_ref)
 
     def one(c, carry):
+        off = pl.multiple_of(c * CHUNK, CHUNK)
+
         def source(r, q, begin, end):
             return block_ref[q, :, r * cols + begin : r * cols + end].astype(F32)
 
-        final_rows(source, coef_ref, out_ref, c, cols, patches, ((1, rows - 2),))
+        def put(r, value):
+            for k in range(CHUNK // 128):
+                lines_ref[k, pl.ds(r, members, stride=pitch), :] = value[:, k * 128 : (k + 1) * 128]
+
+        final_rows(source, coef_ref, put, c, cols, patches, ((1, rows - 2),))
+        for m in range(members):
+            tiles = [lines_ref[k, m * pitch : m * pitch + rows, :] for k in range(CHUNK // 128)]
+            out_ref[m, :, pl.ds(off, CHUNK)] = jnp.concatenate(tiles, axis=1).astype(BF16)
         return carry
 
     lax.fori_loop(0, patches * cols // CHUNK, one, 0)
@@ -420,45 +470,79 @@
     rows, width = coef.shape
     return pl.pallas_call(
         middle_kernel,
-        out_shape=jax.ShapeDtypeStruct((rows, members, width), BF16),
+        out_shape=jax.ShapeDtypeStruct((members, rows, width), BF16),
         in_specs=vmem_specs(2),
         out_specs=pl.BlockSpec(memory_space=pltpu.VMEM),
+        scratch_shapes=[pltpu.VMEM((CHUNK // 128, members * (rows + 8), 128), F32)],
         compiler_params=params(),
         name="middle",
     )(blocks, coef)
 
 
-def rim_kernel(odd_ref, block_ref, one_ref, two_ref, coef_ref, part_ref, out_ref):
-    patches, _, cells = block_ref.shape
+def rim_kernel(block_ref, one_ref, two_ref, coef_ref, part_ref, out_ref, whole_ref, ends_ref, done):
+    patches, members, cells = block_ref.shape
     rows = coef_ref.shape[0]
     cols = cells // rows
-    odd = odd_ref[0] > 0
-    del part_ref
+    chunks = patches * cols // CHUNK
+    odd = is_odd()
+    line = lax.broadcasted_iota(jnp.int32, (rows, CHUNK), 0)
+
+    def source(r, q, begin, end):
+        if 0 <= r < rows:
+            return block_ref[q, :, r * cols + begin : r * cols + end].astype(F32)
+        a = one_ref[q, :, begin:end].astype(F32)
+        b = two_ref[q, :, begin:end].astype(F32)
+        return jnp.where(odd, a, b) if r < 0 else jnp.where(odd, b, a)
 
     def one(c, carry):
-        def source(r, q, begin, end):
-            if 0 <= r < rows:
-                return block_ref[q, :, r * cols + begin : r * cols + end].astype(F32)
-            a = one_ref[q, :, begin:end].astype(F32)
-            b = two_ref[q, :, begin:end].astype(F32)
-            return jnp.where(odd, a, b) if r < 0 else jnp.where(odd, b, a)
-
-        final_rows(source, coef_ref, out_ref, c, cols, patches, ((0, 1), (rows - 1, 1)))
-        return carry
-
-    lax.fori_loop(0, patches * cols // CHUNK, one, 0)
-
-
-def rim_rows(odd, blocks, one, two, coef, part):
+        off = pl.multiple_of(c * CHUNK, CHUNK)
+
+        def put(r, value):
+            ends_ref[min(r, 1), :, pl.ds(off, CHUNK)] = value
+
+        final_rows(source, coef_ref, put, c, cols, patches, ((0, 1), (rows - 1, 1)))
+        return carry
+
+    lax.fori_loop(0, chunks, one, 0, unroll=4)
+
+    def move(c):
+        where = pl.ds(pl.multiple_of(c * CHUNK, CHUNK), CHUNK)
+        return pltpu.make_async_copy(whole_ref.at[:, :, where], out_ref.at[:, :, where], done.at[c])
+
+    def merge(c, carry):
+        where = pl.ds(pl.multiple_of(c * CHUNK, CHUNK), CHUNK)
+        for m in range(members):
+            old = part_ref[m, :, where].astype(F32)
+            new = jnp.where(line == 0, ends_ref[0, m : m + 1, where], old)
+            new = jnp.where(line == rows - 1, ends_ref[1, m : m + 1, where], new)
+            whole_ref[m, :, where] = new.astype(BF16)
+        move(c).start()
+        return carry
+
+    lax.fori_loop(0, chunks, merge, 0)
+
+    def settle(c, carry):
+        move(c).wait()
+        return carry
+
+    lax.fori_loop(0, chunks, settle, 0)
+
+
+def rim_rows(blocks, one, two, coef, part):
+    members, _, width = part.shape
     return pl.pallas_call(
         rim_kernel,
         out_shape=jax.ShapeDtypeStruct(part.shape, BF16),
-        in_specs=[pl.BlockSpec(memory_space=pltpu.SMEM)] + vmem_specs(5),
-        out_specs=pl.BlockSpec(memory_space=pltpu.VMEM),
-        input_output_aliases={5: 0},
+        in_specs=vmem_specs(5),
+        out_specs=pl.BlockSpec(memory_space=pl.ANY),
+        scratch_shapes=[
+            pltpu.VMEM(part.shape, BF16),
+            pltpu.VMEM((2, members, width), F32),
+            pltpu.SemaphoreType.DMA((width // CHUNK,)),
+        ],
         compiler_params=params(),
         name="rim",
-    )(odd, blocks, one, two, coef, part)
+    )(blocks, one, two, coef, part)
 
 
 def swaps(axis, in_one, in_two):
@@ -481,14 +565,12 @@
     measurement_weightings,
 ):
     patches = lax.axis_size(MEM)
-    _, _, width = prior_samples.shape
+    _, rows, width = prior_samples.shape
     cols = width // patches
-    odd = lax.bitwise_and(lax.axis_index("space"), 1)
-    flag = odd.reshape(1)
-    one, two = swaps("space", *ends(flag, prior_samples, diffusivity_field))
+    one, two = swaps("space", *ends(prior_samples, diffusivity_field[:: rows - 1]))
     turned_prior = jnp.swapaxes(prior_samples, 0, 1)
     part = inner_forecast(turned_prior, diffusivity_field, patches)
-    blocks = outer_forecast(flag, turned_prior, one, two, diffusivity_field, part)
+    blocks = outer_forecast(turned_prior, one, two, diffusivity_field, part)
     gathered = lax.all_to_all(blocks, MEM, 0, 0, tiled=True)
     own = gram_of(
         gathered, measured_site_position[0], measured_quantities[0], measurement_weightings[0]
@@ -499,11 +581,9 @@
     one, two = swaps("space", band, band)
     updated = update(root_of(one, band, two), mean, deviation, gathered.shape)
     returned = lax.all_to_all(updated, MEM, 0, 0, tiled=True)
-    last, start = returned[:, :, -cols:], returned[:, :, :cols]
-    one, two = swaps("space", jnp.where(odd > 0, start, last), jnp.where(odd > 0, last, start))
+    one, two = swaps("space", *edges(returned, cols))
     part = middle_rows(returned, diffusivity_field)
-    done = rim_rows(flag, returned, one, two, diffusivity_field, part)
-    return jnp.swapaxes(done, 0, 1)
+    return rim_rows(returned, one, two, diffusivity_field, part)
 
 
 def solution(mesh):

time: 184 us -> 179 us (0.973)
  blocking collectives: 61 us -> 117 us
  waiting for transfers between devices: 65.8 us -> 13.3 us
  starting transfers between devices: 22.6 us -> 18.8 us
  local copies, waits for them, and re-layouts: 7.61 us -> 4.71 us
    all_to_all x0 -> x1, blocking collectives: none -> 55.8 us  [body(): returned = lax.all_to_all(updated, MEM, 0, 0, tiled=True)]
    all_to_all x1 -> x0, waiting for transfers between devices: 51.3 us -> none  [body(): returned = lax.all_to_all(updated, MEM, 0, 0, tiled=True)]
    all_to_all x1 -> x0, starting transfers between devices: 3.8 us -> none  [body(): returned = lax.all_to_all(updated, MEM, 0, 0, tiled=True)]
    transpose x1 -> x0, local copies, waits for them, and re-layouts: 2.48 us -> none  [body(): return jnp.swapaxes(done, 0, 1)]
    unnamed x15 -> x11, local copies, waits for them, and re-layouts: 5.13 us -> 2.77 us
    slice x0 -> x1, local copies, waits for them, and re-layouts: none -> 1.94 us  [body(): diffusivity_field[::rows - 1]]
    pallas_call x2 -> x3, Pallas kernels: 3.49 us -> 3.86 us  [the longest x1 2.91 us: middle_rows(): pl.pallas_call(middle_kernel, out_shape=jax.ShapeDtypeStruct((members, ro...]
  transfers between devices with their start and end apart: 9 -> 8, of which waited for: 5 -> 4; matrix products, arithmetic and copies ran while one was open for 1% -> 1% of each run, Pallas kernels for 5% -> 5%
where the time goes in v4:
time: 179 us; the launch traced here: 178 us
  blocking collectives  117 us (65%)
  Pallas kernels  24 us (13%)
  starting transfers between devices  18.8 us (11%)
  waiting for transfers between devices  13.3 us (7%)
  local copies, waits for them, and re-layouts  4.71 us (3%)
    all_to_all x1, blocking collectives, body(): gathered = lax.all_to_all(blocks, MEM, 0, 0, tiled=True)  61 us
    all_to_all x1, blocking collectives, body(): returned = lax.all_to_all(updated, MEM, 0, 0, tiled=True)  55.8 us
    ppermute x4, starting transfers between devices, swaps(): two = lax.ppermute(in_two, axis, pairs(1))  17.7 us
    ppermute x4, waiting for transfers between devices, swaps(): two = lax.ppermute(in_two, axis, pairs(1))  13.3 us
    pallas_call x1, Pallas kernels, root_of(): pl.pallas_call(root_kernel, out_shape=jax.ShapeDtypeStruct((members, memb...  6.41 us
    pallas_call x1, Pallas kernels, inner_forecast(): pl.pallas_call(inner_kernel, out_shape=jax.ShapeDtypeStruct((patches, mem...  5.72 us
  transfers between devices with their start and end apart: 8, of which 4 were waited for; matrix products, arithmetic and copies ran while one was open for 1% of the time, Pallas kernels for 5%

profile of v4, /device:TPU:56, one launch (start us, length us, event | category | flops | bytes accessed | tf_op | source)
XLA Modules:
  0.0 177.8 jit_solution(17014983284076182132)
XLA Ops:
  0.0 1.9 %slice.3.field_ref = f32[2,8192]{1,0:T(2,128)S(1)} slice(f32[16,8192]{1,0:T(8,128)} %coef_ref.3), slice={[0:16:15], [0:8192:1]} | slice | bytes 131072 | tf_op jit(solution)/shard_map/slice | solution.py:570
  2.0 1.6 copy-done.1
  3.5 0.9 ends.1
  4.4 0.8 collective-permute-start
  5.3 5.5 %collective-permute-start.1 = (bf16[8,19456]{1,0:T(8,128)(2,1)S(1)}, bf16[8,19456]{1,0:T(8,128)(2,1)S(1)}, u32[]{:S(2)}, u32[]{:S(2)}) collective-permute-start(bf16[8,19456]{1,0:T(8,128)(2,1)S(1)} %get-tuple-element.12), channel_id=1, source_target_pairs={{1,2},{3,4},{5,6},{2,1},{4,3},{6,5},{9,10},{11,12},{13,14},{10,9},... | collective-permute-start | bytes 933896 | tf_op jit(solution)/shard_map/ppermute | solution.py:555
  10.8 1.2 copy.9
  12.0 5.7 %inner.1.part_ref = bf16[32,8,4096]{2,1,0:T(8,128)(2,1)S(1)} custom-call(bf16[16,8,8192]{2,1,0:T(8,128)(2,1)S(1)} %bitcast.6, f32[16,8192]{1,0:T(8,128)S(1)} %copy-done), custom_call_target="tpu_custom_call" | custom-call | tf_op jit(solution)/shard_map/inner/pallas_call | solution.py:160
  17.7 2.0 %collective-permute-done.1.two_ref = bf16[8,19456]{1,0:T(8,128)(2,1)S(1)} collective-permute-done((bf16[8,19456]{1,0:T(8,128)(2,1)S(1)}, bf16[8,19456]{1,0:T(8,128)(2,1)S(1)}, u32[]{:S(2)}, u32[]{:S(2)}) %collective-permute-start.1) | collective-permute-done | bytes 311328 | tf_op jit(solution)/shard_map/ppermute | solution.py:555
  19.7 2.4 %outer.1 = bf16[32,8,4096]{2,1,0:T(8,128)(2,1)S(1)} custom-call(bf16[16,8,8192]{2,1,0:T(8,128)(2,1)S(1)} %bitcast.7, bf16[8,19456]{1,0:T(8,128)(2,1)S(1)} %collective-permute-done.one_ref, bf16[8,19456]{1,0:T(8,128)(2,1)S(1)} %collective-permute-done.1.two_ref, f32[16,8192]{1,0:T(8,128)S(1)} %copy-done, ...), custom_call_target="tpu_custom_call", output_to_operand_aliasing={{}: (4, {})} | custom-call | tf_op jit(solution)/shard_map/outer/pallas_call | solution.py:209
  22.2 61.0 %all_to_all.10.block_ref = bf16[32,8,4096]{2,1,0:T(8,128)(2,1)S(1)} all-to-all(bf16[32,8,4096]{2,1,0:T(8,128)(2,1)S(1)} %outer.1), channel_id=1, replica_groups=mesh['mem_0'=2,'mem_1'=8,'mem_2'=2,'space'=8] {'mem_0','mem_1','mem_2'}, dimensions={0} | all-to-all | bytes 4194304 | tf_op jit(solution)/shard_map/all_to_all | solution.py:574
  83.2 1.6 gram.1
  84.8 1.9 %collective-permute-start.3 = (f32[136,256]{1,0:T(8,128)S(1)}, f32[136,256]{1,0:T(8,128)S(1)}, u32[]{:S(2)}, u32[]{:S(2)}) collective-permute-start(f32[136,256]{1,0:T(8,128)S(1)} %gram.1), channel_id=1, source_target_pairs={{8,16},{24,32},{40,48},{56,64},{72,80},{88,96},{104,112},{120,128}... | collective-permute-start | bytes 417800 | tf_op jit(solution)/shard_map/ppermute | solution.py:555
  86.7 0.1 collective-permute-start.2
  86.8 4.3 %collective-permute-done.3 = f32[136,256]{1,0:T(8,128)S(1)} collective-permute-done((f32[136,256]{1,0:T(8,128)S(1)}, f32[136,256]{1,0:T(8,128)S(1)}, u32[]{:S(2)}, u32[]{:S(2)}) %collective-permute-start.3) | collective-permute-done | bytes 139296 | tf_op jit(solution)/shard_map/ppermute | solution.py:555
  91.2 5.1 %collective-permute-start.5 = (f32[136,256]{1,0:T(8,128)S(1)}, f32[136,256]{1,0:T(8,128)S(1)}, u32[]{:S(2)}, u32[]{:S(2)}) collective-permute-start(f32[136,256]{1,0:T(8,128)S(1)} %multiply_add_fusion.mid_ref), channel_id=1, source_target_pairs={{1,2},{3,4},{5,6},{2,1},{4,3},{6,5},{9,10},{11,12},{13,14},{10,9},... | collective-permute-start | bytes 417800 | tf_op jit(solution)/shard_map/ppermute | solution.py:555
  96.4 0.8 center.1
  97.2 4.5 %collective-permute-done.5.two_ref = f32[136,256]{1,0:T(8,128)S(1)} collective-permute-done((f32[136,256]{1,0:T(8,128)S(1)}, f32[136,256]{1,0:T(8,128)S(1)}, u32[]{:S(2)}, u32[]{:S(2)}) %collective-permute-start.5) | collective-permute-done | bytes 139296 | tf_op jit(solution)/shard_map/ppermute | solution.py:555
  101.8 6.4 %root.1.turned_ref = bf16[256,256]{1,0:T(8,128)(2,1)S(1)} custom-call(f32[136,256]{1,0:T(8,128)S(1)} %collective-permute-done.4.one_ref, f32[136,256]{1,0:T(8,128)S(1)} %multiply_add_fusion.mid_ref, f32[136,256]{1,0:T(8,128)S(1)} %collective-permute-done.5.two_ref), custom_call_target="tpu_custom_call" | custom-call | tf_op jit(solution)/shard_map/root/pallas_call | solution.py:338
  108.2 1.2 update.1
  109.4 55.8 %all_to_all.11.block_ref = bf16[32,8,4096]{2,1,0:T(8,128)(2,1)S(1)} all-to-all(bf16[32,8,4096]{2,1,0:T(8,128)(2,1)S(1)} %update.1), channel_id=1, replica_groups=mesh['mem_0'=2,'mem_1'=8,'mem_2'=2,'space'=8] {'mem_0','mem_1','mem_2'}, dimensions={0} | all-to-all | bytes 4194304 | tf_op jit(solution)/shard_map/all_to_all | solution.py:583
  165.4 5.1 %collective-permute-start.7 = (bf16[32,8,256]{2,1,0:T(8,128)(2,1)S(1)}, bf16[32,8,256]{2,1,0:T(8,128)(2,1)S(1)}, u32[]{:S(2)}, u32[]{:S(2)}) collective-permute-start(bf16[32,8,256]{2,1,0:T(8,128)(2,1)S(1)} %get-tuple-element.16), channel_id=1, source_target_pairs={{1,2},{3,4},{5,6},{2,1},{4,3},{6,5},{9,10},{11,12},{13,14},{10,9},... | collective-permute-start | bytes 393224 | tf_op jit(solution)/shard_map/ppermute | solution.py:555
  170.5 2.9 %middle.1.part_ref = bf16[8,16,8192]{2,1,0:T(8,128)(2,1)S(1)} custom-call(bf16[32,8,4096]{2,1,0:T(8,128)(2,1)S(1)} %all_to_all.11.block_ref, f32[16,8192]{1,0:T(8,128)S(1)} %copy-done), custom_call_target="tpu_custom_call" | custom-call | tf_op jit(solution)/shard_map/middle/pallas_call | solution.py:471
  173.5 2.4 %collective-permute-done.7.two_ref = bf16[32,8,256]{2,1,0:T(8,128)(2,1)S(1)} collective-permute-done((bf16[32,8,256]{2,1,0:T(8,128)(2,1)S(1)}, bf16[32,8,256]{2,1,0:T(8,128)(2,1)S(1)}, u32[]{:S(2)}, u32[]{:S(2)}) %collective-permute-start.7) | collective-permute-done | bytes 131104 | tf_op jit(solution)/shard_map/ppermute | solution.py:555
  175.9 2.0 %rim.1 = bf16[8,16,8192]{2,1,0:T(8,128)(2,1)} custom-call(bf16[32,8,4096]{2,1,0:T(8,128)(2,1)S(1)} %all_to_all.11.block_ref, bf16[32,8,256]{2,1,0:T(8,128)(2,1)S(1)} %collective-permute-done.6.one_ref, bf16[32,8,256]{2,1,0:T(8,128)(2,1)S(1)} %collective-permute-done.7.two_ref, f32[16,8192]{1,0:T(8,128)S(1)} %copy-done, bf16[8,16,8192]{2,1,0:T(8,128)(2,1)S(1)} %middle.1.part_ref), custom_call_target="tpu_custom_call" | custom-call | tf_op jit(solution)/shard_map/rim/pallas_call | solution.py:533
  (17 shorter events, 0.3 us)
Async XLA Ops:
  1.9 1.6 copy-start.1
  4.4 13.3 %collective-permute-start = (bf16[8,19456]{1,0:T(8,128)(2,1)S(1)}, bf16[8,19456]{1,0:T(8,128)(2,1)S(1)}, u32[]{:S(2)}, u32[]{:S(2)}) collective-permute-start(bf16[8,19456]{1,0:T(8,128)(2,1)S(1)} %get-tuple-element.11), channel_id=1, source_target_pairs={{0,1},{2,3},{4,5},{6,7},{1,0},{3,2},{5,4},{7,6},{8,9},{10,11},{12,... | collective-permute-start | bytes 933896 | tf_op jit(solution)/shard_map/ppermute | solution.py:556
  5.3 6.7 %copy-start = (f32[16,8192]{1,0:T(8,128)S(1)}, f32[16,8192]{1,0:T(8,128)}, u32[]{:S(2)}) copy-start(f32[16,8192]{1,0:T(8,128)} %coef_ref.3) | copy-start | bytes 1572868
  5.3 14.4 %collective-permute-start.1 = (bf16[8,19456]{1,0:T(8,128)(2,1)S(1)}, bf16[8,19456]{1,0:T(8,128)(2,1)S(1)}, u32[]{:S(2)}, u32[]{:S(2)}) collective-permute-start(bf16[8,19456]{1,0:T(8,128)(2,1)S(1)} %get-tuple-element.12), channel_id=1, source_target_pairs={{1,2},{3,4},{5,6},{2,1},{4,3},{6,5},{9,10},{11,12},{13,14},{10,9},... | collective-permute-start | bytes 933896 | tf_op jit(solution)/shard_map/ppermute | solution.py:555
  22.1 61.1 %copy-start.2 = (s32[1,1,512]{2,1,0:T(1,128)S(1)}, s32[1,1,512]{2,1,0:T(1,128)}, u32[]{:S(2)}) copy-start(s32[1,1,512]{2,1,0:T(1,128)} %param.7) | copy-start | bytes 6148
  22.2 61.1 %copy-start.3 = (f32[1,1,512]{2,1,0:T(1,128)S(1)}, f32[1,1,512]{2,1,0:T(1,128)}, u32[]{:S(2)}) copy-start(f32[1,1,512]{2,1,0:T(1,128)} %param.8) | copy-start | bytes 6148
  22.2 61.0 %copy-start.4 = (f32[1,1,512]{2,1,0:T(1,128)S(1)}, f32[1,1,512]{2,1,0:T(1,128)}, u32[]{:S(2)}) copy-start(f32[1,1,512]{2,1,0:T(1,128)} %param.9) | copy-start | bytes 6148
  84.8 6.4 %collective-permute-start.3 = (f32[136,256]{1,0:T(8,128)S(1)}, f32[136,256]{1,0:T(8,128)S(1)}, u32[]{:S(2)}, u32[]{:S(2)}) collective-permute-start(f32[136,256]{1,0:T(8,128)S(1)} %gram.1), channel_id=1, source_target_pairs={{8,16},{24,32},{40,48},{56,64},{72,80},{88,96},{104,112},{120,128}... | collective-permute-start | bytes 417800 | tf_op jit(solution)/shard_map/ppermute | solution.py:555
  86.7 4.4 %collective-permute-start.2 = (f32[136,256]{1,0:T(8,128)S(1)}, f32[136,256]{1,0:T(8,128)S(1)}, u32[]{:S(2)}, u32[]{:S(2)}) collective-permute-start(f32[136,256]{1,0:T(8,128)S(1)} %gram.1), channel_id=1, source_target_pairs={{0,8},{16,24},{32,40},{48,56},{64,72},{80,88},{96,104},{112,120},{... | collective-permute-start | bytes 417800 | tf_op jit(solution)/shard_map/ppermute | solution.py:556
  91.2 10.6 %collective-permute-start.5 = (f32[136,256]{1,0:T(8,128)S(1)}, f32[136,256]{1,0:T(8,128)S(1)}, u32[]{:S(2)}, u32[]{:S(2)}) collective-permute-start(f32[136,256]{1,0:T(8,128)S(1)} %multiply_add_fusion.mid_ref), channel_id=1, source_target_pairs={{1,2},{3,4},{5,6},{2,1},{4,3},{6,5},{9,10},{11,12},{13,14},{10,9},... | collective-permute-start | bytes 417800 | tf_op jit(solution)/shard_map/ppermute | solution.py:555
  96.3 5.4 %collective-permute-start.4 = (f32[136,256]{1,0:T(8,128)S(1)}, f32[136,256]{1,0:T(8,128)S(1)}, u32[]{:S(2)}, u32[]{:S(2)}) collective-permute-start(f32[136,256]{1,0:T(8,128)S(1)} %multiply_add_fusion.mid_ref), channel_id=1, source_target_pairs={{0,1},{2,3},{4,5},{6,7},{1,0},{3,2},{5,4},{7,6},{8,9},{10,11},{12,... | collective-permute-start | bytes 417800 | tf_op jit(solution)/shard_map/ppermute | solution.py:556
  165.3 8.2 %collective-permute-start.6 = (bf16[32,8,256]{2,1,0:T(8,128)(2,1)S(1)}, bf16[32,8,256]{2,1,0:T(8,128)(2,1)S(1)}, u32[]{:S(2)}, u32[]{:S(2)}) collective-permute-start(bf16[32,8,256]{2,1,0:T(8,128)(2,1)S(1)} %get-tuple-element.15), channel_id=1, source_target_pairs={{0,1},{2,3},{4,5},{6,7},{1,0},{3,2},{5,4},{7,6},{8,9},{10,11},{12,... | collective-permute-start | bytes 393224 | tf_op jit(solution)/shard_map/ppermute | solution.py:556
  165.4 10.5 %collective-permute-start.7 = (bf16[32,8,256]{2,1,0:T(8,128)(2,1)S(1)}, bf16[32,8,256]{2,1,0:T(8,128)(2,1)S(1)}, u32[]{:S(2)}, u32[]{:S(2)}) collective-permute-start(bf16[32,8,256]{2,1,0:T(8,128)(2,1)S(1)} %get-tuple-element.16), channel_id=1, source_target_pairs={{1,2},{3,4},{5,6},{2,1},{4,3},{6,5},{9,10},{11,12},{13,14},{10,9},... | collective-permute-start | bytes 393224 | tf_op jit(solution)/shard_map/ppermute | solution.py:555

commit v5 on v4

--- a/solution.py
+++ b/solution.py
@@ -75,7 +75,7 @@
             put(pl.ds(pl.multiple_of(k * width + off, CHUNK), CHUNK), low, high)
         return carry
 
-    lax.fori_loop(0, width // CHUNK, some, 0)
+    lax.fori_loop(0, width // CHUNK, some, 0, unroll=2)
     piece = width // members
 
     def folded(row):
@@ -85,7 +85,7 @@
         low = whole - high.astype(F32) - rest.astype(F32)
         return [high.astype(F32), rest.astype(F32), low]
 
-    for k, (low, high) in enumerate(zip(folded(0), folded(1))):
+    for k, (low, high) in enumerate(zip(folded(0), folded(rows - 1))):
         begin = 2 * width + k * piece
         put(slice(begin, begin + piece), low, high)
 
@@ -151,8 +151,8 @@
         second_pass(field_ref, v1_ref, out_ref, c, width, ((2, rows - 4),), 0)
         return carry
 
-    lax.fori_loop(0, width // CHUNK, first, 0)
-    lax.fori_loop(0, width // CHUNK, second, 0)
+    lax.fori_loop(0, width // CHUNK, first, 0, unroll=4)
+    lax.fori_loop(0, width // CHUNK, second, 0, unroll=4)
 
 
 def inner_forecast(x, field, patches):
@@ -200,7 +200,7 @@
         second_pass(coef_ref, v1_ref, out_ref, c, width, ((0, 2), (rows - 2, 2)), 8)
         return carry
 
-    lax.fori_loop(0, width // CHUNK, first, 0, unroll=2)
+    lax.fori_loop(0, width // CHUNK, first, 0, unroll=4)
     lax.fori_loop(0, width // CHUNK, second, 0, unroll=4)
 
 
@@ -462,7 +462,7 @@
             out_ref[m, :, pl.ds(off, CHUNK)] = jnp.concatenate(tiles, axis=1).astype(BF16)
         return carry
 
-    lax.fori_loop(0, patches * cols // CHUNK, one, 0)
+    lax.fori_loop(0, patches * cols // CHUNK, one, 0, unroll=2)
 
 
 def middle_rows(blocks, coef):
@@ -494,23 +494,17 @@
         b = two_ref[q, :, begin:end].astype(F32)
         return jnp.where(odd, a, b) if r < 0 else jnp.where(odd, b, a)
 
-    def one(c, carry):
-        off = pl.multiple_of(c * CHUNK, CHUNK)
-
-        def put(r, value):
-            ends_ref[min(r, 1), :, pl.ds(off, CHUNK)] = value
-
-        final_rows(source, coef_ref, put, c, cols, patches, ((0, 1), (rows - 1, 1)))
-        return carry
-
-    lax.fori_loop(0, chunks, one, 0, unroll=4)
-
     def move(c):
         where = pl.ds(pl.multiple_of(c * CHUNK, CHUNK), CHUNK)
         return pltpu.make_async_copy(whole_ref.at[:, :, where], out_ref.at[:, :, where], done.at[c])
 
-    def merge(c, carry):
+    def one(c, carry):
         where = pl.ds(pl.multiple_of(c * CHUNK, CHUNK), CHUNK)
+
+        def put(r, value):
+            ends_ref[min(r, 1), :, where] = value
+
+        final_rows(source, coef_ref, put, c, cols, patches, ((0, 1), (rows - 1, 1)))
         for m in range(members):
             old = part_ref[m, :, where].astype(F32)
             new = jnp.where(line == 0, ends_ref[0, m : m + 1, where], old)
@@ -519,7 +513,7 @@
         move(c).start()
         return carry
 
-    lax.fori_loop(0, chunks, merge, 0)
+    lax.fori_loop(0, chunks, one, 0, unroll=4)
 
     def settle(c, carry):
         move(c).wait()
@@ -565,12 +559,12 @@
     measurement_weightings,
 ):
     patches = lax.axis_size(MEM)
-    _, rows, width = prior_samples.shape
-    cols = width // patches
-    one, two = swaps("space", *ends(prior_samples, diffusivity_field[:: rows - 1]))
+    cols = prior_samples.shape[2] // patches
+    field = diffusivity_field
+    one, two = swaps("space", *ends(prior_samples, field))
     turned_prior = jnp.swapaxes(prior_samples, 0, 1)
-    part = inner_forecast(turned_prior, diffusivity_field, patches)
-    blocks = outer_forecast(turned_prior, one, two, diffusivity_field, part)
+    part = inner_forecast(turned_prior, field, patches)
+    blocks = outer_forecast(turned_prior, one, two, field, part)
     gathered = lax.all_to_all(blocks, MEM, 0, 0, tiled=True)
     own = gram_of(
         gathered, measured_site_position[0], measured_quantities[0], measurement_weightings[0]
@@ -582,8 +576,8 @@
     updated = update(root_of(one, band, two), mean, deviation, gathered.shape)
     returned = lax.all_to_all(updated, MEM, 0, 0, tiled=True)
     one, two = swaps("space", *edges(returned, cols))
-    part = middle_rows(returned, diffusivity_field)
-    return rim_rows(returned, one, two, diffusivity_field, part)
+    part = middle_rows(returned, field)
+    return rim_rows(returned, one, two, field, part)
 
 
 def solution(mesh):

time: 179 us -> 177 us (0.989)
  Pallas kernels: 24 us -> 21.5 us
  waiting for transfers between devices: 13.3 us -> 15.3 us
    ppermute x4, waiting for transfers between devices: 13.3 us -> 15.3 us  [swaps(): two = lax.ppermute(in_two, axis, pairs(1))]
    slice x1 -> x0, local copies, waits for them, and re-layouts: 1.94 us -> none  [body(): diffusivity_field[::rows - 1]]
    unnamed x11 -> x13, local copies, waits for them, and re-layouts: 2.77 us -> 3.81 us
  transfers between devices with their start and end apart: 8 -> 8, of which waited for: 4 -> 4; matrix products, arithmetic and copies ran while one was open for 1% -> 1% of each run, Pallas kernels for 5% -> 4%
where the time goes in v5:
time: 177 us; the launch traced here: 176 us
  blocking collectives  117 us (66%)
  Pallas kernels  21.5 us (12%)
  starting transfers between devices  18.8 us (11%)
  waiting for transfers between devices  15.3 us (9%)
  local copies, waits for them, and re-layouts  3.81 us (2%)
    all_to_all x1, blocking collectives, body(): gathered = lax.all_to_all(blocks, MEM, 0, 0, tiled=True)  61 us
    all_to_all x1, blocking collectives, body(): returned = lax.all_to_all(updated, MEM, 0, 0, tiled=True)  55.8 us
    ppermute x4, starting transfers between devices, swaps(): two = lax.ppermute(in_two, axis, pairs(1))  17.7 us
    ppermute x4, waiting for transfers between devices, swaps(): two = lax.ppermute(in_two, axis, pairs(1))  15.3 us
    pallas_call x1, Pallas kernels, root_of(): pl.pallas_call(root_kernel, out_shape=jax.ShapeDtypeStruct((members, memb...  6.41 us
    pallas_call x1, Pallas kernels, inner_forecast(): pl.pallas_call(inner_kernel, out_shape=jax.ShapeDtypeStruct((patches, mem...  4.25 us
    unnamed x13, local copies, waits for them, and re-layouts  3.81 us
  transfers between devices with their start and end apart: 8, of which 4 were waited for; matrix products, arithmetic and copies ran while one was open for 1% of the time, Pallas kernels for 4%

profile of v5, /device:TPU:56, one launch (start us, length us, event | category | flops | bytes accessed | tf_op | source)
XLA Modules:
  0.0 176.5 jit_solution(15113650721672558530)
XLA Ops:
  0.0 1.0 copy-done
  1.0 1.6 copy-done.2
  2.6 0.8 ends.1
  3.5 0.8 collective-permute-start
  4.3 5.5 %collective-permute-start.1 = (bf16[8,19456]{1,0:T(8,128)(2,1)S(1)}, bf16[8,19456]{1,0:T(8,128)(2,1)S(1)}, u32[]{:S(2)}, u32[]{:S(2)}) collective-permute-start(bf16[8,19456]{1,0:T(8,128)(2,1)S(1)} %get-tuple-element.12), channel_id=1, source_target_pairs={{1,2},{3,4},{5,6},{2,1},{4,3},{6,5},{9,10},{11,12},{13,14},{10,9},... | collective-permute-start | bytes 933896 | tf_op jit(solution)/shard_map/ppermute | solution.py:549
  9.9 1.2 copy.9
  11.0 4.3 %inner.1.part_ref = bf16[32,8,4096]{2,1,0:T(8,128)(2,1)S(1)} custom-call(bf16[16,8,8192]{2,1,0:T(8,128)(2,1)S(1)} %bitcast.6, f32[16,8192]{1,0:T(8,128)S(1)} %copy-done.1), custom_call_target="tpu_custom_call" | custom-call | tf_op jit(solution)/shard_map/inner/pallas_call | solution.py:160
  15.3 3.4 %collective-permute-done.1.two_ref = bf16[8,19456]{1,0:T(8,128)(2,1)S(1)} collective-permute-done((bf16[8,19456]{1,0:T(8,128)(2,1)S(1)}, bf16[8,19456]{1,0:T(8,128)(2,1)S(1)}, u32[]{:S(2)}, u32[]{:S(2)}) %collective-permute-start.1) | collective-permute-done | bytes 311328 | tf_op jit(solution)/shard_map/ppermute | solution.py:549
  18.8 2.2 %outer.1 = bf16[32,8,4096]{2,1,0:T(8,128)(2,1)S(1)} custom-call(bf16[16,8,8192]{2,1,0:T(8,128)(2,1)S(1)} %bitcast.7, bf16[8,19456]{1,0:T(8,128)(2,1)S(1)} %collective-permute-done.one_ref, bf16[8,19456]{1,0:T(8,128)(2,1)S(1)} %collective-permute-done.1.two_ref, f32[16,8192]{1,0:T(8,128)S(1)} %copy-done.1, ...), custom_call_target="tpu_custom_call", output_to_operand_aliasing={{}: (4, {})} | custom-call | tf_op jit(solution)/shard_map/outer/pallas_call | solution.py:209
  21.0 61.0 %all_to_all.10.block_ref = bf16[32,8,4096]{2,1,0:T(8,128)(2,1)S(1)} all-to-all(bf16[32,8,4096]{2,1,0:T(8,128)(2,1)S(1)} %outer.1), channel_id=1, replica_groups=mesh['mem_0'=2,'mem_1'=8,'mem_2'=2,'space'=8] {'mem_0','mem_1','mem_2'}, dimensions={0} | all-to-all | bytes 4194304 | tf_op jit(solution)/shard_map/all_to_all | solution.py:568
  82.1 1.6 gram.1
  83.7 1.9 %collective-permute-start.3 = (f32[136,256]{1,0:T(8,128)S(1)}, f32[136,256]{1,0:T(8,128)S(1)}, u32[]{:S(2)}, u32[]{:S(2)}) collective-permute-start(f32[136,256]{1,0:T(8,128)S(1)} %gram.1), channel_id=1, source_target_pairs={{8,16},{24,32},{40,48},{56,64},{72,80},{88,96},{104,112},{120,128}... | collective-permute-start | bytes 417800 | tf_op jit(solution)/shard_map/ppermute | solution.py:549
  85.6 0.1 collective-permute-start.2
  85.7 4.3 %collective-permute-done.3 = f32[136,256]{1,0:T(8,128)S(1)} collective-permute-done((f32[136,256]{1,0:T(8,128)S(1)}, f32[136,256]{1,0:T(8,128)S(1)}, u32[]{:S(2)}, u32[]{:S(2)}) %collective-permute-start.3) | collective-permute-done | bytes 139296 | tf_op jit(solution)/shard_map/ppermute | solution.py:549
  90.1 5.1 %collective-permute-start.5 = (f32[136,256]{1,0:T(8,128)S(1)}, f32[136,256]{1,0:T(8,128)S(1)}, u32[]{:S(2)}, u32[]{:S(2)}) collective-permute-start(f32[136,256]{1,0:T(8,128)S(1)} %multiply_add_fusion.mid_ref), channel_id=1, source_target_pairs={{1,2},{3,4},{5,6},{2,1},{4,3},{6,5},{9,10},{11,12},{13,14},{10,9},... | collective-permute-start | bytes 417800 | tf_op jit(solution)/shard_map/ppermute | solution.py:549
  95.3 0.8 center.1
  96.1 4.5 %collective-permute-done.5.two_ref = f32[136,256]{1,0:T(8,128)S(1)} collective-permute-done((f32[136,256]{1,0:T(8,128)S(1)}, f32[136,256]{1,0:T(8,128)S(1)}, u32[]{:S(2)}, u32[]{:S(2)}) %collective-permute-start.5) | collective-permute-done | bytes 139296 | tf_op jit(solution)/shard_map/ppermute | solution.py:549
  100.6 6.4 %root.1.turned_ref = bf16[256,256]{1,0:T(8,128)(2,1)S(1)} custom-call(f32[136,256]{1,0:T(8,128)S(1)} %collective-permute-done.4.one_ref, f32[136,256]{1,0:T(8,128)S(1)} %multiply_add_fusion.mid_ref, f32[136,256]{1,0:T(8,128)S(1)} %collective-permute-done.5.two_ref), custom_call_target="tpu_custom_call" | custom-call | tf_op jit(solution)/shard_map/root/pallas_call | solution.py:338
  107.1 1.2 update.1
  108.3 55.8 %all_to_all.11.block_ref = bf16[32,8,4096]{2,1,0:T(8,128)(2,1)S(1)} all-to-all(bf16[32,8,4096]{2,1,0:T(8,128)(2,1)S(1)} %update.1), channel_id=1, replica_groups=mesh['mem_0'=2,'mem_1'=8,'mem_2'=2,'space'=8] {'mem_0','mem_1','mem_2'}, dimensions={0} | all-to-all | bytes 4194304 | tf_op jit(solution)/shard_map/all_to_all | solution.py:577
  164.3 5.1 %collective-permute-start.7 = (bf16[32,8,256]{2,1,0:T(8,128)(2,1)S(1)}, bf16[32,8,256]{2,1,0:T(8,128)(2,1)S(1)}, u32[]{:S(2)}, u32[]{:S(2)}) collective-permute-start(bf16[32,8,256]{2,1,0:T(8,128)(2,1)S(1)} %get-tuple-element.16), channel_id=1, source_target_pairs={{1,2},{3,4},{5,6},{2,1},{4,3},{6,5},{9,10},{11,12},{13,14},{10,9},... | collective-permute-start | bytes 393224 | tf_op jit(solution)/shard_map/ppermute | solution.py:549
  169.4 2.4 %middle.1.part_ref = bf16[8,16,8192]{2,1,0:T(8,128)(2,1)S(1)} custom-call(bf16[32,8,4096]{2,1,0:T(8,128)(2,1)S(1)} %all_to_all.11.block_ref, f32[16,8192]{1,0:T(8,128)S(1)} %copy-done.1), custom_call_target="tpu_custom_call" | custom-call | tf_op jit(solution)/shard_map/middle/pallas_call | solution.py:471
  171.8 2.9 %collective-permute-done.7.two_ref = bf16[32,8,256]{2,1,0:T(8,128)(2,1)S(1)} collective-permute-done((bf16[32,8,256]{2,1,0:T(8,128)(2,1)S(1)}, bf16[32,8,256]{2,1,0:T(8,128)(2,1)S(1)}, u32[]{:S(2)}, u32[]{:S(2)}) %collective-permute-start.7) | collective-permute-done | bytes 131104 | tf_op jit(solution)/shard_map/ppermute | solution.py:549
  174.7 1.7 rim.1
  (18 shorter events, 0.3 us)
Async XLA Ops:
  0.0 1.0 copy-start
  1.0 1.6 copy-start.2
  3.5 11.8 %collective-permute-start = (bf16[8,19456]{1,0:T(8,128)(2,1)S(1)}, bf16[8,19456]{1,0:T(8,128)(2,1)S(1)}, u32[]{:S(2)}, u32[]{:S(2)}) collective-permute-start(bf16[8,19456]{1,0:T(8,128)(2,1)S(1)} %get-tuple-element.11), channel_id=1, source_target_pairs={{0,1},{2,3},{4,5},{6,7},{1,0},{3,2},{5,4},{7,6},{8,9},{10,11},{12,... | collective-permute-start | bytes 933896 | tf_op jit(solution)/shard_map/ppermute | solution.py:550
  4.3 6.7 %copy-start.1 = (f32[16,8192]{1,0:T(8,128)S(1)}, f32[16,8192]{1,0:T(8,128)}, u32[]{:S(2)}) copy-start(f32[16,8192]{1,0:T(8,128)} %coef_ref.3) | copy-start | bytes 1572868
  4.3 14.4 %collective-permute-start.1 = (bf16[8,19456]{1,0:T(8,128)(2,1)S(1)}, bf16[8,19456]{1,0:T(8,128)(2,1)S(1)}, u32[]{:S(2)}, u32[]{:S(2)}) collective-permute-start(bf16[8,19456]{1,0:T(8,128)(2,1)S(1)} %get-tuple-element.12), channel_id=1, source_target_pairs={{1,2},{3,4},{5,6},{2,1},{4,3},{6,5},{9,10},{11,12},{13,14},{10,9},... | collective-permute-start | bytes 933896 | tf_op jit(solution)/shard_map/ppermute | solution.py:549
  21.0 61.1 %copy-start.3 = (s32[1,1,512]{2,1,0:T(1,128)S(1)}, s32[1,1,512]{2,1,0:T(1,128)}, u32[]{:S(2)}) copy-start(s32[1,1,512]{2,1,0:T(1,128)} %param.7) | copy-start | bytes 6148
  21.0 61.1 %copy-start.4 = (f32[1,1,512]{2,1,0:T(1,128)S(1)}, f32[1,1,512]{2,1,0:T(1,128)}, u32[]{:S(2)}) copy-start(f32[1,1,512]{2,1,0:T(1,128)} %param.8) | copy-start | bytes 6148
  21.0 61.0 %copy-start.5 = (f32[1,1,512]{2,1,0:T(1,128)S(1)}, f32[1,1,512]{2,1,0:T(1,128)}, u32[]{:S(2)}) copy-start(f32[1,1,512]{2,1,0:T(1,128)} %param.9) | copy-start | bytes 6148
  83.7 6.4 %collective-permute-start.3 = (f32[136,256]{1,0:T(8,128)S(1)}, f32[136,256]{1,0:T(8,128)S(1)}, u32[]{:S(2)}, u32[]{:S(2)}) collective-permute-start(f32[136,256]{1,0:T(8,128)S(1)} %gram.1), channel_id=1, source_target_pairs={{8,16},{24,32},{40,48},{56,64},{72,80},{88,96},{104,112},{120,128}... | collective-permute-start | bytes 417800 | tf_op jit(solution)/shard_map/ppermute | solution.py:549
  85.6 4.4 %collective-permute-start.2 = (f32[136,256]{1,0:T(8,128)S(1)}, f32[136,256]{1,0:T(8,128)S(1)}, u32[]{:S(2)}, u32[]{:S(2)}) collective-permute-start(f32[136,256]{1,0:T(8,128)S(1)} %gram.1), channel_id=1, source_target_pairs={{0,8},{16,24},{32,40},{48,56},{64,72},{80,88},{96,104},{112,120},{... | collective-permute-start | bytes 417800 | tf_op jit(solution)/shard_map/ppermute | solution.py:550
  90.1 10.6 %collective-permute-start.5 = (f32[136,256]{1,0:T(8,128)S(1)}, f32[136,256]{1,0:T(8,128)S(1)}, u32[]{:S(2)}, u32[]{:S(2)}) collective-permute-start(f32[136,256]{1,0:T(8,128)S(1)} %multiply_add_fusion.mid_ref), channel_id=1, source_target_pairs={{1,2},{3,4},{5,6},{2,1},{4,3},{6,5},{9,10},{11,12},{13,14},{10,9},... | collective-permute-start | bytes 417800 | tf_op jit(solution)/shard_map/ppermute | solution.py:549
  95.2 5.4 %collective-permute-start.4 = (f32[136,256]{1,0:T(8,128)S(1)}, f32[136,256]{1,0:T(8,128)S(1)}, u32[]{:S(2)}, u32[]{:S(2)}) collective-permute-start(f32[136,256]{1,0:T(8,128)S(1)} %multiply_add_fusion.mid_ref), channel_id=1, source_target_pairs={{0,1},{2,3},{4,5},{6,7},{1,0},{3,2},{5,4},{7,6},{8,9},{10,11},{12,... | collective-permute-start | bytes 417800 | tf_op jit(solution)/shard_map/ppermute | solution.py:550
  164.2 7.6 %collective-permute-start.6 = (bf16[32,8,256]{2,1,0:T(8,128)(2,1)S(1)}, bf16[32,8,256]{2,1,0:T(8,128)(2,1)S(1)}, u32[]{:S(2)}, u32[]{:S(2)}) collective-permute-start(bf16[32,8,256]{2,1,0:T(8,128)(2,1)S(1)} %get-tuple-element.15), channel_id=1, source_target_pairs={{0,1},{2,3},{4,5},{6,7},{1,0},{3,2},{5,4},{7,6},{8,9},{10,11},{12,... | collective-permute-start | bytes 393224 | tf_op jit(solution)/shard_map/ppermute | solution.py:550
  164.3 10.5 %collective-permute-start.7 = (bf16[32,8,256]{2,1,0:T(8,128)(2,1)S(1)}, bf16[32,8,256]{2,1,0:T(8,128)(2,1)S(1)}, u32[]{:S(2)}, u32[]{:S(2)}) collective-permute-start(bf16[32,8,256]{2,1,0:T(8,128)(2,1)S(1)} %get-tuple-element.16), channel_id=1, source_target_pairs={{1,2},{3,4},{5,6},{2,1},{4,3},{6,5},{9,10},{11,12},{13,14},{10,9},... | collective-permute-start | bytes 393224 | tf_op jit(solution)/shard_map/ppermute | solution.py:549

commit v6 on v5

--- a/solution.py
+++ b/solution.py
@@ -10,7 +10,7 @@
 MEM = ("mem_0", "mem_1", "mem_2")
 F32 = jnp.float32
 BF16 = jnp.bfloat16
-VMEM_LIMIT = 48 << 20
+VMEM_LIMIT = 24 << 20
 
 
 def params():
@@ -58,13 +58,38 @@
 CHUNK = 512
 
 
-def ends_kernel(x_ref, field_ref, one_ref, two_ref):
+def ends_kernel(x_hbm, field_hbm, one_ref, two_ref, x_ref, field_ref, arrived):
     members, rows, width = x_ref.shape
     odd = is_odd()
+    parts = arrived.shape[0] - 1
+    size = width // parts
+
+    def fetch(k):
+        where = slice(k * size, (k + 1) * size)
+        return pltpu.make_async_copy(x_hbm.at[:, :, where], x_ref.at[:, :, where], arrived.at[k])
+
+    whole = pltpu.make_async_copy(field_hbm, field_ref, arrived.at[parts])
+    whole.start()
+    for k in range(parts):
+        fetch(k).start()
 
     def put(where, low, high):
         one_ref[:, where] = jnp.where(odd, low, high).astype(BF16)
         two_ref[:, where] = jnp.where(odd, high, low).astype(BF16)
+
+    piece = width // members
+
+    def folded(row):
+        lines = [field_ref[row : row + 1, s * piece : (s + 1) * piece] for s in range(members)]
+        block = jnp.concatenate(lines, axis=0)
+        high, rest = halves(block)
+        low = block - high.astype(F32) - rest.astype(F32)
+        return [high.astype(F32), rest.astype(F32), low]
+
+    whole.wait()
+    for k, (low, high) in enumerate(zip(folded(0), folded(rows - 1))):
+        begin = 2 * width + k * piece
+        put(slice(begin, begin + piece), low, high)
 
     def some(c, carry):
         off = pl.multiple_of(c * CHUNK, CHUNK)
@@ -75,19 +100,10 @@
             put(pl.ds(pl.multiple_of(k * width + off, CHUNK), CHUNK), low, high)
         return carry
 
-    lax.fori_loop(0, width // CHUNK, some, 0, unroll=2)
-    piece = width // members
-
-    def folded(row):
-        lines = [field_ref[row : row + 1, s * piece : (s + 1) * piece] for s in range(members)]
-        whole = jnp.concatenate(lines, axis=0)
-        high, rest = halves(whole)
-        low = whole - high.astype(F32) - rest.astype(F32)
-        return [high.astype(F32), rest.astype(F32), low]
-
-    for k, (low, high) in enumerate(zip(folded(0), folded(rows - 1))):
-        begin = 2 * width + k * piece
-        put(slice(begin, begin + piece), low, high)
+    each = size // CHUNK
+    for k in range(parts):
+        fetch(k).wait()
+        lax.fori_loop(k * each, (k + 1) * each, some, 0, unroll=2)
 
 
 def ends(x, field):
@@ -95,15 +111,21 @@
     shape = jax.ShapeDtypeStruct((members, 2 * width + 3 * width // members), BF16)
     return pl.pallas_call(
         ends_kernel,
-        out_shape=(shape, shape),
-        in_specs=vmem_specs(2),
-        out_specs=tuple(vmem_specs(2)),
+        out_shape=(
+            shape,
+            shape,
+            jax.ShapeDtypeStruct(x.shape, x.dtype),
+            jax.ShapeDtypeStruct(field.shape, field.dtype),
+        ),
+        in_specs=[pl.BlockSpec(memory_space=pltpu.HBM)] * 2,
+        out_specs=tuple(vmem_specs(4)),
+        scratch_shapes=[pltpu.SemaphoreType.DMA((5,))],
         compiler_params=params(),
         name="ends",
-    )(x, field)
-
-
-def first_pass(source, coef_ref, v1_ref, index, width, spans, shift):
+    )(*(pltpu.with_memory_space_constraint(v, pltpu.HBM) for v in (x, field)))
+
+
+def first_pass(source, coef_ref, keep, index, width, spans, shift):
     off, before, after = edges_of(index, CHUNK, width)
 
     def load(r):
@@ -113,18 +135,18 @@
     for begin, count in spans:
 
         def put(r, value):
-            v1_ref[r + 1, :, pl.ds(off, CHUNK)] = value
+            keep(r, pl.ds(off, CHUNK), value)
 
         sweep(load, coef_ref, put, begin, count, shift, off, CHUNK)
 
 
-def second_pass(coef_ref, v1_ref, out_ref, index, width, spans, shift):
+def second_pass(coef_ref, pick, out_ref, index, width, spans, shift):
     cols = width // out_ref.shape[0]
     each = CHUNK // cols
     off, before, after = edges_of(index, CHUNK, width)
 
     def load(r):
-        pieces = [v1_ref[r + 1, :, pl.ds(o, s)] for o, s in ((before, 128), (off, CHUNK), (after, 128))]
+        pieces = [pick(r, o, s) for o, s in ((before, 128), (off, CHUNK), (after, 128))]
         return framed(*pieces, index, width // CHUNK)
 
     def put(r, value):
@@ -137,38 +159,51 @@
         sweep(load, coef_ref, put, begin, count, shift, off, CHUNK)
 
 
-def inner_kernel(x_ref, field_ref, out_ref, v1_ref):
+def inner_kernel(x_ref, field_ref, out_ref, kept_ref, v1_ref):
     rows, _, width = x_ref.shape
+    chunks = width // CHUNK
+    kept = (1, 2, rows - 3, rows - 2)
 
     def first(c, carry):
         def source(r, off, size):
             return x_ref[r, :, pl.ds(off, size)].astype(F32)
 
-        first_pass(source, field_ref, v1_ref, c, width, ((1, rows - 2),), 0)
-        return carry
+        def keep(r, where, value):
+            v1_ref[r + 1, :, where] = value
+            if r in kept:
+                kept_ref[kept.index(r), :, where] = value
+
+        first_pass(source, field_ref, keep, c, width, ((1, rows - 2),), 0)
+        return carry
+
+    def pick(r, off, size):
+        return v1_ref[r + 1, :, pl.ds(off, size)]
 
     def second(c, carry):
-        second_pass(field_ref, v1_ref, out_ref, c, width, ((2, rows - 4),), 0)
-        return carry
-
-    lax.fori_loop(0, width // CHUNK, first, 0, unroll=4)
-    lax.fori_loop(0, width // CHUNK, second, 0, unroll=4)
+        second_pass(field_ref, pick, out_ref, c, width, ((2, rows - 4),), 0)
+        return carry
+
+    lax.fori_loop(0, chunks, first, 0, unroll=4)
+    lax.fori_loop(0, chunks, second, 0, unroll=4)
 
 
 def inner_forecast(x, field, patches):
     rows, members, width = x.shape
     return pl.pallas_call(
         inner_kernel,
-        out_shape=jax.ShapeDtypeStruct((patches, members, rows * width // patches), BF16),
+        out_shape=(
+            jax.ShapeDtypeStruct((patches, members, rows * width // patches), BF16),
+            jax.ShapeDtypeStruct((4, members, width), F32),
+        ),
         in_specs=vmem_specs(2),
-        out_specs=pl.BlockSpec(memory_space=pltpu.VMEM),
+        out_specs=tuple(vmem_specs(2)),
         scratch_shapes=[pltpu.VMEM((rows + 2, members, width), F32)],
         compiler_params=params(),
         name="inner",
     )(x, field)
 
 
-def outer_kernel(x_ref, one_ref, two_ref, field_ref, part_ref, out_ref, v1_ref, coef_ref):
+def outer_kernel(x_ref, one_ref, two_ref, field_ref, part_ref, kept_ref, out_ref, v1_ref, coef_ref):
     rows, members, width = x_ref.shape
     del part_ref
     odd = is_odd()
@@ -193,29 +228,39 @@
             b = two_ref[:, pl.ds(at + off, size)].astype(F32)
             return jnp.where(odd, a, b) if r < 0 else jnp.where(odd, b, a)
 
-        first_pass(source, coef_ref, v1_ref, c, width, ((-1, 4), (rows - 3, 4)), 8)
-        return carry
+        def keep(r, where, value):
+            v1_ref[r + 1, :, where] = value
+
+        first_pass(source, coef_ref, keep, c, width, ((-1, 2), (rows - 1, 2)), 8)
+        return carry
+
+    kept = (1, 2, rows - 3, rows - 2)
+
+    def pick(r, off, size):
+        if r in kept:
+            return kept_ref[kept.index(r), :, pl.ds(off, size)]
+        return v1_ref[r + 1, :, pl.ds(off, size)]
 
     def second(c, carry):
-        second_pass(coef_ref, v1_ref, out_ref, c, width, ((0, 2), (rows - 2, 2)), 8)
+        second_pass(coef_ref, pick, out_ref, c, width, ((0, 2), (rows - 2, 2)), 8)
         return carry
 
     lax.fori_loop(0, width // CHUNK, first, 0, unroll=4)
     lax.fori_loop(0, width // CHUNK, second, 0, unroll=4)
 
 
-def outer_forecast(x, one, two, field, part):
+def outer_forecast(x, one, two, field, part, kept):
     rows, members, width = x.shape
     return pl.pallas_call(
         outer_kernel,
         out_shape=jax.ShapeDtypeStruct(part.shape, BF16),
-        in_specs=vmem_specs(5),
+        in_specs=vmem_specs(6),
         out_specs=pl.BlockSpec(memory_space=pltpu.VMEM),
         scratch_shapes=[pltpu.VMEM((rows + 2, members, width), F32), pltpu.VMEM((rows + 16, width), F32)],
         input_output_aliases={4: 0},
         compiler_params=params(),
         name="outer",
-    )(x, one, two, field, part)
+    )(x, one, two, field, part, kept)
 
 
 def gram_kernel(block_ref, site_ref, value_ref, weight_ref, out_ref):
@@ -560,11 +605,11 @@
 ):
     patches = lax.axis_size(MEM)
     cols = prior_samples.shape[2] // patches
-    field = diffusivity_field
-    one, two = swaps("space", *ends(prior_samples, field))
-    turned_prior = jnp.swapaxes(prior_samples, 0, 1)
-    part = inner_forecast(turned_prior, field, patches)
-    blocks = outer_forecast(turned_prior, one, two, field, part)
+    one, two, prior, field = ends(prior_samples, diffusivity_field)
+    one, two = swaps("space", one, two)
+    turned_prior = jnp.swapaxes(prior, 0, 1)
+    part, kept = inner_forecast(turned_prior, field, patches)
+    blocks = outer_forecast(turned_prior, one, two, field, part, kept)
     gathered = lax.all_to_all(blocks, MEM, 0, 0, tiled=True)
     own = gram_of(
         gathered, measured_site_position[0], measured_quantities[0], measurement_weightings[0]

time: 177 us -> 175 us (0.989)
  local copies, waits for them, and re-layouts: 3.81 us -> 1.18 us
    unnamed x13 -> x6, local copies, waits for them, and re-layouts: 3.81 us -> 0.02 us
where the time goes in v6:
time: 175 us; the launch traced here: 174 us
  blocking collectives  117 us (67%)
  Pallas kernels  22.2 us (13%)
  starting transfers between devices  18.7 us (11%)
  waiting for transfers between devices  15.3 us (9%)
    all_to_all x1, blocking collectives, body(): gathered = lax.all_to_all(blocks, MEM, 0, 0, tiled=True)  61 us
    all_to_all x1, blocking collectives, body(): returned = lax.all_to_all(updated, MEM, 0, 0, tiled=True)  55.8 us
    ppermute x4, starting transfers between devices, swaps(): two = lax.ppermute(in_two, axis, pairs(1))  17.6 us
    ppermute x4, waiting for transfers between devices, swaps(): two = lax.ppermute(in_two, axis, pairs(1))  15.3 us
    pallas_call x1, Pallas kernels, root_of(): pl.pallas_call(root_kernel, out_shape=jax.ShapeDtypeStruct((members, memb...  6.41 us
    pallas_call x1, Pallas kernels, inner_forecast(): pl.pallas_call(inner_kernel, out_shape=(jax.ShapeDtypeStruct((patches, me...  4.26 us
  transfers between devices with their start and end apart: 8, of which 4 were waited for; matrix products, arithmetic and copies ran while one was open for 1% of the time, Pallas kernels for 4%

profile of v6, /device:TPU:56, one launch (start us, length us, event | category | flops | bytes accessed | tf_op | source)
XLA Modules:
  0.0 174.4 jit_solution(757270149570891645)
XLA Ops:
  0.0 2.0 %ends.1 = (bf16[8,19456]{1,0:T(8,128)(2,1)S(1)}, bf16[8,19456]{1,0:T(8,128)(2,1)S(1)}, bf16[8,16,8192]{2,1,0:T(8,128)(2,1)S(1)}, f32[16,8192]{1,0:T(8,128)S(1)}) custom-call(bf16[8,16,8192]{2,1,0:T(8,128)(2,1)} %x_hbm.1, f32[16,8192]{1,0:T(8,128)} %field_hbm.1), custom_call_target="tpu_custom_call" | custom-call | tf_op jit(solution)/shard_map/ends/pallas_call | solution.py:112
  2.0 0.8 collective-permute-start
  2.9 5.4 %collective-permute-start.1 = (bf16[8,19456]{1,0:T(8,128)(2,1)S(1)}, bf16[8,19456]{1,0:T(8,128)(2,1)S(1)}, u32[]{:S(2)}, u32[]{:S(2)}) collective-permute-start(bf16[8,19456]{1,0:T(8,128)(2,1)S(1)} %get-tuple-element.17), channel_id=1, source_target_pairs={{1,2},{3,4},{5,6},{2,1},{4,3},{6,5},{9,10},{11,12},{13,14},{10,9},... | collective-permute-start | bytes 933896 | tf_op jit(solution)/shard_map/ppermute | solution.py:594
  8.3 1.2 copy.9
  9.4 4.3 %inner.1 = (bf16[32,8,4096]{2,1,0:T(8,128)(2,1)S(1)}, f32[4,8,8192]{2,1,0:T(8,128)S(1)}) custom-call(bf16[16,8,8192]{2,1,0:T(8,128)(2,1)S(1)} %bitcast.6, f32[16,8192]{1,0:T(8,128)S(1)} %get-tuple-element.18.field_ref.coef_ref), custom_call_target="tpu_custom_call" | custom-call | tf_op jit(solution)/shard_map/inner/pallas_call | solution.py:192
  13.7 3.5 %collective-permute-done.1.two_ref = bf16[8,19456]{1,0:T(8,128)(2,1)S(1)} collective-permute-done((bf16[8,19456]{1,0:T(8,128)(2,1)S(1)}, bf16[8,19456]{1,0:T(8,128)(2,1)S(1)}, u32[]{:S(2)}, u32[]{:S(2)}) %collective-permute-start.1) | collective-permute-done | bytes 311328 | tf_op jit(solution)/shard_map/ppermute | solution.py:594
  17.2 1.7 outer.1
  19.0 61.0 %all_to_all.10.block_ref = bf16[32,8,4096]{2,1,0:T(8,128)(2,1)S(1)} all-to-all(bf16[32,8,4096]{2,1,0:T(8,128)(2,1)S(1)} %outer.1), channel_id=1, replica_groups=mesh['mem_0'=2,'mem_1'=8,'mem_2'=2,'space'=8] {'mem_0','mem_1','mem_2'}, dimensions={0} | all-to-all | bytes 4194304 | tf_op jit(solution)/shard_map/all_to_all | solution.py:613
  80.0 1.6 gram.1
  81.6 1.9 %collective-permute-start.3 = (f32[136,256]{1,0:T(8,128)S(1)}, f32[136,256]{1,0:T(8,128)S(1)}, u32[]{:S(2)}, u32[]{:S(2)}) collective-permute-start(f32[136,256]{1,0:T(8,128)S(1)} %gram.1), channel_id=1, source_target_pairs={{8,16},{24,32},{40,48},{56,64},{72,80},{88,96},{104,112},{120,128}... | collective-permute-start | bytes 417800 | tf_op jit(solution)/shard_map/ppermute | solution.py:594
  83.5 0.1 collective-permute-start.2
  83.6 4.3 %collective-permute-done.3 = f32[136,256]{1,0:T(8,128)S(1)} collective-permute-done((f32[136,256]{1,0:T(8,128)S(1)}, f32[136,256]{1,0:T(8,128)S(1)}, u32[]{:S(2)}, u32[]{:S(2)}) %collective-permute-start.3) | collective-permute-done | bytes 139296 | tf_op jit(solution)/shard_map/ppermute | solution.py:594
  88.0 5.1 %collective-permute-start.5 = (f32[136,256]{1,0:T(8,128)S(1)}, f32[136,256]{1,0:T(8,128)S(1)}, u32[]{:S(2)}, u32[]{:S(2)}) collective-permute-start(f32[136,256]{1,0:T(8,128)S(1)} %multiply_add_fusion.mid_ref), channel_id=1, source_target_pairs={{1,2},{3,4},{5,6},{2,1},{4,3},{6,5},{9,10},{11,12},{13,14},{10,9},... | collective-permute-start | bytes 417800 | tf_op jit(solution)/shard_map/ppermute | solution.py:594
  93.1 0.1 collective-permute-start.4
  93.2 0.8 center.1
  94.0 4.5 %collective-permute-done.5.two_ref = f32[136,256]{1,0:T(8,128)S(1)} collective-permute-done((f32[136,256]{1,0:T(8,128)S(1)}, f32[136,256]{1,0:T(8,128)S(1)}, u32[]{:S(2)}, u32[]{:S(2)}) %collective-permute-start.5) | collective-permute-done | bytes 139296 | tf_op jit(solution)/shard_map/ppermute | solution.py:594
  98.6 6.4 %root.1.turned_ref = bf16[256,256]{1,0:T(8,128)(2,1)S(1)} custom-call(f32[136,256]{1,0:T(8,128)S(1)} %collective-permute-done.4.one_ref, f32[136,256]{1,0:T(8,128)S(1)} %multiply_add_fusion.mid_ref, f32[136,256]{1,0:T(8,128)S(1)} %collective-permute-done.5.two_ref), custom_call_target="tpu_custom_call" | custom-call | tf_op jit(solution)/shard_map/root/pallas_call | solution.py:383
  105.0 1.2 update.1
  106.2 55.8 %all_to_all.11.block_ref = bf16[32,8,4096]{2,1,0:T(8,128)(2,1)S(1)} all-to-all(bf16[32,8,4096]{2,1,0:T(8,128)(2,1)S(1)} %update.1), channel_id=1, replica_groups=mesh['mem_0'=2,'mem_1'=8,'mem_2'=2,'space'=8] {'mem_0','mem_1','mem_2'}, dimensions={0} | all-to-all | bytes 4194304 | tf_op jit(solution)/shard_map/all_to_all | solution.py:622
  162.1 0.1 collective-permute-start.6
  162.2 5.1 %collective-permute-start.7 = (bf16[32,8,256]{2,1,0:T(8,128)(2,1)S(1)}, bf16[32,8,256]{2,1,0:T(8,128)(2,1)S(1)}, u32[]{:S(2)}, u32[]{:S(2)}) collective-permute-start(bf16[32,8,256]{2,1,0:T(8,128)(2,1)S(1)} %get-tuple-element.24), channel_id=1, source_target_pairs={{1,2},{3,4},{5,6},{2,1},{4,3},{6,5},{9,10},{11,12},{13,14},{10,9},... | collective-permute-start | bytes 393224 | tf_op jit(solution)/shard_map/ppermute | solution.py:594
  167.3 2.4 %middle.1.part_ref = bf16[8,16,8192]{2,1,0:T(8,128)(2,1)S(1)} custom-call(bf16[32,8,4096]{2,1,0:T(8,128)(2,1)S(1)} %all_to_all.11.block_ref, f32[16,8192]{1,0:T(8,128)S(1)} %get-tuple-element.18.field_ref.coef_ref), custom_call_target="tpu_custom_call" | custom-call | tf_op jit(solution)/shard_map/middle/pallas_call | solution.py:516
  169.7 2.9 %collective-permute-done.7.two_ref = bf16[32,8,256]{2,1,0:T(8,128)(2,1)S(1)} collective-permute-done((bf16[32,8,256]{2,1,0:T(8,128)(2,1)S(1)}, bf16[32,8,256]{2,1,0:T(8,128)(2,1)S(1)}, u32[]{:S(2)}, u32[]{:S(2)}) %collective-permute-start.7) | collective-permute-done | bytes 131104 | tf_op jit(solution)/shard_map/ppermute | solution.py:594
  172.7 1.7 rim.1
  (12 shorter events, 0.1 us)
Async XLA Ops:
  2.0 11.7 %collective-permute-start = (bf16[8,19456]{1,0:T(8,128)(2,1)S(1)}, bf16[8,19456]{1,0:T(8,128)(2,1)S(1)}, u32[]{:S(2)}, u32[]{:S(2)}) collective-permute-start(bf16[8,19456]{1,0:T(8,128)(2,1)S(1)} %get-tuple-element.16), channel_id=1, source_target_pairs={{0,1},{2,3},{4,5},{6,7},{1,0},{3,2},{5,4},{7,6},{8,9},{10,11},{12,... | collective-permute-start | bytes 933896 | tf_op jit(solution)/shard_map/ppermute | solution.py:595
  2.9 14.3 %collective-permute-start.1 = (bf16[8,19456]{1,0:T(8,128)(2,1)S(1)}, bf16[8,19456]{1,0:T(8,128)(2,1)S(1)}, u32[]{:S(2)}, u32[]{:S(2)}) collective-permute-start(bf16[8,19456]{1,0:T(8,128)(2,1)S(1)} %get-tuple-element.17), channel_id=1, source_target_pairs={{1,2},{3,4},{5,6},{2,1},{4,3},{6,5},{9,10},{11,12},{13,14},{10,9},... | collective-permute-start | bytes 933896 | tf_op jit(solution)/shard_map/ppermute | solution.py:594
  18.9 61.1 %copy-start = (s32[1,1,512]{2,1,0:T(1,128)S(1)}, s32[1,1,512]{2,1,0:T(1,128)}, u32[]{:S(2)}) copy-start(s32[1,1,512]{2,1,0:T(1,128)} %param.7) | copy-start | bytes 6148
  18.9 61.1 %copy-start.1 = (f32[1,1,512]{2,1,0:T(1,128)S(1)}, f32[1,1,512]{2,1,0:T(1,128)}, u32[]{:S(2)}) copy-start(f32[1,1,512]{2,1,0:T(1,128)} %param.8) | copy-start | bytes 6148
  18.9 61.0 %copy-start.2 = (f32[1,1,512]{2,1,0:T(1,128)S(1)}, f32[1,1,512]{2,1,0:T(1,128)}, u32[]{:S(2)}) copy-start(f32[1,1,512]{2,1,0:T(1,128)} %param.9) | copy-start | bytes 6148
  81.6 6.4 %collective-permute-start.3 = (f32[136,256]{1,0:T(8,128)S(1)}, f32[136,256]{1,0:T(8,128)S(1)}, u32[]{:S(2)}, u32[]{:S(2)}) collective-permute-start(f32[136,256]{1,0:T(8,128)S(1)} %gram.1), channel_id=1, source_target_pairs={{8,16},{24,32},{40,48},{56,64},{72,80},{88,96},{104,112},{120,128}... | collective-permute-start | bytes 417800 | tf_op jit(solution)/shard_map/ppermute | solution.py:594
  83.5 4.4 %collective-permute-start.2 = (f32[136,256]{1,0:T(8,128)S(1)}, f32[136,256]{1,0:T(8,128)S(1)}, u32[]{:S(2)}, u32[]{:S(2)}) collective-permute-start(f32[136,256]{1,0:T(8,128)S(1)} %gram.1), channel_id=1, source_target_pairs={{0,8},{16,24},{32,40},{48,56},{64,72},{80,88},{96,104},{112,120},{... | collective-permute-start | bytes 417800 | tf_op jit(solution)/shard_map/ppermute | solution.py:595
  88.0 10.6 %collective-permute-start.5 = (f32[136,256]{1,0:T(8,128)S(1)}, f32[136,256]{1,0:T(8,128)S(1)}, u32[]{:S(2)}, u32[]{:S(2)}) collective-permute-start(f32[136,256]{1,0:T(8,128)S(1)} %multiply_add_fusion.mid_ref), channel_id=1, source_target_pairs={{1,2},{3,4},{5,6},{2,1},{4,3},{6,5},{9,10},{11,12},{13,14},{10,9},... | collective-permute-start | bytes 417800 | tf_op jit(solution)/shard_map/ppermute | solution.py:594
  93.1 5.4 %collective-permute-start.4 = (f32[136,256]{1,0:T(8,128)S(1)}, f32[136,256]{1,0:T(8,128)S(1)}, u32[]{:S(2)}, u32[]{:S(2)}) collective-permute-start(f32[136,256]{1,0:T(8,128)S(1)} %multiply_add_fusion.mid_ref), channel_id=1, source_target_pairs={{0,1},{2,3},{4,5},{6,7},{1,0},{3,2},{5,4},{7,6},{8,9},{10,11},{12,... | collective-permute-start | bytes 417800 | tf_op jit(solution)/shard_map/ppermute | solution.py:595
  162.1 7.6 %collective-permute-start.6 = (bf16[32,8,256]{2,1,0:T(8,128)(2,1)S(1)}, bf16[32,8,256]{2,1,0:T(8,128)(2,1)S(1)}, u32[]{:S(2)}, u32[]{:S(2)}) collective-permute-start(bf16[32,8,256]{2,1,0:T(8,128)(2,1)S(1)} %get-tuple-element.23), channel_id=1, source_target_pairs={{0,1},{2,3},{4,5},{6,7},{1,0},{3,2},{5,4},{7,6},{8,9},{10,11},{12,... | collective-permute-start | bytes 393224 | tf_op jit(solution)/shard_map/ppermute | solution.py:595
  162.2 10.5 %collective-permute-start.7 = (bf16[32,8,256]{2,1,0:T(8,128)(2,1)S(1)}, bf16[32,8,256]{2,1,0:T(8,128)(2,1)S(1)}, u32[]{:S(2)}, u32[]{:S(2)}) collective-permute-start(bf16[32,8,256]{2,1,0:T(8,128)(2,1)S(1)} %get-tuple-element.24), channel_id=1, source_target_pairs={{1,2},{3,4},{5,6},{2,1},{4,3},{6,5},{9,10},{11,12},{13,14},{10,9},... | collective-permute-start | bytes 393224 | tf_op jit(solution)/shard_map/ppermute | solution.py:594
